TPU v7x, 32 devices: a whole 2x2x4 slice. The times are simulated.
32 devices in a mesh: gx: 2 (over x), gy: 4 (over z), gz: 4 (over y, core).
Axes of the slice: x: 2, y: 2, z: 4, core: 2. Of those that a mesh axis runs over, the one named last changes fastest.
Arguments:
- state_old: float32 [5, 32, 128, 512], P(None, 'gx', 'gy', 'gz'), as said below
- state_section: float32 [5, 32, 128, 512], P(None, 'gx', 'gy', 'gz'), as said below
- panel_record: bfloat16 [131072, 512], P(('gx', 'gy', 'gz')), may hold values from -6 to 6
- panel_cell: int32 [1024, 128], P(('gx', 'gy', 'gz')), may hold values from 0 to 65535
- panel_angles: float32 [2, 131072], P(None, ('gx', 'gy', 'gz')), may hold values from -3.140625 to 3.140625
- owned_blocks: int32 [32], P(('gx', 'gy', 'gz')), may hold values from 1 to 32, 256 in all
- listener_angles: float32 [2, 1024], replicated, may hold values from -3.140625 to 3.140625
- listener_range: float32 [1024], replicated, may hold values from 1.2 to 2.5
Outputs:
- state_next: float32 [5, 32, 128, 512], P(None, 'gx', 'gy', 'gz')
- observer_spectra: float32 [2, 1024, 128], P(None, 'gz')
Inputs may be any that keep to these rules, and one draw needn't show every extreme that they name: `state_old`: density between 0.5 and 2, velocity components of magnitude 0.3 at most, stiffened-gas pressure between 0.3 and 2. `state_section`: density between 0.5 and 2, velocity components of magnitude 0.3 at most, stiffened-gas pressure between 0.3 and 2. A device's live blocks fill its first owned_blocks slots; some device owns 32 blocks, and they total 8 times the number of devices.
All inputs are finite; a program needn't handle non-finite values.
Results may differ from a plain program's by a relative error of at most 0.0003.
The roundings to bfloat16 on the way count: a program that leaves them out, or rounds other values in their place, can miss the bound.
Values may be sent and summed in bfloat16 or wider, within the bound.
No kernel may reach another device: no remote copies, remote signals or barrier semaphores. Data moves between devices by JAX's collectives and lax.ppermute only.
A program may use at most 64 MiB of HBM per device.

v0:
```python
import math

import jax
import jax.numpy as jnp
from jax import lax
from jax.sharding import PartitionSpec as P

FREQS = 128
GROUP = 4


GAMMA_GAS = 4.4
PRESSURE_INF = 1.0
WENO_EPS = 1e-06
WAVE_STEP = 0.25
COURANT = 0.08


def with_halo(shard, sides, width):
    for axis, dim in sides:
        size, length = (lax.axis_size(axis), shard.shape[dim])
        up = [(i, (i + 1) % size) for i in range(size)]
        down = [(j, i) for i, j in up]
        last = lax.slice_in_dim(shard, length - width, length, axis=dim)
        initial = lax.slice_in_dim(shard, 0, width, axis=dim)
        before = lax.ppermute(last, axis, up)
        after = lax.ppermute(initial, axis, down)
        shard = jnp.concatenate([before, shard, after], axis=dim)
    return shard


def weno_face(far_left, near_left, middle, near_right, far_right):
    cand_a = (2.0 * far_left - 7.0 * near_left + 11.0 * middle) / 6.0
    cand_b = (-near_left + 5.0 * middle + 2.0 * near_right) / 6.0
    cand_c = (2.0 * middle + 5.0 * near_right - far_right) / 6.0
    rough_a = (
        13.0 / 12.0 * (far_left - 2.0 * near_left + middle) ** 2
        + 0.25 * (far_left - 4.0 * near_left + 3.0 * middle) ** 2
    )
    rough_b = (
        13.0 / 12.0 * (near_left - 2.0 * middle + near_right) ** 2
        + 0.25 * (near_left - near_right) ** 2
    )
    rough_c = (
        13.0 / 12.0 * (middle - 2.0 * near_right + far_right) ** 2
        + 0.25 * (3.0 * middle - 4.0 * near_right + far_right) ** 2
    )
    weight_a = 0.1 / (WENO_EPS + rough_a) ** 2
    weight_b = 0.6 / (WENO_EPS + rough_b) ** 2
    weight_c = 0.3 / (WENO_EPS + rough_c) ** 2
    return (weight_a * cand_a + weight_b * cand_b + weight_c * cand_c) / (
        weight_a + weight_b + weight_c
    )


def euler_flux(state_slab, axis_d):
    density = state_slab[0]
    momenta = state_slab[1:4]
    energy = state_slab[4]
    velocity = momenta / density[None]
    kinetic = 0.5 * jnp.sum(momenta * velocity, axis=0)
    pressure = (GAMMA_GAS - 1.0) * (energy - kinetic) - GAMMA_GAS * PRESSURE_INF
    normal_speed = velocity[axis_d]
    sound_speed = jnp.sqrt(GAMMA_GAS * (pressure + PRESSURE_INF) / density)
    rows_out = [momenta[axis_d]]
    for component in range(3):
        carried = momenta[component] * normal_speed
        if component == axis_d:
            carried = carried + pressure
        rows_out.append(carried)
    rows_out.append((energy + pressure) * normal_speed)
    return (jnp.stack(rows_out), jnp.abs(normal_speed) + sound_speed)


def face_difference(padded, axis_d, count_d):
    array_axis = axis_d + 1
    picker = [slice(None), slice(3, -3), slice(3, -3), slice(3, -3)]
    picker[array_axis] = slice(None)
    state_slab = padded[tuple(picker)]
    fluxes, speeds = euler_flux(state_slab, axis_d)
    cell_count = state_slab.shape[array_axis] - 6

    def shifted(values, offset, along):
        return lax.slice_in_dim(values, offset, offset + cell_count + 1, axis=along)

    wave_speed = shifted(speeds, 0, axis_d)
    for offset in range(1, 6):
        wave_speed = jnp.maximum(wave_speed, shifted(speeds, offset, axis_d))
    split_up = [
        0.5
        * (
            shifted(fluxes, offset, array_axis)
            + wave_speed[None] * shifted(state_slab, offset, array_axis)
        )
        for offset in range(6)
    ]
    split_down = [
        0.5
        * (
            shifted(fluxes, offset, array_axis)
            - wave_speed[None] * shifted(state_slab, offset, array_axis)
        )
        for offset in range(6)
    ]
    face_flux = weno_face(
        split_up[0], split_up[1], split_up[2], split_up[3], split_up[4]
    ) + weno_face(split_down[5], split_down[4], split_down[3], split_down[2], split_down[1])
    after = lax.slice_in_dim(face_flux, 1, cell_count + 1, axis=array_axis)
    before = lax.slice_in_dim(face_flux, 0, cell_count, axis=array_axis)
    return (after - before) * float(count_d)


def section_update(padded, old_block, counts, step_size):
    change = (
        face_difference(padded, 0, counts[0])
        + face_difference(padded, 1, counts[1])
        + face_difference(padded, 2, counts[2])
    )
    return 0.75 * old_block + 0.25 * (padded[:, 3:-3, 3:-3, 3:-3] - step_size * change)


def directions(angles):
    polar_angle = 0.5 * angles[0]
    azimuth = angles[1]
    return jnp.stack(
        [
            jnp.cos(polar_angle) * jnp.cos(azimuth),
            jnp.cos(polar_angle) * jnp.sin(azimuth),
            jnp.sin(polar_angle),
        ]
    )


def panel_places(cell_rows, block_x, block_y, block_z, cells_x, cells_y, cells_z, counts):
    along_x = cell_rows // (cells_y * cells_z)
    along_y = cell_rows // cells_z % cells_y
    along_z = cell_rows % cells_z
    place_x = ((block_x * cells_x + along_x).astype(jnp.float32) + 0.5) / counts[0]
    place_y = ((block_y * cells_y + along_y).astype(jnp.float32) + 0.5) / counts[1]
    place_z = ((block_z * cells_z + along_z).astype(jnp.float32) + 0.5) / counts[2]
    return jnp.stack([place_x, place_y, place_z], axis=1)


def dft_table(sample_count, freq_count):
    times = jnp.arange(sample_count, dtype=jnp.int32)[:, None]
    orders = jnp.arange(1, freq_count + 1, dtype=jnp.int32)[None, :]
    phases = 2.0 * math.pi / sample_count * (times * orders % sample_count).astype(jnp.float32)
    scaling = 1.0 / math.sqrt(sample_count)
    return (jnp.concatenate([jnp.cos(phases), -jnp.sin(phases)], axis=1) * scaling).astype(
        jnp.bfloat16
    )


def observer_group(sources, geometry, live_flags, dft_rows, listeners, wave_numbers):
    places = geometry[:, 0:3]
    normals = geometry[:, 3:6]
    spectra = jnp.einsum(
        "gpt,tk->gpk", sources, dft_rows, preferred_element_type=jnp.float32
    ).astype(jnp.bfloat16)
    offsets = listeners[None, :, :, None] - places[:, :, None, :]
    dist_sq = jnp.sum(offsets * offsets, axis=1)
    facing = jnp.sum(normals[:, :, None, :] * offsets, axis=1)
    weights = (facing / (4.0 * math.pi * dist_sq)).astype(jnp.bfloat16)
    product = jnp.einsum("gop,gpk->gok", weights, spectra, preferred_element_type=jnp.float32)
    centres = jnp.mean(places, axis=2)
    separation = listeners[None, :, :] - centres[:, :, None]
    centre_reach = jnp.sqrt(jnp.sum(separation * separation, axis=1))
    phase_now = centre_reach[:, :, None] * wave_numbers[None, None, :]
    cosine = jnp.cos(phase_now)
    sine_part = jnp.sin(phase_now)
    freq_count = wave_numbers.shape[0]
    real_part = product[:, :, :freq_count] * cosine + product[:, :, freq_count:] * sine_part
    imag_part = product[:, :, freq_count:] * cosine - product[:, :, :freq_count] * sine_part
    masks = live_flags[:, None, None]
    return jnp.stack([jnp.sum(masks * real_part, axis=0), jnp.sum(masks * imag_part, axis=0)])


def local(
    state_old,
    state_section,
    panel_record,
    panel_cell,
    panel_angles,
    owned_blocks,
    listener_angles,
    listener_range,
):
    cells_x = state_section.shape[1]
    cells_y = state_section.shape[2]
    cells_z = state_section.shape[3]
    counts = (
        cells_x * lax.axis_size("gx"),
        cells_y * lax.axis_size("gy"),
        cells_z * lax.axis_size("gz"),
    )
    step_size = COURANT / max(counts)
    padded = with_halo(state_section, (("gx", 1), ("gy", 2), ("gz", 3)), 3)
    updated = section_update(padded, state_old, counts, step_size)
    slot_count = panel_cell.shape[0]
    block_rows = panel_cell.shape[1]
    samples = panel_record.shape[1]
    density = updated[0].reshape(cells_x * cells_y * cells_z)
    sampled = density[panel_cell]
    sources = (
        panel_record.reshape(slot_count, block_rows, samples).astype(jnp.float32)
        * sampled[:, :, None]
    ).astype(jnp.bfloat16)
    places = panel_places(
        panel_cell,
        lax.axis_index("gx"),
        lax.axis_index("gy"),
        lax.axis_index("gz"),
        cells_x,
        cells_y,
        cells_z,
        counts,
    )
    normals = jnp.transpose(directions(panel_angles.reshape(2, slot_count, block_rows)), (1, 0, 2))
    geometry = jnp.concatenate([places, normals], axis=1)
    live_count = owned_blocks[0]
    live_flags = (jnp.arange(slot_count, dtype=jnp.int32) < live_count).astype(jnp.float32)
    dft_rows = dft_table(samples, FREQS)
    listeners = 0.5 + listener_range[None, :] * directions(listener_angles)
    wave_numbers = WAVE_STEP * jnp.arange(1, FREQS + 1, dtype=jnp.int32).astype(jnp.float32)

    def add_group(group_turn, running):
        first_row = group_turn * GROUP
        group_sources = lax.dynamic_slice_in_dim(sources, first_row, GROUP, 0)
        group_geometry = lax.dynamic_slice_in_dim(geometry, first_row, GROUP, 0)
        group_flags = lax.dynamic_slice_in_dim(live_flags, first_row, GROUP, 0)
        return running + observer_group(
            group_sources, group_geometry, group_flags, dft_rows, listeners, wave_numbers
        )

    group_total = (live_count + GROUP - 1) // GROUP
    running = lax.fori_loop(
        0, group_total, add_group, jnp.zeros((2, listeners.shape[1], FREQS), jnp.float32)
    )
    gz_share = lax.psum_scatter(running, "gz", scatter_dimension=1, tiled=True)
    spectra_out = lax.psum(gz_share, ("gx", "gy"))
    return (updated, spectra_out)


def solution(mesh):
    return jax.shard_map(
        local,
        mesh=mesh,
        in_specs=(
            P(None, "gx", "gy", "gz"),
            P(None, "gx", "gy", "gz"),
            P(("gx", "gy", "gz"), None),
            P(("gx", "gy", "gz"), None),
            P(None, ("gx", "gy", "gz")),
            P(("gx", "gy", "gz")),
            P(),
            P(),
        ),
        out_specs=(P(None, "gx", "gy", "gz"), P(None, "gz", None)),
        check_vma=False,
    )
```

profile of v0, /device:TPU:0, one launch (start us, length us, event | category | flops | bytes accessed | tf_op | source)
XLA Modules:
  0.0 390.7 jit_solution(911386908631650255)
XLA Ops:
  7.2 1.9 fusion.121
  9.1 3.0 collective-permute-start
  12.8 1.8 multiply_bitcast_fusion.1
  20.3 3.0 collective-permute-done.1
  24.4 1.9 collective-permute-start.2
  26.3 2.1 collective-permute-start.3
  28.4 7.8 %divide_add_fusion.2 = f32[5,17,32,128]{3,2,1,0:T(8,128)} fusion(f32[5,19,32,128]{3,2,1,0:T(8,128)S(1)} %get-tuple-element.123, f32[5,22,32,128]{3,2,1,0:T(8,128)S(1)} %multiply_dynamic-update-slice_fusion.1, f32[5,19,32,128]{3,2,1,0:T(8,128)S(1)} %get-tuple-element.116, f32[17,32,128]{2,1,0:T(8,128)S(1)} %slice_maximum_fusion.10), kind=kLoop, calls=%fused_computation.92 | loop fusion | flops 51179520 | bytes 18382848 | tf_op jit(solution)/shard_map/add | solution.py:105
  38.0 2.7 fusion.119
  42.2 3.3 copy.41
  45.5 3.3 copy.42
  50.5 11.8 %divide_add_fusion.1 = f32[5,16,33,128]{3,2,1,0:T(8,128)} fusion(f32[5,22,3,128]{3,2,1,0:T(4,128)} %copy-done.5, f32[5,22,32,128]{3,2,1,0:T(8,128)S(1)} %get-tuple-element.124, f32[5,16,38,128]{3,2,1,0:T(8,128)S(1)} %multiply_dynamic-update-slice_fusion.2, f32[5,22,3,128]{3,2,1,0:T(4,128)} %copy-done.3, f32[16,33,128]{2,1,0:T(8,128)} %slice_maximum_fusion.5), kind=kLoop, calls=%fused_computation.75 | loop fusion | flops 51701760 | bytes 11872256 | tf_op jit(solution)/shard_map/add | solution.py:105
  62.3 3.2 copy.43
  65.5 3.2 copy.44
  68.7 4.9 %pad_maximum_fusion = f32[5,22,38,134]{3,2,1,0:T(8,128)S(1)} fusion(f32[5,22,38,3]{3,2,1,0:T(8,128)} %copy.44, f32[5,22,3,128]{3,2,1,0:T(4,128)S(1)} %copy-done.6, f32[5,22,32,128]{3,2,1,0:T(8,128)S(1)} %get-tuple-element.124, f32[5,22,3,128]{3,2,1,0:T(4,128)S(1)} %copy-done.4, f32[5,22,38,3]{3,2,1,0:T(8,128)} %copy.43), kind=kLoop, calls=%fused_computation.34 | loop fusion | flops 2240480 | bytes 4480960 | tf_op jit(solution)/shard_map/concatenate | solution.py:28
  76.8 2.8 maximum_maximum_fusion
  79.6 15.3 %divide_add_fusion = f32[5,16,32,129]{3,2,1,0:T(8,128)S(1)} fusion(f32[5,22,38,131]{3,2,1,0:T(8,128)S(1)} %get-tuple-element.109, f32[5,16,32,134]{3,2,1,0:T(8,128)S(1)} %multiply_dynamic-update-slice_fusion, f32[5,22,38,131]{3,2,1,0:T(8,128)S(1)} %get-tuple-element.108, f32[16,32,129]{2,1,0:T(8,128)S(1)} %slice_maximum_fusion), kind=kLoop, calls=%fused_computation.49 | loop fusion | flops 48545280 | bytes 17436672 | tf_op jit(solution)/shard_map/add | solution.py:105
  95.8 23.0 %gather_fusion = f32[4096]{0:T(1024)S(1)} fusion(f32[65536]{0:T(1024)S(1)} %bitcast.126, s32[4096]{0:T(1024)S(1)} %fusion.111), kind=kCustom, calls=%fused_computation | custom fusion | bytes 49152 | tf_op jit(solution)/shard_map/gather | solution.py:203
  118.9 4.1 %fusion.23 = bf16[32,128,512]{2,1,0:T(8,128)(2,1)} fusion(bf16[32,128,512]{2,1,0:T(8,128)(2,1)} %bitcast.129, f32[32,128]{1,0:T(8,128)S(1)} %bitcast.133), kind=kLoop, calls=%fused_computation.33 | loop fusion | flops 6291456 | bytes 8404992 | tf_op jit(solution)/shard_map/convert_element_type | solution.py:207
  123.1 20.4 %while.11 = (s32[]{:T(128)}, f32[2,1024,128]{2,1,0:T(8,128)S(1)}, s32[]{:T(128)}, f32[32]{0:T(128)S(1)}, f32[32,6,128]{2,1,0:T(8,128)}, /*index=5*/f32[3,1024]{1...) while((s32[]{:T(128)}, f32[2,1024,128]{2,1,0:T(8,128)S(1)}, ...), condition=%wide.region_10.11_spmd.clone, body=%wide.region_3.10_spmd.clone.sunk | while | flops 417236864 | bytes 21886488 | solution.py:236
  124.2 2.9 fusion.131
  127.1 4.8 %fusion.132 = f32[4,1024,256]{2,1,0:T(8,128)} fusion(f32[4,1024,128]{2,1,0:T(8,128)} %get-tuple-element.195, f32[4,1024,128]{2,1,0:T(8,128)S(1)} %get-tuple-element.196, bf16[32,128,512]{2,1,0:T(8,128)(2,1)} %get-tuple-element.232, s32[]{:T(128)S(6)} %select_n.94, bf16[512,256]{1,0:T(8,128)(2,1)S(1)} %get-tuple-element.233), kind=kOutput, calls=%fused_computation.20.clone.1 | convolution fusion | flops 404357120 | bytes 9175044 | tf_op jit(solution)/shard_map/while/body/gop,gpk->gok/dot_general | solution.py:164
  132.2 11.0 %fusion.133 = (f32[1024,128]{1,0:T(8,128)S(1)}, f32[1024,128]{1,0:T(8,128)S(1)}) fusion(f32[4,1024,256]{2,1,0:T(8,128)} %fusion.132, f32[128]{0:T(128)S(1)} %convert_multiply_fusion.3, f32[4,1024]{1,0:T(4,128)S(1)} %sqrt.30, f32[4]{0:T(128)S(1)} %dynamic_slice.18), kind=kLoop, calls=%fused_computation.14.clone.1 | loop fusion | flops 5505024 | bytes 5259792 | tf_op jit(solution)/shard_map/while/body/reduce_sum | solution.py:175
  144.5 163.3 %reduce-scatter.2.cloned.1.call-done = f32[2,256,128]{2,1,0:T(8,128)} async-done(((f32[2,1024,128]{2,1,0:T(8,128)}), f32[2,256,128]{2,1,0:T(8,128)}) %reduce-scatter.2.cloned.1.call-update) | async-done | bytes 262160 | tf_op jit(solution)/shard_map/reduce_scatter | solution.py:239
  307.8 74.4 %all-reduce.2.cloned.1.call-done = f32[2,256,128]{2,1,0:T(8,128)} async-done(((f32[2,256,128]{2,1,0:T(8,128)}), f32[2,256,128]{2,1,0:T(8,128)}) %all-reduce.2.cloned.1.call-update) | async-done | bytes 262160 | tf_op jit(solution)/shard_map/psum | solution.py:240
  (95 shorter events, 19.8 us)
Async XLA Ops:
  7.2 12.8 %copy-start.10 = (f32[5,16,32,128]{3,2,1,0:T(8,128)S(1)}, f32[5,16,32,128]{3,2,1,0:T(8,128)}, u32[]{:S(2)}) copy-start(f32[5,16,32,128]{3,2,1,0:T(8,128)} %param.11) | copy-start | bytes 3932164
  7.2 10.3 %copy-start.14 = (s32[32,128]{1,0:T(8,128)S(1)}, s32[32,128]{1,0:T(8,128)}, u32[]{:S(2)}) copy-start(s32[32,128]{1,0:T(8,128)} %param.13) | copy-start | bytes 49156
  7.2 11.1 %copy-start.15 = (f32[1024]{0:T(1024)S(1)}, f32[1024]{0:T(1024)}, u32[]{:S(2)}) copy-start(f32[1024]{0:T(1024)} %param.17) | copy-start | bytes 12292
  7.2 300.6 %reduce-scatter.2.cloned.1.call-start = ((), (), s32[]{:S(2)}) async-start(), calls=%async_computation.1 | async-start | bytes 1310720 | tf_op jit(solution)/shard_map/reduce_scatter | solution.py:239
  9.1 9.9 %collective-permute-start = (f32[5,3,32,128]{3,2,1,0:T(8,128)S(1)}, f32[5,3,32,128]{3,2,1,0:T(8,128)}, u32[]{:S(2)}, u32[]{:S(2)}) collective-permute-start(f32[5,3,32,128]{3,2,1,0:T(8,128)S(1)} %get-tuple-element.120), channel_id=1, source_target_pairs={{0,16},{16,0},{1,17},{17,1},{2,18},{18,2},{3,19},{19,3},{4,20},{20... | collective-permute-start | bytes 737288 | tf_op jit(solution)/shard_map/ppermute | solution.py:26
  12.1 11.2 %collective-permute-start.1 = (f32[5,3,32,128]{3,2,1,0:T(8,128)}, f32[5,3,32,128]{3,2,1,0:T(8,128)S(1)}, u32[]{:S(2)}, u32[]{:S(2)}) collective-permute-start(f32[5,3,32,128]{3,2,1,0:T(8,128)} %get-tuple-element.119), channel_id=1, source_target_pairs={{16,0},{0,16},{17,1},{1,17},{18,2},{2,18},{19,3},{3,19},{20,4},{4,... | collective-permute-start | bytes 737288 | tf_op jit(solution)/shard_map/ppermute | solution.py:27
  24.4 11.8 %collective-permute-start.2 = (f32[5,22,3,128]{3,2,1,0:T(4,128)S(1)}, f32[5,22,3,128]{3,2,1,0:T(4,128)S(1)}, u32[]{:S(2)}, u32[]{:S(2)}) collective-permute-start(f32[5,22,3,128]{3,2,1,0:T(4,128)S(1)} %get-tuple-element.114), channel_id=1, source_target_pairs={{0,4},{4,8},{8,12},{12,0},{1,5},{5,9},{9,13},{13,1},{2,6},{6,10},{... | collective-permute-start | bytes 506888 | tf_op jit(solution)/shard_map/ppermute | solution.py:26
  26.3 10.9 %collective-permute-start.3 = (f32[5,22,3,128]{3,2,1,0:T(4,128)S(1)}, f32[5,22,3,128]{3,2,1,0:T(4,128)S(1)}, u32[]{:S(2)}, u32[]{:S(2)}) collective-permute-start(f32[5,22,3,128]{3,2,1,0:T(4,128)S(1)} %get-tuple-element.115), channel_id=1, source_target_pairs={{4,0},{8,4},{12,8},{0,12},{5,1},{9,5},{13,9},{1,13},{6,2},{10,6},{... | collective-permute-start | bytes 506888 | tf_op jit(solution)/shard_map/ppermute | solution.py:27
  36.2 1.4 copy-start.3
  37.2 0.7 copy-start.5
  45.5 16.8 %collective-permute-start.4 = (f32[5,22,38,3]{2,1,3,0:T(8,128)}, f32[5,22,38,3]{2,1,3,0:T(8,128)}, u32[]{:S(2)}, u32[]{:S(2)}) collective-permute-start(f32[5,22,38,3]{2,1,3,0:T(8,128)} %copy.41), channel_id=1, source_target_pairs={{0,1},{1,2},{2,3},{3,0},{4,5},{5,6},{6,7},{7,4},{8,9},{9,10},{10,1... | collective-permute-start | bytes 150488 | tf_op jit(solution)/shard_map/ppermute | solution.py:26
  48.7 16.7 %collective-permute-start.5 = (f32[5,22,38,3]{2,1,3,0:T(8,128)}, f32[5,22,38,3]{2,1,3,0:T(8,128)}, u32[]{:S(2)}, u32[]{:S(2)}) collective-permute-start(f32[5,22,38,3]{2,1,3,0:T(8,128)} %copy.42), channel_id=1, source_target_pairs={{1,0},{2,1},{3,2},{0,3},{5,4},{6,5},{7,6},{4,7},{9,8},{10,9},{11,1... | collective-permute-start | bytes 150488 | tf_op jit(solution)/shard_map/ppermute | solution.py:27
  65.5 3.2 copy-start.4
  65.5 3.2 copy-start.6
  68.7 4.9 %copy-start = (f32[5,22,38,3]{3,2,1,0:T(8,128)S(1)}, f32[5,22,38,3]{3,2,1,0:T(8,128)}, u32[]{:S(2)}) copy-start(f32[5,22,38,3]{3,2,1,0:T(8,128)} %copy.43) | copy-start | bytes 150484
  68.7 4.9 %copy-start.1 = (f32[5,22,38,3]{3,2,1,0:T(8,128)S(1)}, f32[5,22,38,3]{3,2,1,0:T(8,128)}, u32[]{:S(2)}) copy-start(f32[5,22,38,3]{3,2,1,0:T(8,128)} %copy.44) | copy-start | bytes 150484
  79.6 15.4 %copy-start.7 = (f32[5,17,32,128]{3,2,1,0:T(8,128)S(1)}, f32[5,17,32,128]{3,2,1,0:T(8,128)}, u32[]{:S(2)}) copy-start(f32[5,17,32,128]{3,2,1,0:T(8,128)} %divide_add_fusion.2) | copy-start | bytes 4177924
  79.6 15.4 %copy-start.8 = (f32[5,16,33,128]{3,2,1,0:T(8,128)S(1)}, f32[5,16,33,128]{3,2,1,0:T(8,128)}, u32[]{:S(2)}) copy-start(f32[5,16,33,128]{3,2,1,0:T(8,128)} %divide_add_fusion.1) | copy-start | bytes 4055044
  79.6 15.4 %copy-start.11 = (f32[5,16,32,128]{3,2,1,0:T(8,128)S(1)}, f32[5,16,32,128]{3,2,1,0:T(8,128)}, u32[]{:S(2)}) copy-start(f32[5,16,32,128]{3,2,1,0:T(8,128)} %param.11) | copy-start | bytes 3932164
  79.6 15.4 %copy-start.13 = (f32[5,16,32,128]{3,2,1,0:T(8,128)S(1)}, f32[5,16,32,128]{3,2,1,0:T(8,128)}, u32[]{:S(2)}) copy-start(f32[5,16,32,128]{3,2,1,0:T(8,128)} %param.10) | copy-start | bytes 3932164
  95.8 23.1 %copy-start.12 = (f32[5,16,32,128]{3,2,1,0:T(8,128)}, f32[5,16,32,128]{3,2,1,0:T(8,128)S(1)}, u32[]{:S(2)}) copy-start(f32[5,16,32,128]{3,2,1,0:T(8,128)S(1)} %fusion.54) | copy-start | bytes 3932164
  118.9 4.2 %copy-start.9 = (bf16[512,256]{1,0:T(8,128)(2,1)S(1)}, bf16[512,256]{1,0:T(8,128)(2,1)}, u32[]{:S(2)}) copy-start(bf16[512,256]{1,0:T(8,128)(2,1)} %fusion.60) | copy-start | bytes 786436
  143.4 1.0 copy-start.2
  144.5 237.7 %all-reduce.2.cloned.1.call-start = ((), (), s32[]{:S(2)}) async-start(), calls=%async_computation.2 | async-start | bytes 524288 | tf_op jit(solution)/shard_map/psum | solution.py:240
Sparse Core Ops, SparseCore 0:
  144.6 163.1 reduce-scatter.1
  311.1 70.9 all-reduce.1
where the time goes:
time: 393 us; the launch traced here: 391 us
  waiting for transfers between devices  242 us (62%)
  other arithmetic  73.8 us (19%)
  local copies, waits for them, and re-layouts  45.4 us (12%)
  between operations  15.2 us (4%)
  starting transfers between devices  8.79 us (2%)
  matrix products  4.77 us (1%)
    reduce_scatter x1, waiting for transfers between devices, local(): gz_share = lax.psum_scatter(running, 'gz', scatter_dimension=1, tiled=True)  163 us
    psum x1, waiting for transfers between devices, local(): spectra_out = lax.psum(gz_share, ('gx', 'gy'))  74.4 us
    add x3, other arithmetic, face_difference(): weno_face(split_up[0], split_up[1], split_up[2], split_up[3], split_up[4])  34.9 us
    gather x1, local copies, waits for them, and re-layouts, local(): sampled = density[panel_cell]  23 us
    reduce_sum x1, other arithmetic, observer_group(): jnp.sum(masks * real_part, axis=0)  11 us
    concatenate x3, other arithmetic, with_halo(): shard = jnp.concatenate([before, shard, after], axis=dim)  8.06 us
  transfers between devices with their start and end apart: 8, of which 5 were waited for; matrix products, arithmetic and copies ran while one was open for 8% of the time, Pallas kernels for 0%

commit v1 on v0

--- a/solution.py
+++ b/solution.py
@@ -2,11 +2,14 @@
 
 import jax
 import jax.numpy as jnp
+import numpy as np
 from jax import lax
+from jax.experimental import pallas as pl
+from jax.experimental.pallas import tpu as pltpu
 from jax.sharding import PartitionSpec as P
 
 FREQS = 128
-GROUP = 4
+NT = (((1,), (1,)), ((), ()))
 
 
 GAMMA_GAS = 4.4
@@ -142,37 +145,189 @@
 
 
 def dft_table(sample_count, freq_count):
-    times = jnp.arange(sample_count, dtype=jnp.int32)[:, None]
-    orders = jnp.arange(1, freq_count + 1, dtype=jnp.int32)[None, :]
-    phases = 2.0 * math.pi / sample_count * (times * orders % sample_count).astype(jnp.float32)
+    times = np.arange(sample_count, dtype=np.int64)[None, :]
+    orders = np.arange(1, freq_count + 1, dtype=np.int64)[:, None]
+    phases = (np.float32(2.0 * math.pi / sample_count) * (times * orders % sample_count).astype(np.float32)).astype(np.float64)
     scaling = 1.0 / math.sqrt(sample_count)
-    return (jnp.concatenate([jnp.cos(phases), -jnp.sin(phases)], axis=1) * scaling).astype(
-        jnp.bfloat16
-    )
-
-
-def observer_group(sources, geometry, live_flags, dft_rows, listeners, wave_numbers):
-    places = geometry[:, 0:3]
-    normals = geometry[:, 3:6]
-    spectra = jnp.einsum(
-        "gpt,tk->gpk", sources, dft_rows, preferred_element_type=jnp.float32
-    ).astype(jnp.bfloat16)
-    offsets = listeners[None, :, :, None] - places[:, :, None, :]
-    dist_sq = jnp.sum(offsets * offsets, axis=1)
-    facing = jnp.sum(normals[:, :, None, :] * offsets, axis=1)
-    weights = (facing / (4.0 * math.pi * dist_sq)).astype(jnp.bfloat16)
-    product = jnp.einsum("gop,gpk->gok", weights, spectra, preferred_element_type=jnp.float32)
-    centres = jnp.mean(places, axis=2)
-    separation = listeners[None, :, :] - centres[:, :, None]
-    centre_reach = jnp.sqrt(jnp.sum(separation * separation, axis=1))
-    phase_now = centre_reach[:, :, None] * wave_numbers[None, None, :]
-    cosine = jnp.cos(phase_now)
-    sine_part = jnp.sin(phase_now)
-    freq_count = wave_numbers.shape[0]
-    real_part = product[:, :, :freq_count] * cosine + product[:, :, freq_count:] * sine_part
-    imag_part = product[:, :, freq_count:] * cosine - product[:, :, :freq_count] * sine_part
-    masks = live_flags[:, None, None]
-    return jnp.stack([jnp.sum(masks * real_part, axis=0), jnp.sum(masks * imag_part, axis=0)])
+    both = np.concatenate([np.cos(phases), -np.sin(phases)], axis=0).astype(np.float32) * np.float32(scaling)
+    return jnp.asarray(both, jnp.bfloat16)
+
+
+def sincos_turns(turns):
+    r = turns - jnp.round(turns)
+    x = r * math.pi
+    x2 = x * x
+    s = 1.0 / 6227020800.0
+    s = s * x2 - 1.0 / 39916800.0
+    s = s * x2 + 1.0 / 362880.0
+    s = s * x2 - 1.0 / 5040.0
+    s = s * x2 + 1.0 / 120.0
+    s = s * x2 - 1.0 / 6.0
+    s = (s * x2) * x + x
+    c = 1.0 / 479001600.0
+    c = c * x2 - 1.0 / 3628800.0
+    c = c * x2 + 1.0 / 40320.0
+    c = c * x2 - 1.0 / 720.0
+    c = c * x2 + 1.0 / 24.0
+    c = c * x2 - 0.5
+    c = c * x2 + 1.0
+    s2 = s + s
+    return 1.0 - s2 * s, s2 * c
+
+
+def recip(d):
+    r = pl.reciprocal(d, approx=True)
+    return r * (2.0 - d * r)
+
+
+def panels_kernel(live, dens, rec, geo, cell, lis, table, out, dens3, lisb, sp, wts, prod, fine, coarse, acc):
+    slots, bp = cell.shape
+    rows = dens.shape[0]
+    tiles = lis.shape[1]
+    half = table.shape[0] // 2
+    count = live[0]
+
+    d = dens[...]
+    hi = d.astype(jnp.bfloat16)
+    left = d - hi.astype(jnp.float32)
+    mid = left.astype(jnp.bfloat16)
+    lo = (left - mid.astype(jnp.float32)).astype(jnp.bfloat16)
+    dens3[:, 0:128] = hi
+    dens3[:, 128:256] = mid
+    dens3[:, 256:384] = lo
+    for k in range(3):
+        for t in range(tiles):
+            row = lis[k, t : t + 1, :]
+            lisb[k, t * 128 : (t + 1) * 128, :] = jnp.transpose(jnp.broadcast_to(row, (128, 128)))
+    acc[...] = jnp.zeros(acc.shape, jnp.float32)
+    lane = lax.broadcasted_iota(jnp.int32, (128, 128), 1).astype(jnp.float32)
+
+    def spectrum(b, _):
+        cells = cell[pl.ds(b, 1), :]
+        high = (cells >> 7).astype(jnp.float32)
+        low = (cells & 127).astype(jnp.float32)
+        high_col = jnp.transpose(jnp.broadcast_to(high, (128, 128)))
+        low_col = jnp.transpose(jnp.broadcast_to(low, (128, 128)))
+        g = jnp.zeros((128, 384), jnp.float32)
+        for j in range(rows // 128):
+            onehot = jnp.where(high_col == lane + float(128 * j), 1.0, 0.0).astype(jnp.bfloat16)
+            g = g + jnp.dot(onehot, dens3[j * 128 : (j + 1) * 128, :], preferred_element_type=jnp.float32)
+        gs = (g[:, 0:128] + g[:, 128:256]) + g[:, 256:384]
+        sampled = jnp.sum(jnp.where(low_col == lane, gs, 0.0), axis=1, keepdims=True)
+        src = (rec[pl.ds(pl.multiple_of(b * bp, bp), bp), :].astype(jnp.float32) * sampled).astype(jnp.bfloat16)
+        sp[b] = lax.dot_general(table[...], src, NT, preferred_element_type=jnp.float32).astype(jnp.bfloat16)
+        return 0
+
+    lax.fori_loop(0, count, spectrum, 0)
+
+    sub8 = lax.broadcasted_iota(jnp.int32, (8, 128), 0).astype(jnp.float32) + 1.0
+    turn = WAVE_STEP / (2.0 * math.pi)
+
+    def block(b, _):
+        px, py, pz, nx, ny, nz = [geo[k, pl.ds(b, 1), :] for k in range(6)]
+        cx, cy, cz = [jnp.sum(v, axis=1, keepdims=True) * (1.0 / bp) for v in (px, py, pz)]
+        sx, sy, sz = lis[0] - cx, lis[1] - cy, lis[2] - cz
+        theta = jnp.sqrt(sx * sx + sy * sy + sz * sz) * turn
+        c1, s1 = sincos_turns(8.0 * theta)
+        cs = [None, (c1, s1)]
+        for a in range(2, half // 8):
+            (ca, sa), (cb, sb) = cs[a // 2], cs[a - a // 2]
+            cs.append((ca * cb - sa * sb, sa * cb + ca * sb))
+        for a in range(1, half // 8):
+            coarse[0, a] = cs[a][0]
+            coarse[1, a] = cs[a][1]
+        coarse[0, 0] = theta
+        for t in range(tiles):
+            th = jnp.broadcast_to(coarse[0, 0, t : t + 1, :], (8, 128)) * sub8
+            c, s = sincos_turns(th)
+            fine[0, t] = c
+            fine[1, t] = s
+        for r in range(0, tiles * 128, 16):
+            ox = lisb[0, r : r + 16, :] - px
+            oy = lisb[1, r : r + 16, :] - py
+            oz = lisb[2, r : r + 16, :] - pz
+            d2 = ox * ox + oy * oy + oz * oz
+            face = nx * ox + ny * oy + nz * oz
+            wts[r : r + 16, :] = (face * recip(d2)).astype(jnp.bfloat16)
+        for q in range(tiles // 2):
+            prod[q % 2] = lax.dot_general(sp[b], wts[q * 256 : (q + 1) * 256, :], NT, preferred_element_type=jnp.float32)
+            for u in range(2):
+                t = 2 * q + u
+                bc, bs = fine[0, t], fine[1, t]
+                for a in range(half // 8):
+                    if a == 0:
+                        c, s = bc, bs
+                    else:
+                        ec = jnp.broadcast_to(coarse[0, a, t : t + 1, :], (8, 128))
+                        es = jnp.broadcast_to(coarse[1, a, t : t + 1, :], (8, 128))
+                        c = ec * bc - es * bs
+                        s = es * bc + ec * bs
+                    re = prod[q % 2, a * 8 : a * 8 + 8, u * 128 : u * 128 + 128]
+                    im = prod[q % 2, half + a * 8 : half + a * 8 + 8, u * 128 : u * 128 + 128]
+                    acc[0, a * 8 : a * 8 + 8, t * 128 : t * 128 + 128] += re * c + im * s
+                    acc[1, a * 8 : a * 8 + 8, t * 128 : t * 128 + 128] += im * c - re * s
+        return 0
+
+    lax.fori_loop(0, count, block, 0)
+    shares = out.shape[0]
+    per = tiles // shares
+    for g in range(shares):
+        for k in range(2):
+            for t in range(per):
+                col = (g * per + t) * 128
+                out[g, k, t * 128 : (t + 1) * 128, :] = jnp.transpose(acc[k, :, col : col + 128])
+
+
+def panels(live, dens, rec, geo, cell, lis, table, shares):
+    slots, bp = cell.shape
+    rows = dens.shape[0]
+    tiles = lis.shape[1]
+    k2 = table.shape[0]
+    obs = tiles * 128
+    vm = pl.BlockSpec(memory_space=pltpu.VMEM)
+    return pl.pallas_call(
+        panels_kernel,
+        out_shape=jax.ShapeDtypeStruct((shares, 2, obs // shares, k2 // 2), jnp.float32),
+        in_specs=[pl.BlockSpec(memory_space=pltpu.SMEM)] + [vm] * 6,
+        out_specs=vm,
+        scratch_shapes=[
+            pltpu.VMEM((rows, 384), jnp.bfloat16),
+            pltpu.VMEM((3, obs, 128), jnp.float32),
+            pltpu.VMEM((slots, k2, bp), jnp.bfloat16),
+            pltpu.VMEM((obs, bp), jnp.bfloat16),
+            pltpu.VMEM((2, k2, 256), jnp.float32),
+            pltpu.VMEM((2, tiles, 8, 128), jnp.float32),
+            pltpu.VMEM((2, k2 // 16, tiles, 128), jnp.float32),
+            pltpu.VMEM((2, k2 // 2, obs), jnp.float32),
+        ],
+        name="panels",
+        compiler_params=pltpu.CompilerParams(vmem_limit_bytes=48 * 1024 * 1024),
+    )(live, dens, rec, geo, cell, lis, table)
+
+
+def swap(value, axis, bit):
+    size = lax.axis_size(axis)
+    return lax.ppermute(value, axis, [(i, i ^ bit) for i in range(size)])
+
+
+def reduce_spectra(shares):
+    size = shares.shape[0]
+    here = lax.axis_index("gz")
+    bit = 1
+    while bit < size:
+        pairs = shares.reshape((shares.shape[0] // 2, 2) + shares.shape[1:])
+        up = (here // bit) % 2
+        mine = lax.dynamic_index_in_dim(pairs, up, 1, keepdims=False)
+        theirs = lax.dynamic_index_in_dim(pairs, 1 - up, 1, keepdims=False)
+        shares = mine + swap(theirs, "gz", bit)
+        bit *= 2
+    total = shares[0]
+    for axis in ("gx", "gy"):
+        bit = 1
+        while bit < lax.axis_size(axis):
+            total = total + swap(total, axis, bit)
+            bit *= 2
+    return total
 
 
 def local(
@@ -199,12 +354,7 @@
     slot_count = panel_cell.shape[0]
     block_rows = panel_cell.shape[1]
     samples = panel_record.shape[1]
-    density = updated[0].reshape(cells_x * cells_y * cells_z)
-    sampled = density[panel_cell]
-    sources = (
-        panel_record.reshape(slot_count, block_rows, samples).astype(jnp.float32)
-        * sampled[:, :, None]
-    ).astype(jnp.bfloat16)
+    density = updated[0].reshape(cells_x * cells_y, cells_z)
     places = panel_places(
         panel_cell,
         lax.axis_index("gx"),
@@ -216,28 +366,22 @@
         counts,
     )
     normals = jnp.transpose(directions(panel_angles.reshape(2, slot_count, block_rows)), (1, 0, 2))
-    geometry = jnp.concatenate([places, normals], axis=1)
-    live_count = owned_blocks[0]
-    live_flags = (jnp.arange(slot_count, dtype=jnp.int32) < live_count).astype(jnp.float32)
-    dft_rows = dft_table(samples, FREQS)
+    geometry = jnp.transpose(
+        jnp.concatenate([places, normals * (0.25 / math.pi)], axis=1), (1, 0, 2)
+    )
     listeners = 0.5 + listener_range[None, :] * directions(listener_angles)
-    wave_numbers = WAVE_STEP * jnp.arange(1, FREQS + 1, dtype=jnp.int32).astype(jnp.float32)
-
-    def add_group(group_turn, running):
-        first_row = group_turn * GROUP
-        group_sources = lax.dynamic_slice_in_dim(sources, first_row, GROUP, 0)
-        group_geometry = lax.dynamic_slice_in_dim(geometry, first_row, GROUP, 0)
-        group_flags = lax.dynamic_slice_in_dim(live_flags, first_row, GROUP, 0)
-        return running + observer_group(
-            group_sources, group_geometry, group_flags, dft_rows, listeners, wave_numbers
-        )
-
-    group_total = (live_count + GROUP - 1) // GROUP
-    running = lax.fori_loop(
-        0, group_total, add_group, jnp.zeros((2, listeners.shape[1], FREQS), jnp.float32)
-    )
-    gz_share = lax.psum_scatter(running, "gz", scatter_dimension=1, tiled=True)
-    spectra_out = lax.psum(gz_share, ("gx", "gy"))
+    listeners = listeners.reshape(3, -1, 128)
+    shares = panels(
+        owned_blocks,
+        density,
+        panel_record,
+        geometry,
+        panel_cell,
+        listeners,
+        dft_table(samples, FREQS),
+        lax.axis_size("gz"),
+    )
+    spectra_out = reduce_spectra(shares)
     return (updated, spectra_out)
 
 

time: 393 us -> 177 us (0.45)
  waiting for transfers between devices: 242 us -> 39.6 us
  starting transfers between devices: 8.79 us -> 36 us
  local copies, waits for them, and re-layouts: 45.4 us -> 21.6 us
  Pallas kernels: 0 us -> 23.3 us
  other arithmetic: 73.8 us -> 54.5 us
  between operations: 15.2 us -> 1.82 us
  matrix products: 4.77 us -> 0 us
    reduce_scatter x1 -> x0, waiting for transfers between devices: 163 us -> none  [local(): gz_share = lax.psum_scatter(running, 'gz', scatter_dimension=1, tiled=True)]
    psum x1 -> x0, waiting for transfers between devices: 74.4 us -> none  [local(): spectra_out = lax.psum(gz_share, ('gx', 'gy'))]
    ppermute x0 -> x5, waiting for transfers between devices: none -> 34.8 us  [swap(): return lax.ppermute(value, axis, [(i, i ^ bit) for i in range(size)])]
    ppermute x0 -> x5, starting transfers between devices: none -> 27.3 us  [swap(): return lax.ppermute(value, axis, [(i, i ^ bit) for i in range(size)])]
    pallas_call x0 -> x1, Pallas kernels: none -> 23.3 us  [panels(): pl.pallas_call(panels_kernel, out_shape=jax.ShapeDtypeStruct((shares, 2,...]
    gather x1 -> x0, local copies, waits for them, and re-layouts: 23 us -> none  [local(): sampled = density[panel_cell]]
    reduce_sum x4 -> x0, other arithmetic: 14.9 us -> none  [the longest x1 11 us: observer_group(): jnp.sum(masks * real_part, axis=0)]
    convert_element_type x3 -> x0, other arithmetic: 4.82 us -> none  [the longest x1 4.07 us: local(): sources = (panel_record.reshape(slot_count, block_rows, samples).astype(j...]
  transfers between devices with their start and end apart: 8 -> 11, of which waited for: 5 -> 7; matrix products, arithmetic and copies ran while one was open for 8% -> 18% of each run, Pallas kernels for 0% -> 0%
where the time goes in v1:
time: 177 us
  other arithmetic  54.5 us (31%)
  waiting for transfers between devices  39.6 us (22%)
  starting transfers between devices  36 us (20%)
  Pallas kernels  23.3 us (13%)
  local copies, waits for them, and re-layouts  21.6 us (12%)
  between operations  1.82 us (1%)
    add x3, other arithmetic, face_difference(): weno_face(split_up[0], split_up[1], split_up[2], split_up[3], split_up[4])  34.9 us
    ppermute x5, waiting for transfers between devices, swap(): return lax.ppermute(value, axis, [(i, i ^ bit) for i in range(size)])  34.8 us
    ppermute x5, starting transfers between devices, swap(): return lax.ppermute(value, axis, [(i, i ^ bit) for i in range(size)])  27.3 us
    pallas_call x1, Pallas kernels, panels(): pl.pallas_call(panels_kernel, out_shape=jax.ShapeDtypeStruct((shares, 2,...  23.3 us
    concatenate x3, other arithmetic, with_halo(): shard = jnp.concatenate([before, shard, after], axis=dim)  8.08 us
    slice x3, local copies, waits for them, and re-layouts, with_halo(): last = lax.slice_in_dim(shard, length - width, length, axis=dim)  6.17 us
    slice x2, local copies, waits for them, and re-layouts, with_halo(): initial = lax.slice_in_dim(shard, 0, width, axis=dim)  5.17 us
    ppermute x3, starting transfers between devices, with_halo(): before = lax.ppermute(last, axis, up)  4.85 us
  transfers between devices with their start and end apart: 11, of which 7 were waited for; matrix products, arithmetic and copies ran while one was open for 18% of the time, Pallas kernels for 0%

profile of v1, /device:TPU:0, one launch (start us, length us, event | category | flops | bytes accessed | tf_op | source)
XLA Modules:
  0.0 176.9 jit_solution(15461321530530746710)
XLA Ops:
  0.6 1.9 %fusion.91 = (f32[5,3,32,128]{3,2,1,0:T(8,128)}, f32[5,3,32,128]{3,2,1,0:T(8,128)S(1)}) fusion(f32[5,16,32,128]{3,2,1,0:T(8,128)} %param.10), kind=kLoop, calls=%fused_computation.211 | loop fusion | bytes 983040 | tf_op jit(solution)/shard_map/slice | solution.py:28
  2.5 3.0 %collective-permute-start = (f32[5,3,32,128]{3,2,1,0:T(8,128)S(1)}, f32[5,3,32,128]{3,2,1,0:T(8,128)}, u32[]{:S(2)}, u32[]{:S(2)}) collective-permute-start(f32[5,3,32,128]{3,2,1,0:T(8,128)S(1)} %get-tuple-element.33), channel_id=1, source_target_pairs={{0,16},{16,0},{1,17},{17,1},{2,18},{18,2},{3,19},{19,3},{4,20},{20... | collective-permute-start | bytes 737288 | tf_op jit(solution)/shard_map/ppermute | solution.py:29
  10.5 1.9 %collective-permute-done = f32[5,3,32,128]{3,2,1,0:T(8,128)} collective-permute-done((f32[5,3,32,128]{3,2,1,0:T(8,128)S(1)}, f32[5,3,32,128]{3,2,1,0:T(8,128)}, u32[]{:S(2)}, u32[]{:S(2)}) %collective-permute-start) | collective-permute-done | bytes 245792 | tf_op jit(solution)/shard_map/ppermute | solution.py:29
  13.8 2.9 %collective-permute-done.1 = f32[5,3,32,128]{3,2,1,0:T(8,128)S(1)} collective-permute-done((f32[5,3,32,128]{3,2,1,0:T(8,128)}, f32[5,3,32,128]{3,2,1,0:T(8,128)S(1)}, u32[]{:S(2)}, u32[]{:S(2)}) %collective-permute-start.1) | collective-permute-done | bytes 245792 | tf_op jit(solution)/shard_map/ppermute | solution.py:30
  17.9 1.9 %collective-permute-start.2 = (f32[5,22,3,128]{3,1,2,0:T(8,128)S(1)}, f32[5,22,3,128]{3,1,2,0:T(8,128)S(1)}, u32[]{:S(2)}, u32[]{:S(2)}) collective-permute-start(f32[5,22,3,128]{3,1,2,0:T(8,128)S(1)} %copy.126), channel_id=1, source_target_pairs={{0,4},{4,8},{8,12},{12,0},{1,5},{5,9},{9,13},{13,1},{2,6},{6,10},{... | collective-permute-start | bytes 506888 | tf_op jit(solution)/shard_map/ppermute | solution.py:29
  19.8 2.1 %collective-permute-start.3 = (f32[5,22,3,128]{3,1,2,0:T(8,128)S(1)}, f32[5,22,3,128]{3,1,2,0:T(8,128)S(1)}, u32[]{:S(2)}, u32[]{:S(2)}) collective-permute-start(f32[5,22,3,128]{3,1,2,0:T(8,128)S(1)} %copy.127), channel_id=1, source_target_pairs={{4,0},{8,4},{12,8},{0,12},{5,1},{9,5},{13,9},{1,13},{6,2},{10,6},{... | collective-permute-start | bytes 506888 | tf_op jit(solution)/shard_map/ppermute | solution.py:30
  21.9 7.8 %divide_add_fusion.2 = f32[5,17,32,128]{3,2,1,0:T(8,128)} fusion(f32[5,19,32,128]{3,2,1,0:T(8,128)S(1)} %get-tuple-element.36, f32[5,22,32,128]{3,2,1,0:T(8,128)S(1)} %multiply_dynamic-update-slice_fusion.1, f32[5,19,32,128]{3,2,1,0:T(8,128)S(1)} %get-tuple-element.29, f32[17,32,128]{2,1,0:T(8,128)S(1)} %slice_maximum_fusion.10), kind=kLoop, calls=%fused_computation.58 | loop fusion | flops 51179520 | bytes 18382848 | tf_op jit(solution)/shard_map/add | solution.py:108
  30.5 2.8 %fusion.89 = (f32[5,22,38,3]{3,2,1,0:T(8,128)}, f32[5,22,38,3]{3,2,1,0:T(8,128)}) fusion(f32[5,22,38,128]{3,2,1,0:T(8,128)S(1)} %pad_maximum_fusion.2), kind=kLoop, calls=%fused_computation.209 | loop fusion | bytes 200640 | tf_op jit(solution)/shard_map/slice | solution.py:27
  34.8 3.3 %copy.120 = f32[5,22,38,3]{2,1,3,0:T(8,128)} copy(f32[5,22,38,3]{3,2,1,0:T(8,128)} %get-tuple-element.23) | data formatting | bytes 100320 | tf_op jit(solution)/shard_map/slice | solution.py:27
  38.1 3.3 %copy.121 = f32[5,22,38,3]{2,1,3,0:T(8,128)} copy(f32[5,22,38,3]{3,2,1,0:T(8,128)} %get-tuple-element.24) | data formatting | bytes 100320 | tf_op jit(solution)/shard_map/slice | solution.py:28
  43.1 11.8 %divide_add_fusion.1 = f32[5,16,33,128]{3,2,1,0:T(8,128)} fusion(f32[5,22,3,128]{3,2,1,0:T(4,128)} %copy-done.7, f32[5,22,32,128]{3,2,1,0:T(8,128)S(1)} %get-tuple-element.37, f32[5,16,38,128]{3,2,1,0:T(8,128)S(1)} %multiply_dynamic-update-slice_fusion.2, f32[5,22,3,128]{3,2,1,0:T(4,128)} %copy-done.5, f32[16,33,128]{2,1,0:T(8,128)} %slice_maximum_fusion.5), kind=kLoop, calls=%fused_computation.41 | loop fusion | flops 51701760 | bytes 11872256 | tf_op jit(solution)/shard_map/add | solution.py:108
  54.9 3.2 %copy.122 = f32[5,22,38,3]{3,2,1,0:T(8,128)} copy(f32[5,22,38,3]{2,1,3,0:T(8,128)} %collective-permute-done.4) | data formatting | bytes 100320 | tf_op jit(solution)/shard_map/ppermute | solution.py:29
  58.1 3.3 %copy.123 = f32[5,22,38,3]{3,2,1,0:T(8,128)} copy(f32[5,22,38,3]{2,1,3,0:T(8,128)} %collective-permute-done.5) | data formatting | bytes 100320 | tf_op jit(solution)/shard_map/ppermute | solution.py:30
  61.4 4.9 %pad_maximum_fusion = f32[5,22,38,134]{3,2,1,0:T(8,128)S(1)} fusion(f32[5,22,38,3]{3,2,1,0:T(8,128)} %copy.123, f32[5,22,3,128]{3,2,1,0:T(4,128)S(1)} %copy-done.8, f32[5,22,32,128]{3,2,1,0:T(8,128)S(1)} %get-tuple-element.37, f32[5,22,3,128]{3,2,1,0:T(4,128)S(1)} %copy-done.6, f32[5,22,38,3]{3,2,1,0:T(8,128)} %copy.122), kind=kLoop, calls=%fused_computation | loop fusion | flops 2240480 | bytes 4480960 | tf_op jit(solution)/shard_map/concatenate | solution.py:31
  66.9 2.8 %maximum_maximum_fusion = (f32[5,22,38,131]{3,2,1,0:T(8,128)S(1)}, f32[5,22,38,131]{3,2,1,0:T(8,128)S(1)}) fusion(f32[5,22,3,128]{3,2,1,0:T(4,128)S(1)} %copy-done.8, f32[5,22,32,128]{3,2,1,0:T(8,128)S(1)} %get-tuple-element.37, f32[5,22,3,128]{3,2,1,0:T(4,128)S(1)} %copy-done.6, f32[5,22,38,3]{3,2,1,0:T(8,128)S(1)} %copy-done.3, ...), kind=kLoop, calls=%fused_computation.1 | loop fusion | flops 3285480 | bytes 6621120 | tf_op jit(solution)/shard_map/concatenate | solution.py:31
  72.4 15.3 %divide_add_fusion = f32[5,16,32,129]{3,2,1,0:T(8,128)S(1)} fusion(f32[5,22,38,131]{3,2,1,0:T(8,128)S(1)} %get-tuple-element.22, f32[5,16,32,134]{3,2,1,0:T(8,128)S(1)} %multiply_dynamic-update-slice_fusion, f32[5,22,38,131]{3,2,1,0:T(8,128)S(1)} %get-tuple-element.21, f32[16,32,129]{2,1,0:T(8,128)S(1)} %slice_maximum_fusion), kind=kLoop, calls=%fused_computation.15 | loop fusion | flops 48545280 | bytes 17436672 | tf_op jit(solution)/shard_map/add | solution.py:108
  90.4 23.3 %panels.1 = f32[4,2,256,128]{3,2,1,0:T(8,128)S(1)} custom-call(s32[1]{0:T(128)S(6)} %copy.144.live, f32[512,128]{1,0:T(8,128)S(1)} %bitcast.115, bf16[4096,512]{1,0:T(8,128)(2,1)S(1)} %copy-done, f32[6,32,128]{2,1,0:T(8,128)S(1)} %maximum_bitcast_fusion.1.geo, s32[32,128]{1,0:T(8,128)S(1)} %copy-done.2, f32[3,8,128]{2,1,0:T(8,128)S(1)} %fusion.83.lis, ...), custom_call_target="tpu_custom_call" | custom-call | tf_op jit(solution)/shard_map/panels/pallas_call | solution.py:288
  113.9 1.9 %collective-permute-done.6 = f32[2,2,256,128]{3,2,1,0:T(8,128)S(1)} collective-permute-done((f32[2,2,256,128]{3,2,1,0:T(8,128)S(1)}, f32[2,2,256,128]{3,2,1,0:T(8,128)S(1)}, u32[]{:S(2)}, u32[]{:S(2)}) %collective-permute-start.6) | collective-permute-done | bytes 524320 | tf_op jit(solution)/shard_map/ppermute | solution.py:310
  115.9 3.3 %collective-permute-start.7 = (f32[1,2,256,128]{3,2,1,0:T(8,128)S(1)}, f32[1,2,256,128]{3,2,1,0:T(8,128)S(1)}, u32[]{:S(2)}, u32[]{:S(2)}) collective-permute-start(f32[1,2,256,128]{3,2,1,0:T(8,128)S(1)} %constant_dynamic-slice_fusion), channel_id=1, source_target_pairs={{0,2},{1,3},{2,0},{3,1},{4,6},{5,7},{6,4},{7,5},{8,10},{9,11},{10,... | collective-permute-start | bytes 786440 | tf_op jit(solution)/shard_map/ppermute | solution.py:310
  119.2 6.6 %collective-permute-done.7 = f32[1,2,256,128]{3,2,1,0:T(8,128)S(1)} collective-permute-done((f32[1,2,256,128]{3,2,1,0:T(8,128)S(1)}, f32[1,2,256,128]{3,2,1,0:T(8,128)S(1)}, u32[]{:S(2)}, u32[]{:S(2)}) %collective-permute-start.7) | collective-permute-done | bytes 262176 | tf_op jit(solution)/shard_map/ppermute | solution.py:310
  125.9 7.8 %collective-permute-done.8 = f32[2,256,128]{2,1,0:T(8,128)S(1)} collective-permute-done((f32[2,256,128]{2,1,0:T(8,128)S(1)}, f32[2,256,128]{2,1,0:T(8,128)S(1)}, u32[]{:S(2)}, u32[]{:S(2)}) %collective-permute-start.8) | collective-permute-done | bytes 262176 | tf_op jit(solution)/shard_map/ppermute | solution.py:310
  133.7 23.8 %collective-permute-start.9 = (f32[2,256,128]{2,1,0:T(8,128)S(1)}, f32[2,256,128]{2,1,0:T(8,128)S(1)}, u32[]{:S(2)}, u32[]{:S(2)}) collective-permute-start(f32[2,256,128]{2,1,0:T(8,128)S(1)} %add.728), channel_id=1, source_target_pairs={{0,4},{4,0},{8,12},{12,8},{1,5},{5,1},{9,13},{13,9},{2,6},{6,2},{1... | collective-permute-start | bytes 786440 | tf_op jit(solution)/shard_map/ppermute | solution.py:310
  157.5 5.5 %collective-permute-done.9 = f32[2,256,128]{2,1,0:T(8,128)S(1)} collective-permute-done((f32[2,256,128]{2,1,0:T(8,128)S(1)}, f32[2,256,128]{2,1,0:T(8,128)S(1)}, u32[]{:S(2)}, u32[]{:S(2)}) %collective-permute-start.9) | collective-permute-done | bytes 262176 | tf_op jit(solution)/shard_map/ppermute | solution.py:310
  163.0 13.1 %collective-permute-done.10 = f32[2,256,128]{2,1,0:T(8,128)S(1)} collective-permute-done((f32[2,256,128]{2,1,0:T(8,128)S(1)}, f32[2,256,128]{2,1,0:T(8,128)S(1)}, u32[]{:S(2)}, u32[]{:S(2)}) %collective-permute-start.10) | collective-permute-done | bytes 262176 | tf_op jit(solution)/shard_map/ppermute | solution.py:310
  (88 shorter events, 17.8 us)
Async XLA Ops:
  0.6 12.8 %copy-start.11 = (f32[5,16,32,128]{3,2,1,0:T(8,128)S(1)}, f32[5,16,32,128]{3,2,1,0:T(8,128)}, u32[]{:S(2)}) copy-start(f32[5,16,32,128]{3,2,1,0:T(8,128)} %param.10) | copy-start | bytes 3932164
  2.5 9.9 %collective-permute-start = (f32[5,3,32,128]{3,2,1,0:T(8,128)S(1)}, f32[5,3,32,128]{3,2,1,0:T(8,128)}, u32[]{:S(2)}, u32[]{:S(2)}) collective-permute-start(f32[5,3,32,128]{3,2,1,0:T(8,128)S(1)} %get-tuple-element.33), channel_id=1, source_target_pairs={{0,16},{16,0},{1,17},{17,1},{2,18},{18,2},{3,19},{19,3},{4,20},{20... | collective-permute-start | bytes 737288 | tf_op jit(solution)/shard_map/ppermute | solution.py:29
  5.5 11.2 %collective-permute-start.1 = (f32[5,3,32,128]{3,2,1,0:T(8,128)}, f32[5,3,32,128]{3,2,1,0:T(8,128)S(1)}, u32[]{:S(2)}, u32[]{:S(2)}) collective-permute-start(f32[5,3,32,128]{3,2,1,0:T(8,128)} %get-tuple-element.32), channel_id=1, source_target_pairs={{16,0},{0,16},{17,1},{1,17},{18,2},{2,18},{19,3},{3,19},{20,4},{4,... | collective-permute-start | bytes 737288 | tf_op jit(solution)/shard_map/ppermute | solution.py:30
  17.9 11.8 %collective-permute-start.2 = (f32[5,22,3,128]{3,1,2,0:T(8,128)S(1)}, f32[5,22,3,128]{3,1,2,0:T(8,128)S(1)}, u32[]{:S(2)}, u32[]{:S(2)}) collective-permute-start(f32[5,22,3,128]{3,1,2,0:T(8,128)S(1)} %copy.126), channel_id=1, source_target_pairs={{0,4},{4,8},{8,12},{12,0},{1,5},{5,9},{9,13},{13,1},{2,6},{6,10},{... | collective-permute-start | bytes 506888 | tf_op jit(solution)/shard_map/ppermute | solution.py:29
  19.8 10.0 %collective-permute-start.3 = (f32[5,22,3,128]{3,1,2,0:T(8,128)S(1)}, f32[5,22,3,128]{3,1,2,0:T(8,128)S(1)}, u32[]{:S(2)}, u32[]{:S(2)}) collective-permute-start(f32[5,22,3,128]{3,1,2,0:T(8,128)S(1)} %copy.127), channel_id=1, source_target_pairs={{4,0},{8,4},{12,8},{0,12},{5,1},{9,5},{13,9},{1,13},{6,2},{10,6},{... | collective-permute-start | bytes 506888 | tf_op jit(solution)/shard_map/ppermute | solution.py:30
  38.1 16.8 %collective-permute-start.4 = (f32[5,22,38,3]{2,1,3,0:T(8,128)}, f32[5,22,38,3]{2,1,3,0:T(8,128)}, u32[]{:S(2)}, u32[]{:S(2)}) collective-permute-start(f32[5,22,38,3]{2,1,3,0:T(8,128)} %copy.120), channel_id=1, source_target_pairs={{0,1},{1,2},{2,3},{3,0},{4,5},{5,6},{6,7},{7,4},{8,9},{9,10},{10,1... | collective-permute-start | bytes 150488 | tf_op jit(solution)/shard_map/ppermute | solution.py:29
  41.4 16.7 %collective-permute-start.5 = (f32[5,22,38,3]{2,1,3,0:T(8,128)}, f32[5,22,38,3]{2,1,3,0:T(8,128)}, u32[]{:S(2)}, u32[]{:S(2)}) collective-permute-start(f32[5,22,38,3]{2,1,3,0:T(8,128)} %copy.121), channel_id=1, source_target_pairs={{1,0},{2,1},{3,2},{0,3},{5,4},{6,5},{7,6},{4,7},{9,8},{10,9},{11,1... | collective-permute-start | bytes 150488 | tf_op jit(solution)/shard_map/ppermute | solution.py:30
  58.1 3.3 %copy-start.6 = (f32[5,22,3,128]{3,2,1,0:T(4,128)S(1)}, f32[5,22,3,128]{3,2,1,0:T(4,128)}, u32[]{:S(2)}) copy-start(f32[5,22,3,128]{3,2,1,0:T(4,128)} %copy-done.5) | copy-start | bytes 506884
  58.1 3.3 %copy-start.8 = (f32[5,22,3,128]{3,2,1,0:T(4,128)S(1)}, f32[5,22,3,128]{3,2,1,0:T(4,128)}, u32[]{:S(2)}) copy-start(f32[5,22,3,128]{3,2,1,0:T(4,128)} %copy-done.7) | copy-start | bytes 506884
  61.4 4.9 %copy-start.3 = (f32[5,22,38,3]{3,2,1,0:T(8,128)S(1)}, f32[5,22,38,3]{3,2,1,0:T(8,128)}, u32[]{:S(2)}) copy-start(f32[5,22,38,3]{3,2,1,0:T(8,128)} %copy.122) | copy-start | bytes 150484
  61.4 4.9 %copy-start.4 = (f32[5,22,38,3]{3,2,1,0:T(8,128)S(1)}, f32[5,22,38,3]{3,2,1,0:T(8,128)}, u32[]{:S(2)}) copy-start(f32[5,22,38,3]{3,2,1,0:T(8,128)} %copy.123) | copy-start | bytes 150484
  72.3 15.4 %copy-start.9 = (f32[5,17,32,128]{3,2,1,0:T(8,128)S(1)}, f32[5,17,32,128]{3,2,1,0:T(8,128)}, u32[]{:S(2)}) copy-start(f32[5,17,32,128]{3,2,1,0:T(8,128)} %divide_add_fusion.2) | copy-start | bytes 4177924
  72.3 15.4 %copy-start.10 = (f32[5,16,33,128]{3,2,1,0:T(8,128)S(1)}, f32[5,16,33,128]{3,2,1,0:T(8,128)}, u32[]{:S(2)}) copy-start(f32[5,16,33,128]{3,2,1,0:T(8,128)} %divide_add_fusion.1) | copy-start | bytes 4055044
  72.3 15.4 %copy-start.12 = (f32[5,16,32,128]{3,2,1,0:T(8,128)S(1)}, f32[5,16,32,128]{3,2,1,0:T(8,128)}, u32[]{:S(2)}) copy-start(f32[5,16,32,128]{3,2,1,0:T(8,128)} %param.10) | copy-start | bytes 3932164
  72.4 15.4 %copy-start.14 = (f32[5,16,32,128]{3,2,1,0:T(8,128)S(1)}, f32[5,16,32,128]{3,2,1,0:T(8,128)}, u32[]{:S(2)}) copy-start(f32[5,16,32,128]{3,2,1,0:T(8,128)} %param.9) | copy-start | bytes 3932164
  87.8 2.7 %copy-start = (bf16[4096,512]{1,0:T(8,128)(2,1)S(1)}, bf16[4096,512]{1,0:T(8,128)(2,1)}, u32[]{:S(2)}) copy-start(bf16[4096,512]{1,0:T(8,128)(2,1)} %rec.1) | copy-start | bytes 12582916
  87.8 2.7 %copy-start.1 = (bf16[256,512]{1,0:T(8,128)(2,1)S(1)}, bf16[256,512]{1,0:T(8,128)(2,1)}, u32[]{:S(2)}) copy-start(bf16[256,512]{1,0:T(8,128)(2,1)} %constant.304.clone.table) | copy-start | bytes 786436
  87.8 2.7 %copy-start.2 = (s32[32,128]{1,0:T(8,128)S(1)}, s32[32,128]{1,0:T(8,128)}, u32[]{:S(2)}) copy-start(s32[32,128]{1,0:T(8,128)} %cell.1) | copy-start | bytes 49156
  88.7 25.1 %copy-start.13 = (f32[5,16,32,128]{3,2,1,0:T(8,128)}, f32[5,16,32,128]{3,2,1,0:T(8,128)S(1)}, u32[]{:S(2)}) copy-start(f32[5,16,32,128]{3,2,1,0:T(8,128)S(1)} %fusion.30) | copy-start | bytes 3932164
  113.8 2.0 %collective-permute-start.6 = (f32[2,2,256,128]{3,2,1,0:T(8,128)S(1)}, f32[2,2,256,128]{3,2,1,0:T(8,128)S(1)}, u32[]{:S(2)}, u32[]{:S(2)}) collective-permute-start(f32[2,2,256,128]{3,2,1,0:T(8,128)S(1)} %dynamic-slice_bitcast_fusion), channel_id=1, source_target_pairs={{0,1},{1,0},{2,3},{3,2},{4,5},{5,4},{6,7},{7,6},{8,9},{9,8},{10,11... | collective-permute-start | bytes 1572872 | tf_op jit(solution)/shard_map/ppermute | solution.py:310
  115.9 9.9 %collective-permute-start.7 = (f32[1,2,256,128]{3,2,1,0:T(8,128)S(1)}, f32[1,2,256,128]{3,2,1,0:T(8,128)S(1)}, u32[]{:S(2)}, u32[]{:S(2)}) collective-permute-start(f32[1,2,256,128]{3,2,1,0:T(8,128)S(1)} %constant_dynamic-slice_fusion), channel_id=1, source_target_pairs={{0,2},{1,3},{2,0},{3,1},{4,6},{5,7},{6,4},{7,5},{8,10},{9,11},{10,... | collective-permute-start | bytes 786440 | tf_op jit(solution)/shard_map/ppermute | solution.py:310
  125.8 7.8 %collective-permute-start.8 = (f32[2,256,128]{2,1,0:T(8,128)S(1)}, f32[2,256,128]{2,1,0:T(8,128)S(1)}, u32[]{:S(2)}, u32[]{:S(2)}) collective-permute-start(f32[2,256,128]{2,1,0:T(8,128)S(1)} %add_bitcast_fusion), channel_id=1, source_target_pairs={{0,16},{16,0},{1,17},{17,1},{2,18},{18,2},{3,19},{19,3},{4,20},{20... | collective-permute-start | bytes 786440 | tf_op jit(solution)/shard_map/ppermute | solution.py:310
  133.7 29.3 %collective-permute-start.9 = (f32[2,256,128]{2,1,0:T(8,128)S(1)}, f32[2,256,128]{2,1,0:T(8,128)S(1)}, u32[]{:S(2)}, u32[]{:S(2)}) collective-permute-start(f32[2,256,128]{2,1,0:T(8,128)S(1)} %add.728), channel_id=1, source_target_pairs={{0,4},{4,0},{8,12},{12,8},{1,5},{5,1},{9,13},{13,9},{2,6},{6,2},{1... | collective-permute-start | bytes 786440 | tf_op jit(solution)/shard_map/ppermute | solution.py:310
  163.0 13.2 %collective-permute-start.10 = (f32[2,256,128]{2,1,0:T(8,128)S(1)}, f32[2,256,128]{2,1,0:T(8,128)S(1)}, u32[]{:S(2)}, u32[]{:S(2)}) collective-permute-start(f32[2,256,128]{2,1,0:T(8,128)S(1)} %add.729), channel_id=1, source_target_pairs={{0,8},{4,12},{8,0},{12,4},{1,9},{5,13},{9,1},{13,5},{2,10},{6,14},... | collective-permute-start | bytes 786440 | tf_op jit(solution)/shard_map/ppermute | solution.py:310
  (2 other events, 1.4 us)

commit v2 on v1

--- a/solution.py
+++ b/solution.py
@@ -1,3 +1,4 @@
+import functools
 import math
 
 import jax
@@ -19,107 +20,232 @@
 COURANT = 0.08
 
 
-def with_halo(shard, sides, width):
-    for axis, dim in sides:
-        size, length = (lax.axis_size(axis), shard.shape[dim])
-        up = [(i, (i + 1) % size) for i in range(size)]
-        down = [(j, i) for i, j in up]
-        last = lax.slice_in_dim(shard, length - width, length, axis=dim)
-        initial = lax.slice_in_dim(shard, 0, width, axis=dim)
-        before = lax.ppermute(last, axis, up)
-        after = lax.ppermute(initial, axis, down)
-        shard = jnp.concatenate([before, shard, after], axis=dim)
-    return shard
-
-
-def weno_face(far_left, near_left, middle, near_right, far_right):
-    cand_a = (2.0 * far_left - 7.0 * near_left + 11.0 * middle) / 6.0
-    cand_b = (-near_left + 5.0 * middle + 2.0 * near_right) / 6.0
-    cand_c = (2.0 * middle + 5.0 * near_right - far_right) / 6.0
-    rough_a = (
-        13.0 / 12.0 * (far_left - 2.0 * near_left + middle) ** 2
-        + 0.25 * (far_left - 4.0 * near_left + 3.0 * middle) ** 2
-    )
-    rough_b = (
-        13.0 / 12.0 * (near_left - 2.0 * middle + near_right) ** 2
-        + 0.25 * (near_left - near_right) ** 2
-    )
-    rough_c = (
-        13.0 / 12.0 * (middle - 2.0 * near_right + far_right) ** 2
-        + 0.25 * (3.0 * middle - 4.0 * near_right + far_right) ** 2
-    )
-    weight_a = 0.1 / (WENO_EPS + rough_a) ** 2
-    weight_b = 0.6 / (WENO_EPS + rough_b) ** 2
-    weight_c = 0.3 / (WENO_EPS + rough_c) ** 2
-    return (weight_a * cand_a + weight_b * cand_b + weight_c * cand_c) / (
-        weight_a + weight_b + weight_c
-    )
-
-
-def euler_flux(state_slab, axis_d):
-    density = state_slab[0]
-    momenta = state_slab[1:4]
-    energy = state_slab[4]
-    velocity = momenta / density[None]
-    kinetic = 0.5 * jnp.sum(momenta * velocity, axis=0)
-    pressure = (GAMMA_GAS - 1.0) * (energy - kinetic) - GAMMA_GAS * PRESSURE_INF
-    normal_speed = velocity[axis_d]
-    sound_speed = jnp.sqrt(GAMMA_GAS * (pressure + PRESSURE_INF) / density)
-    rows_out = [momenta[axis_d]]
-    for component in range(3):
-        carried = momenta[component] * normal_speed
-        if component == axis_d:
-            carried = carried + pressure
-        rows_out.append(carried)
-    rows_out.append((energy + pressure) * normal_speed)
-    return (jnp.stack(rows_out), jnp.abs(normal_speed) + sound_speed)
-
-
-def face_difference(padded, axis_d, count_d):
-    array_axis = axis_d + 1
-    picker = [slice(None), slice(3, -3), slice(3, -3), slice(3, -3)]
-    picker[array_axis] = slice(None)
-    state_slab = padded[tuple(picker)]
-    fluxes, speeds = euler_flux(state_slab, axis_d)
-    cell_count = state_slab.shape[array_axis] - 6
-
-    def shifted(values, offset, along):
-        return lax.slice_in_dim(values, offset, offset + cell_count + 1, axis=along)
-
-    wave_speed = shifted(speeds, 0, axis_d)
-    for offset in range(1, 6):
-        wave_speed = jnp.maximum(wave_speed, shifted(speeds, offset, axis_d))
-    split_up = [
-        0.5
-        * (
-            shifted(fluxes, offset, array_axis)
-            + wave_speed[None] * shifted(state_slab, offset, array_axis)
-        )
-        for offset in range(6)
-    ]
-    split_down = [
-        0.5
-        * (
-            shifted(fluxes, offset, array_axis)
-            - wave_speed[None] * shifted(state_slab, offset, array_axis)
-        )
-        for offset in range(6)
-    ]
-    face_flux = weno_face(
-        split_up[0], split_up[1], split_up[2], split_up[3], split_up[4]
-    ) + weno_face(split_down[5], split_down[4], split_down[3], split_down[2], split_down[1])
-    after = lax.slice_in_dim(face_flux, 1, cell_count + 1, axis=array_axis)
-    before = lax.slice_in_dim(face_flux, 0, cell_count, axis=array_axis)
-    return (after - before) * float(count_d)
-
-
-def section_update(padded, old_block, counts, step_size):
-    change = (
-        face_difference(padded, 0, counts[0])
-        + face_difference(padded, 1, counts[1])
-        + face_difference(padded, 2, counts[2])
-    )
-    return 0.75 * old_block + 0.25 * (padded[:, 3:-3, 3:-3, 3:-3] - step_size * change)
+def pack_kernel(state, turned, zlo, zhi, ylo, yhi, xlo, xhi, *, cx, cy, cz):
+    plane = cx * cy
+    groups = plane // 128
+    for c in range(5):
+        for g in range(groups):
+            row = c * plane + g * 128
+            turned[row : row + cz, :] = jnp.transpose(state[row : row + 128, :])
+        for k in range(3):
+            ylo[(c * 3 + k) * cx : (c * 3 + k + 1) * cx, :] = state[pl.ds(c * plane + k, cx, stride=cy), :]
+            yhi[(c * 3 + k) * cx : (c * 3 + k + 1) * cx, :] = state[pl.ds(c * plane + cy - 3 + k, cx, stride=cy), :]
+            zlo[(c * 3 + k) * groups : (c * 3 + k + 1) * groups, :] = turned[pl.ds(c * plane + k, groups, stride=128), :]
+            zhi[(c * 3 + k) * groups : (c * 3 + k + 1) * groups, :] = turned[pl.ds(c * plane + cz - 3 + k, groups, stride=128), :]
+        xlo[c * 3 * cy : (c + 1) * 3 * cy, :] = state[c * plane : c * plane + 3 * cy, :]
+        xhi[c * 3 * cy : (c + 1) * 3 * cy, :] = state[c * plane + (cx - 3) * cy : (c + 1) * plane, :]
+
+
+def pack(state, cx, cy, cz):
+    groups = cx * cy // 128
+    rows = [state.shape[0]] + [15 * groups] * 2 + [15 * cx] * 2 + [15 * cy] * 2
+    vm = pl.BlockSpec(memory_space=pltpu.VMEM)
+    return pl.pallas_call(
+        functools.partial(pack_kernel, cx=cx, cy=cy, cz=cz),
+        out_shape=[jax.ShapeDtypeStruct((r, 128), jnp.float32) for r in rows],
+        in_specs=[vm],
+        out_specs=[vm] * 7,
+        name="pack",
+    )(state)
+
+
+def weno_shift(d1, d2, d3, d4):
+    a0, a1, a2 = d2 - d1, d3 - d2, d4 - d3
+    h2, h3 = 0.75 * d2, 0.75 * d3
+    eps = 3.0 * WENO_EPS
+    e0 = (a0 * a0 + eps) + h2 * (d2 + a0)
+    e1 = (a1 * a1 + eps) + h2 * d3
+    e2 = (a2 * a2 + eps) + h3 * (d3 - a2)
+    t1 = e1 * e1
+    u0 = 3.0 * (e0 * e0)
+    u2 = 2.0 * (e2 * e2)
+    w0, w1, w2 = t1 * u2, u0 * u2, u0 * t1
+    below = 0.5 * w0 + (w1 + w2)
+    above = w0 * (a1 - a0) + w2 * (a2 - a1)
+    return (d2 + (d3 + d3)) - above * (1.0 / below)
+
+
+def line_kernel_body(cells, flux, speed, wave, emit, *, n, width, axis):
+    length = n + 6
+    tiles = width // 8
+    span = length * width
+
+    def fluxes(p, _):
+        for w in range(tiles):
+            at = pl.multiple_of(p * width + w * 8, 8)
+            rho = cells[pl.ds(at, 8), :]
+            m = [cells[pl.ds((1 + k) * span + at, 8), :] for k in range(3)]
+            energy = cells[pl.ds(4 * span + at, 8), :]
+            inv = 1.0 / rho
+            u = m[axis] * inv
+            twice = (m[0] * m[0] + m[1] * m[1] + m[2] * m[2]) * inv
+            pressure = (GAMMA_GAS - 1.0) * (energy - 0.5 * twice) - GAMMA_GAS * PRESSURE_INF
+            sound = jnp.sqrt(GAMMA_GAS * (pressure + PRESSURE_INF) * inv)
+            speed[pl.ds(at, 8), :] = jnp.abs(u) + sound
+            flux[pl.ds(at, 8), :] = m[axis]
+            for k in range(3):
+                carried = m[k] * u
+                if k == axis:
+                    carried = carried + pressure
+                flux[pl.ds((1 + k) * span + at, 8), :] = carried
+            flux[pl.ds(4 * span + at, 8), :] = (energy + pressure) * u
+        return 0
+
+    lax.fori_loop(0, length, fluxes, 0, unroll=2)
+
+    def waves(i, _):
+        for w in range(tiles):
+            at = pl.multiple_of(i * width + w * 8, 8)
+            top = speed[pl.ds(at, 8), :]
+            for k in range(1, 6):
+                top = jnp.maximum(top, speed[pl.ds(at + k * width, 8), :])
+            wave[pl.ds(at, 8), :] = top
+        return 0
+
+    lax.fori_loop(0, n + 1, waves, 0)
+
+    def line(index, _):
+        c = index // tiles
+        w = index % tiles
+
+        def load(ref, p):
+            return ref[pl.ds(pl.multiple_of(c * span + p * width + w * 8, 8), 8), :]
+
+        q = [load(cells, p) for p in range(5)]
+        f = [load(flux, p) for p in range(5)]
+        dq = [q[k + 1] - q[k] for k in range(4)]
+        df = [f[k + 1] - f[k] for k in range(4)]
+        q_last, f_last, f_mid, f_near = q[4], f[4], f[2], f[3]
+        before = None
+        for i in range(n + 1):
+            q_new, f_new = load(cells, i + 5), load(flux, i + 5)
+            dq.append(q_new - q_last)
+            df.append(f_new - f_last)
+            alpha = wave[pl.ds(pl.multiple_of(i * width + w * 8, 8), 8), :]
+            drift = [alpha * v for v in dq]
+            up = weno_shift(*[df[k] + drift[k] for k in range(4)])
+            down = weno_shift(*[drift[k] - df[k] for k in (4, 3, 2, 1)])
+            here = 6.0 * ((f_mid + f_near) - drift[2]) + (up + down)
+            if before is not None:
+                emit(c, w, i - 1, here - before)
+            before = here
+            dq, df = dq[1:], df[1:]
+            f_mid, f_near = f_near, f_last
+            q_last, f_last = q_new, f_new
+        return 0
+
+    lax.fori_loop(0, 5 * tiles, line, 0)
+
+
+def z_kernel(turned, left, right, out, cells, flux, speed, wave, part, *, cx, cy, cz, scale):
+    plane = cx * cy
+    groups = plane // 128
+    width = 2 * groups
+    n = cz // 2
+    length = n + 6
+    for c in range(5):
+        base = c * length * width
+        for p in range(3):
+            cells[pl.ds(base + p * width, groups, stride=2), :] = left[(c * 3 + p) * groups : (c * 3 + p + 1) * groups, :]
+            cells[pl.ds(base + p * width + 1, groups, stride=2), :] = turned[pl.ds(c * plane + n - 3 + p, groups, stride=128), :]
+            q = n + 3 + p
+            cells[pl.ds(base + q * width, groups, stride=2), :] = turned[pl.ds(c * plane + n + p, groups, stride=128), :]
+            cells[pl.ds(base + q * width + 1, groups, stride=2), :] = right[(c * 3 + p) * groups : (c * 3 + p + 1) * groups, :]
+        for p in range(n):
+            cells[base + (p + 3) * width : base + (p + 4) * width, :] = turned[pl.ds(c * plane + p, width, stride=n), :]
+
+    def emit(c, w, i, value):
+        part[pl.ds(c * plane + i, width, stride=n), :] = value * scale
+
+    line_kernel_body(cells, flux, speed, wave, emit, n=n, width=width, axis=2)
+    for c in range(5):
+        for g in range(groups):
+            row = c * plane + g * 128
+            out[row : row + 128, :] = jnp.transpose(part[row : row + cz, :])
+
+
+def y_kernel(state, left, right, start, out, cells, flux, speed, wave, *, cx, cy, scale):
+    plane = cx * cy
+    length = cy + 6
+    for c in range(5):
+        base = c * length * cx
+        cells[base : base + 3 * cx, :] = left[c * 3 * cx : (c + 1) * 3 * cx, :]
+        cells[base + (cy + 3) * cx : base + length * cx, :] = right[c * 3 * cx : (c + 1) * 3 * cx, :]
+        for p in range(cy):
+            for x in range(0, cx, 8):
+                cells[base + (p + 3) * cx + x : base + (p + 3) * cx + x + 8, :] = state[pl.ds(c * plane + x * cy + p, 8, stride=cy), :]
+
+    def emit(c, w, i, value):
+        rows = pl.ds(c * plane + w * 8 * cy + i, 8, stride=cy)
+        out[rows, :] = start[rows, :] + value * scale
+
+    line_kernel_body(cells, flux, speed, wave, emit, n=cy, width=cx, axis=1)
+
+
+def x_kernel(state, left, right, start, old, out, cells, flux, speed, wave, *, cx, cy, scale):
+    plane = cx * cy
+    length = cx + 6
+    for c in range(5):
+        base = c * length * cy
+        cells[base : base + 3 * cy, :] = left[c * 3 * cy : (c + 1) * 3 * cy, :]
+        cells[base + 3 * cy : base + (cx + 3) * cy, :] = state[c * plane : (c + 1) * plane, :]
+        cells[base + (cx + 3) * cy : base + length * cy, :] = right[c * 3 * cy : (c + 1) * 3 * cy, :]
+
+    def emit(c, w, i, value):
+        rows = pl.ds(pl.multiple_of(c * plane + i * cy + w * 8, 8), 8)
+        change = start[rows, :] + value * scale
+        out[rows, :] = (0.75 * old[rows, :] + 0.25 * state[rows, :]) - change
+
+    line_kernel_body(cells, flux, speed, wave, emit, n=cx, width=cy, axis=0)
+
+
+def line_call(kernel, operands, n, width, name, more=()):
+    length = n + 6
+    vm = pl.BlockSpec(memory_space=pltpu.VMEM)
+    return pl.pallas_call(
+        kernel,
+        out_shape=jax.ShapeDtypeStruct(operands[0].shape, jnp.float32),
+        in_specs=[vm] * len(operands),
+        out_specs=vm,
+        scratch_shapes=[
+            pltpu.VMEM((5 * length * width, 128), jnp.float32),
+            pltpu.VMEM((5 * length * width, 128), jnp.float32),
+            pltpu.VMEM((length * width, 128), jnp.float32),
+            pltpu.VMEM((length * width, 128), jnp.float32),
+        ]
+        + list(more),
+        name=name,
+    )(*operands)
+
+
+def neighbours(first, last, axis):
+    size = lax.axis_size(axis)
+    up = [(i, (i + 1) % size) for i in range(size)]
+    down = [(j, i) for i, j in up]
+    return lax.ppermute(last, axis, up), lax.ppermute(first, axis, down)
+
+
+def flow(state_old, state_section, counts, step_size):
+    shape = state_section.shape
+    cx, cy, cz = shape[1:]
+    state = state_section.reshape(-1, cz)
+    turned, zlo, zhi, ylo, yhi, xlo, xhi = pack(state, cx, cy, cz)
+    zl, zr = neighbours(zlo, zhi, "gz")
+    yl, yr = neighbours(ylo, yhi, "gy")
+    xl, xr = neighbours(xlo, xhi, "gx")
+    scales = [0.25 * step_size * n / 12.0 for n in counts]
+    plane = cx * cy
+    part = line_call(
+        functools.partial(z_kernel, cx=cx, cy=cy, cz=cz, scale=scales[2]),
+        (turned, zl, zr), cz // 2, plane // 64, "along_z",
+        (pltpu.VMEM((5 * plane, 128), jnp.float32),),
+    )
+    part = line_call(functools.partial(y_kernel, cx=cx, cy=cy, scale=scales[1]), (state, yl, yr, part), cy, cx, "along_y")
+    updated = line_call(
+        functools.partial(x_kernel, cx=cx, cy=cy, scale=scales[0]),
+        (state, xl, xr, part, state_old.reshape(-1, cz)), cx, cy, "along_x",
+    )
+    return updated.reshape(shape)
 
 
 def directions(angles):
@@ -173,11 +299,6 @@
     c = c * x2 + 1.0
     s2 = s + s
     return 1.0 - s2 * s, s2 * c
-
-
-def recip(d):
-    r = pl.reciprocal(d, approx=True)
-    return r * (2.0 - d * r)
 
 
 def panels_kernel(live, dens, rec, geo, cell, lis, table, out, dens3, lisb, sp, wts, prod, fine, coarse, acc):
@@ -248,7 +369,7 @@
             oz = lisb[2, r : r + 16, :] - pz
             d2 = ox * ox + oy * oy + oz * oz
             face = nx * ox + ny * oy + nz * oz
-            wts[r : r + 16, :] = (face * recip(d2)).astype(jnp.bfloat16)
+            wts[r : r + 16, :] = (face * (1.0 / d2)).astype(jnp.bfloat16)
         for q in range(tiles // 2):
             prod[q % 2] = lax.dot_general(sp[b], wts[q * 256 : (q + 1) * 256, :], NT, preferred_element_type=jnp.float32)
             for u in range(2):
@@ -349,8 +470,7 @@
         cells_z * lax.axis_size("gz"),
     )
     step_size = COURANT / max(counts)
-    padded = with_halo(state_section, (("gx", 1), ("gy", 2), ("gz", 3)), 3)
-    updated = section_update(padded, state_old, counts, step_size)
+    updated = flow(state_old, state_section, counts, step_size)
     slot_count = panel_cell.shape[0]
     block_rows = panel_cell.shape[1]
     samples = panel_record.shape[1]

time: 177 us -> 137 us (0.77)
  other arithmetic: 54.5 us -> 2.16 us
  Pallas kernels: 23.3 us -> 48.5 us
  local copies, waits for them, and re-layouts: 21.6 us -> 5.9 us
  starting transfers between devices: 36 us -> 41.9 us
  waiting for transfers between devices: 39.6 us -> 36.3 us
    add x7 -> x0, other arithmetic: 36.6 us -> none  [the longest x3 34.9 us: face_difference(): weno_face(split_up[0], split_up[1], split_up[2], split_up[3], split_up[4])]
    pallas_call x0 -> x4, Pallas kernels: none -> 31.7 us  [the longest x3 28.7 us: line_call(): pl.pallas_call(kernel, out_shape=jax.ShapeDtypeStruct(operands[0].shape,...]
    slice x5 -> x0, local copies, waits for them, and re-layouts: 11.3 us -> none  [the longest x3 6.17 us: with_halo(): last = lax.slice_in_dim(shard, length - width, length, axis=dim)]
    concatenate x3 -> x0, other arithmetic: 8.08 us -> none  [with_halo(): shard = jnp.concatenate([before, shard, after], axis=dim)]
    ppermute x5, starting transfers between devices: 27.3 us -> 34.8 us  [swap(): return lax.ppermute(value, axis, [(i, i ^ bit) for i in range(size)])]
    ppermute x4 -> x0, local copies, waits for them, and re-layouts: 6.6 us -> none  [the longest x2 3.33 us: with_halo(): after = lax.ppermute(initial, axis, down)]
    pallas_call x1, Pallas kernels: 23.3 us -> 16.7 us  [panels(): pl.pallas_call(panels_kernel, out_shape=jax.ShapeDtypeStruct((shares, 2,...]
    ppermute x5, waiting for transfers between devices: 34.8 us -> 32.8 us  [swap(): return lax.ppermute(value, axis, [(i, i ^ bit) for i in range(size)])]
  transfers between devices with their start and end apart: 11 -> 11, of which waited for: 7 -> 7; matrix products, arithmetic and copies ran while one was open for 18% -> 1% of each run, Pallas kernels for 0% -> 14%
where the time goes in v2:
time: 137 us; the launch traced here: 136 us
  Pallas kernels  48.5 us (35%)
  starting transfers between devices  41.9 us (31%)
  waiting for transfers between devices  36.3 us (26%)
  local copies, waits for them, and re-layouts  5.9 us (4%)
  other arithmetic  2.16 us (2%)
  between operations  1.57 us (1%)
    ppermute x5, starting transfers between devices, swap(): return lax.ppermute(value, axis, [(i, i ^ bit) for i in range(size)])  34.8 us
    ppermute x5, waiting for transfers between devices, swap(): return lax.ppermute(value, axis, [(i, i ^ bit) for i in range(size)])  32.8 us
    pallas_call x3, Pallas kernels, line_call(): pl.pallas_call(kernel, out_shape=jax.ShapeDtypeStruct(operands[0].shape,...  28.7 us
    pallas_call x1, Pallas kernels, panels(): pl.pallas_call(panels_kernel, out_shape=jax.ShapeDtypeStruct((shares, 2,...  16.7 us
    ppermute x6, starting transfers between devices, neighbours(): return (lax.ppermute(last, axis, up), lax.ppermute(first, axis, down))  7.11 us
    unnamed x24, local copies, waits for them, and re-layouts  4.87 us
    ppermute x6, waiting for transfers between devices, neighbours(): return (lax.ppermute(last, axis, up), lax.ppermute(first, axis, down))  3.43 us
    pallas_call x1, Pallas kernels, pack(): pl.pallas_call(functools.partial(pack_kernel, cx=cx, cy=cy, cz=cz), out_s...  3.08 us
  transfers between devices with their start and end apart: 11, of which 7 were waited for; matrix products, arithmetic and copies ran while one was open for 1% of the time, Pallas kernels for 14%

profile of v2, /device:TPU:0, one launch (start us, length us, event | category | flops | bytes accessed | tf_op | source)
XLA Modules:
  0.0 136.3 jit_solution(8997575384061023672)
XLA Ops:
  0.7 3.1 %pack.1 = (f32[2560,128]{1,0:T(8,128)}, f32[60,128]{1,0:T(8,128)}, f32[60,128]{1,0:T(8,128)}, f32[240,128]{1,0:T(8,128)}, f32[240,128]{1,0:T(8,128)}, /*index=5*/f32[480,128]{1,0:T(8,128)}, f32[480,128]{1,0:T(8,128)}) custom-call(f32[2560,128]{1,0:T(8,128)} %bitcast.29), custom_call_target="tpu_custom_call" | custom-call | tf_op jit(solution)/shard_map/pack/pallas_call | solution.py:43
  3.7 3.0 %collective-permute-start = (f32[480,128]{1,0:T(8,128)}, f32[480,128]{1,0:T(8,128)S(1)}, u32[]{:S(2)}, u32[]{:S(2)}) collective-permute-start(f32[480,128]{1,0:T(8,128)} %get-tuple-element.9), channel_id=1, source_target_pairs={{0,16},{16,0},{1,17},{17,1},{2,18},{18,2},{3,19},{19,3},{4,20},{20... | collective-permute-start | bytes 737288 | tf_op jit(solution)/shard_map/ppermute | solution.py:225
  6.7 2.1 %collective-permute-start.2 = (f32[240,128]{1,0:T(8,128)}, f32[240,128]{1,0:T(8,128)S(1)}, u32[]{:S(2)}, u32[]{:S(2)}) collective-permute-start(f32[240,128]{1,0:T(8,128)} %get-tuple-element.11), channel_id=1, source_target_pairs={{0,4},{4,8},{8,12},{12,0},{1,5},{5,9},{9,13},{13,1},{2,6},{6,10},{... | collective-permute-start | bytes 368648 | tf_op jit(solution)/shard_map/ppermute | solution.py:225
  8.8 2.0 %collective-permute-start.3 = (f32[240,128]{1,0:T(8,128)}, f32[240,128]{1,0:T(8,128)S(1)}, u32[]{:S(2)}, u32[]{:S(2)}) collective-permute-start(f32[240,128]{1,0:T(8,128)} %get-tuple-element.12), channel_id=1, source_target_pairs={{4,0},{8,4},{12,8},{0,12},{5,1},{9,5},{13,9},{1,13},{6,2},{10,6},{... | collective-permute-start | bytes 368648 | tf_op jit(solution)/shard_map/ppermute | solution.py:225
  10.9 1.0 cosine_multiply_fusion
  12.2 2.2 %collective-permute-done.4.left = f32[60,128]{1,0:T(8,128)S(1)} collective-permute-done((f32[60,128]{1,0:T(8,128)}, f32[60,128]{1,0:T(8,128)S(1)}, u32[]{:S(2)}, u32[]{:S(2)}) %collective-permute-start.4) | collective-permute-done | bytes 30752 | tf_op jit(solution)/shard_map/ppermute | solution.py:225
  15.1 1.2 collective-permute-done.5.right
  16.9 9.6 %along_z.1.start = f32[2560,128]{1,0:T(8,128)} custom-call(f32[2560,128]{1,0:T(8,128)} %get-tuple-element.13.turned, f32[60,128]{1,0:T(8,128)} %copy-done.7, f32[60,128]{1,0:T(8,128)} %copy-done.8), custom_call_target="tpu_custom_call" | custom-call | tf_op jit(solution)/shard_map/along_z/pallas_call | solution.py:205
  26.6 0.6 copy-done.5
  27.2 0.6 copy-done.6
  27.9 9.6 %along_y.1.start = f32[2560,128]{1,0:T(8,128)} custom-call(f32[2560,128]{1,0:T(8,128)} %bitcast.30, f32[240,128]{1,0:T(8,128)} %copy-done.5, f32[240,128]{1,0:T(8,128)} %copy-done.6, f32[2560,128]{1,0:T(8,128)} %along_z.1.start), custom_call_target="tpu_custom_call" | custom-call | tf_op jit(solution)/shard_map/along_y/pallas_call | solution.py:205
  37.5 0.7 copy-done.3
  38.3 9.4 %along_x.1 = f32[2560,128]{1,0:T(8,128)} custom-call(f32[2560,128]{1,0:T(8,128)} %bitcast.31, f32[480,128]{1,0:T(8,128)} %copy-done.3, f32[480,128]{1,0:T(8,128)} %copy-done.4, f32[2560,128]{1,0:T(8,128)} %along_y.1.start, f32[2560,128]{1,0:T(8,128)} %bitcast.33), custom_call_target="tpu_custom_call" | custom-call | tf_op jit(solution)/shard_map/along_x/pallas_call | solution.py:205
  47.7 1.0 slice.23.dens
  48.7 2.2 %copy-done = bf16[4096,512]{1,0:T(8,128)(2,1)S(1)} copy-done((bf16[4096,512]{1,0:T(8,128)(2,1)S(1)}, bf16[4096,512]{1,0:T(8,128)(2,1)}, u32[]{:S(2)}) %copy-start) | copy-done | bytes 4194328
  50.9 16.7 %panels.1 = f32[4,2,256,128]{3,2,1,0:T(8,128)S(1)} custom-call(s32[1]{0:T(128)S(6)} %copy.11.live, f32[512,128]{1,0:T(8,128)S(1)} %slice.23.dens, bf16[4096,512]{1,0:T(8,128)(2,1)S(1)} %copy-done, f32[6,32,128]{2,1,0:T(8,128)S(1)} %maximum_bitcast_fusion.geo, s32[32,128]{1,0:T(8,128)S(1)} %copy-done.2, f32[3,8,128]{2,1,0:T(8,128)S(1)} %fusion.19.lis, ...), custom_call_target="tpu_custom_call" | custom-call | tf_op jit(solution)/shard_map/panels/pallas_call | solution.py:409
  67.8 1.9 %collective-permute-done.6 = f32[2,2,256,128]{3,2,1,0:T(8,128)S(1)} collective-permute-done((f32[2,2,256,128]{3,2,1,0:T(8,128)S(1)}, f32[2,2,256,128]{3,2,1,0:T(8,128)S(1)}, u32[]{:S(2)}, u32[]{:S(2)}) %collective-permute-start.6) | collective-permute-done | bytes 524320 | tf_op jit(solution)/shard_map/ppermute | solution.py:431
  69.8 8.3 %collective-permute-done.7 = f32[1,2,256,128]{3,2,1,0:T(8,128)S(1)} collective-permute-done((f32[1,2,256,128]{3,2,1,0:T(8,128)S(1)}, f32[1,2,256,128]{3,2,1,0:T(8,128)S(1)}, u32[]{:S(2)}, u32[]{:S(2)}) %collective-permute-start.7) | collective-permute-done | bytes 262176 | tf_op jit(solution)/shard_map/ppermute | solution.py:431
  78.3 7.5 %collective-permute-done.8 = f32[2,256,128]{2,1,0:T(8,128)S(1)} collective-permute-done((f32[2,256,128]{2,1,0:T(8,128)S(1)}, f32[2,256,128]{2,1,0:T(8,128)S(1)}, u32[]{:S(2)}, u32[]{:S(2)}) %collective-permute-start.8) | collective-permute-done | bytes 262176 | tf_op jit(solution)/shard_map/ppermute | solution.py:431
  85.8 24.1 %collective-permute-start.9 = (f32[2,256,128]{2,1,0:T(8,128)S(1)}, f32[2,256,128]{2,1,0:T(8,128)S(1)}, u32[]{:S(2)}, u32[]{:S(2)}) collective-permute-start(f32[2,256,128]{2,1,0:T(8,128)S(1)} %add.107), channel_id=1, source_target_pairs={{0,4},{4,0},{8,12},{12,8},{1,5},{5,1},{9,13},{13,9},{2,6},{6,2},{1... | collective-permute-start | bytes 786440 | tf_op jit(solution)/shard_map/ppermute | solution.py:431
  109.9 5.4 %collective-permute-done.9 = f32[2,256,128]{2,1,0:T(8,128)S(1)} collective-permute-done((f32[2,256,128]{2,1,0:T(8,128)S(1)}, f32[2,256,128]{2,1,0:T(8,128)S(1)}, u32[]{:S(2)}, u32[]{:S(2)}) %collective-permute-start.9) | collective-permute-done | bytes 262176 | tf_op jit(solution)/shard_map/ppermute | solution.py:431
  115.3 10.4 %collective-permute-start.10 = (f32[2,256,128]{2,1,0:T(8,128)S(1)}, f32[2,256,128]{2,1,0:T(8,128)S(1)}, u32[]{:S(2)}, u32[]{:S(2)}) collective-permute-start(f32[2,256,128]{2,1,0:T(8,128)S(1)} %add.108), channel_id=1, source_target_pairs={{0,8},{4,12},{8,0},{12,4},{1,9},{5,13},{9,1},{13,5},{2,10},{6,14},... | collective-permute-start | bytes 786440 | tf_op jit(solution)/shard_map/ppermute | solution.py:431
  125.8 9.8 %collective-permute-done.10 = f32[2,256,128]{2,1,0:T(8,128)S(1)} collective-permute-done((f32[2,256,128]{2,1,0:T(8,128)S(1)}, f32[2,256,128]{2,1,0:T(8,128)S(1)}, u32[]{:S(2)}, u32[]{:S(2)}) %collective-permute-start.10) | collective-permute-done | bytes 262176 | tf_op jit(solution)/shard_map/ppermute | solution.py:431
  135.5 0.7 add.109
  (41 shorter events, 1.5 us)
Async XLA Ops:
  0.6 10.2 %copy-start.9 = (f32[2,4096]{1,0:T(2,128)S(1)}, f32[2,4096]{1,0:T(2,128)}, u32[]{:S(2)}) copy-start(f32[2,4096]{1,0:T(2,128)} %param.13) | copy-start | bytes 98308
  0.6 11.2 %copy-start.10 = (f32[2,1024]{1,0:T(2,128)S(1)}, f32[2,1024]{1,0:T(2,128)}, u32[]{:S(2)}) copy-start(f32[2,1024]{1,0:T(2,128)} %param.15) | copy-start | bytes 24580
  0.7 11.5 %copy-start.2 = (s32[32,128]{1,0:T(8,128)S(1)}, s32[32,128]{1,0:T(8,128)}, u32[]{:S(2)}) copy-start(s32[32,128]{1,0:T(8,128)} %cell.1) | copy-start | bytes 49156
  0.7 11.5 %copy-start.11 = (f32[1024]{0:T(1024)S(1)}, f32[1024]{0:T(1024)}, u32[]{:S(2)}) copy-start(f32[1024]{0:T(1024)} %param.16) | copy-start | bytes 12292
  3.7 33.7 %collective-permute-start = (f32[480,128]{1,0:T(8,128)}, f32[480,128]{1,0:T(8,128)S(1)}, u32[]{:S(2)}, u32[]{:S(2)}) collective-permute-start(f32[480,128]{1,0:T(8,128)} %get-tuple-element.9), channel_id=1, source_target_pairs={{0,16},{16,0},{1,17},{17,1},{2,18},{18,2},{3,19},{19,3},{4,20},{20... | collective-permute-start | bytes 737288 | tf_op jit(solution)/shard_map/ppermute | solution.py:225
  6.7 30.8 %collective-permute-start.1 = (f32[480,128]{1,0:T(8,128)}, f32[480,128]{1,0:T(8,128)S(1)}, u32[]{:S(2)}, u32[]{:S(2)}) collective-permute-start(f32[480,128]{1,0:T(8,128)} %get-tuple-element.10), channel_id=1, source_target_pairs={{16,0},{0,16},{17,1},{1,17},{18,2},{2,18},{19,3},{3,19},{20,4},{4,... | collective-permute-start | bytes 737288 | tf_op jit(solution)/shard_map/ppermute | solution.py:225
  6.7 19.8 %collective-permute-start.2 = (f32[240,128]{1,0:T(8,128)}, f32[240,128]{1,0:T(8,128)S(1)}, u32[]{:S(2)}, u32[]{:S(2)}) collective-permute-start(f32[240,128]{1,0:T(8,128)} %get-tuple-element.11), channel_id=1, source_target_pairs={{0,4},{4,8},{8,12},{12,0},{1,5},{5,9},{9,13},{13,1},{2,6},{6,10},{... | collective-permute-start | bytes 368648 | tf_op jit(solution)/shard_map/ppermute | solution.py:225
  8.8 17.8 %collective-permute-start.3 = (f32[240,128]{1,0:T(8,128)}, f32[240,128]{1,0:T(8,128)S(1)}, u32[]{:S(2)}, u32[]{:S(2)}) collective-permute-start(f32[240,128]{1,0:T(8,128)} %get-tuple-element.12), channel_id=1, source_target_pairs={{4,0},{8,4},{12,8},{0,12},{5,1},{9,5},{13,9},{1,13},{6,2},{10,6},{... | collective-permute-start | bytes 368648 | tf_op jit(solution)/shard_map/ppermute | solution.py:225
  10.9 3.6 %collective-permute-start.4 = (f32[60,128]{1,0:T(8,128)}, f32[60,128]{1,0:T(8,128)S(1)}, u32[]{:S(2)}, u32[]{:S(2)}) collective-permute-start(f32[60,128]{1,0:T(8,128)} %get-tuple-element.14), channel_id=1, source_target_pairs={{0,1},{1,2},{2,3},{3,0},{4,5},{5,6},{6,7},{7,4},{8,9},{9,10},{10,1... | collective-permute-start | bytes 92168 | tf_op jit(solution)/shard_map/ppermute | solution.py:225
  14.4 1.9 %copy-start.7 = (f32[60,128]{1,0:T(8,128)}, f32[60,128]{1,0:T(8,128)S(1)}, u32[]{:S(2)}) copy-start(f32[60,128]{1,0:T(8,128)S(1)} %collective-permute-done.4.left) | copy-start | bytes 92164
  14.4 1.9 %collective-permute-start.5 = (f32[60,128]{1,0:T(8,128)}, f32[60,128]{1,0:T(8,128)S(1)}, u32[]{:S(2)}, u32[]{:S(2)}) collective-permute-start(f32[60,128]{1,0:T(8,128)} %get-tuple-element.15), channel_id=1, source_target_pairs={{1,0},{2,1},{3,2},{0,3},{5,4},{6,5},{7,6},{4,7},{9,8},{10,9},{11,1... | collective-permute-start | bytes 92168 | tf_op jit(solution)/shard_map/ppermute | solution.py:225
  16.3 0.6 copy-start.8
  26.6 0.6 copy-start.5
  27.2 0.6 copy-start.6
  37.5 0.7 copy-start.3
  37.5 0.8 copy-start.4
  38.3 10.4 %copy-start.1 = (bf16[256,512]{1,0:T(8,128)(2,1)S(1)}, bf16[256,512]{1,0:T(8,128)(2,1)}, u32[]{:S(2)}) copy-start(bf16[256,512]{1,0:T(8,128)(2,1)} %constant.131.clone.table) | copy-start | bytes 786436
  48.7 2.2 %copy-start = (bf16[4096,512]{1,0:T(8,128)(2,1)S(1)}, bf16[4096,512]{1,0:T(8,128)(2,1)}, u32[]{:S(2)}) copy-start(bf16[4096,512]{1,0:T(8,128)(2,1)} %rec.1) | copy-start | bytes 12582916
  67.7 2.0 %collective-permute-start.6 = (f32[2,2,256,128]{3,2,1,0:T(8,128)S(1)}, f32[2,2,256,128]{3,2,1,0:T(8,128)S(1)}, u32[]{:S(2)}, u32[]{:S(2)}) collective-permute-start(f32[2,2,256,128]{3,2,1,0:T(8,128)S(1)} %dynamic-slice_bitcast_fusion), channel_id=1, source_target_pairs={{0,1},{1,0},{2,3},{3,2},{4,5},{5,4},{6,7},{7,6},{8,9},{9,8},{10,11... | collective-permute-start | bytes 1572872 | tf_op jit(solution)/shard_map/ppermute | solution.py:431
  69.7 8.4 %collective-permute-start.7 = (f32[1,2,256,128]{3,2,1,0:T(8,128)S(1)}, f32[1,2,256,128]{3,2,1,0:T(8,128)S(1)}, u32[]{:S(2)}, u32[]{:S(2)}) collective-permute-start(f32[1,2,256,128]{3,2,1,0:T(8,128)S(1)} %constant_dynamic-slice_fusion), channel_id=1, source_target_pairs={{0,2},{1,3},{2,0},{3,1},{4,6},{5,7},{6,4},{7,5},{8,10},{9,11},{10,... | collective-permute-start | bytes 786440 | tf_op jit(solution)/shard_map/ppermute | solution.py:431
  78.2 7.6 %collective-permute-start.8 = (f32[2,256,128]{2,1,0:T(8,128)S(1)}, f32[2,256,128]{2,1,0:T(8,128)S(1)}, u32[]{:S(2)}, u32[]{:S(2)}) collective-permute-start(f32[2,256,128]{2,1,0:T(8,128)S(1)} %add_bitcast_fusion), channel_id=1, source_target_pairs={{0,16},{16,0},{1,17},{17,1},{2,18},{18,2},{3,19},{19,3},{4,20},{20... | collective-permute-start | bytes 786440 | tf_op jit(solution)/shard_map/ppermute | solution.py:431
  85.8 29.5 %collective-permute-start.9 = (f32[2,256,128]{2,1,0:T(8,128)S(1)}, f32[2,256,128]{2,1,0:T(8,128)S(1)}, u32[]{:S(2)}, u32[]{:S(2)}) collective-permute-start(f32[2,256,128]{2,1,0:T(8,128)S(1)} %add.107), channel_id=1, source_target_pairs={{0,4},{4,0},{8,12},{12,8},{1,5},{5,1},{9,13},{13,9},{2,6},{6,2},{1... | collective-permute-start | bytes 786440 | tf_op jit(solution)/shard_map/ppermute | solution.py:431
  115.3 20.2 %collective-permute-start.10 = (f32[2,256,128]{2,1,0:T(8,128)S(1)}, f32[2,256,128]{2,1,0:T(8,128)S(1)}, u32[]{:S(2)}, u32[]{:S(2)}) collective-permute-start(f32[2,256,128]{2,1,0:T(8,128)S(1)} %add.108), channel_id=1, source_target_pairs={{0,8},{4,12},{8,0},{12,4},{1,9},{5,13},{9,1},{13,5},{2,10},{6,14},... | collective-permute-start | bytes 786440 | tf_op jit(solution)/shard_map/ppermute | solution.py:431

commit v3 on v2

--- a/solution.py
+++ b/solution.py
@@ -10,6 +10,8 @@
 from jax.sharding import PartitionSpec as P
 
 FREQS = 128
+BATCH = 4
+CHUNKS = 4
 NT = (((1,), (1,)), ((), ()))
 
 
@@ -46,6 +48,7 @@
         in_specs=[vm],
         out_specs=[vm] * 7,
         name="pack",
+        compiler_params=pltpu.CompilerParams(vmem_limit_bytes=10 * 1024 * 1024),
     )(state)
 
 
@@ -215,6 +218,7 @@
         ]
         + list(more),
         name=name,
+        compiler_params=pltpu.CompilerParams(vmem_limit_bytes=14 * 1024 * 1024),
     )(*operands)
 
 
@@ -301,129 +305,201 @@
     return 1.0 - s2 * s, s2 * c
 
 
-def panels_kernel(live, dens, rec, geo, cell, lis, table, out, dens3, lisb, sp, wts, prod, fine, coarse, acc):
-    slots, bp = cell.shape
-    rows = dens.shape[0]
+def weights_kernel(live, geo, lis, *refs):
+    outs, lisb = refs[:-1], refs[-1]
     tiles = lis.shape[1]
-    half = table.shape[0] // 2
-    count = live[0]
-
-    d = dens[...]
-    hi = d.astype(jnp.bfloat16)
-    left = d - hi.astype(jnp.float32)
-    mid = left.astype(jnp.bfloat16)
-    lo = (left - mid.astype(jnp.float32)).astype(jnp.bfloat16)
-    dens3[:, 0:128] = hi
-    dens3[:, 128:256] = mid
-    dens3[:, 256:384] = lo
+    span = tiles * 128 // len(outs)
     for k in range(3):
         for t in range(tiles):
             row = lis[k, t : t + 1, :]
             lisb[k, t * 128 : (t + 1) * 128, :] = jnp.transpose(jnp.broadcast_to(row, (128, 128)))
-    acc[...] = jnp.zeros(acc.shape, jnp.float32)
-    lane = lax.broadcasted_iota(jnp.int32, (128, 128), 1).astype(jnp.float32)
-
-    def spectrum(b, _):
-        cells = cell[pl.ds(b, 1), :]
-        high = (cells >> 7).astype(jnp.float32)
-        low = (cells & 127).astype(jnp.float32)
-        high_col = jnp.transpose(jnp.broadcast_to(high, (128, 128)))
-        low_col = jnp.transpose(jnp.broadcast_to(low, (128, 128)))
-        g = jnp.zeros((128, 384), jnp.float32)
-        for j in range(rows // 128):
-            onehot = jnp.where(high_col == lane + float(128 * j), 1.0, 0.0).astype(jnp.bfloat16)
-            g = g + jnp.dot(onehot, dens3[j * 128 : (j + 1) * 128, :], preferred_element_type=jnp.float32)
-        gs = (g[:, 0:128] + g[:, 128:256]) + g[:, 256:384]
-        sampled = jnp.sum(jnp.where(low_col == lane, gs, 0.0), axis=1, keepdims=True)
-        src = (rec[pl.ds(pl.multiple_of(b * bp, bp), bp), :].astype(jnp.float32) * sampled).astype(jnp.bfloat16)
-        sp[b] = lax.dot_general(table[...], src, NT, preferred_element_type=jnp.float32).astype(jnp.bfloat16)
-        return 0
-
-    lax.fori_loop(0, count, spectrum, 0)
-
-    sub8 = lax.broadcasted_iota(jnp.int32, (8, 128), 0).astype(jnp.float32) + 1.0
-    turn = WAVE_STEP / (2.0 * math.pi)
 
     def block(b, _):
         px, py, pz, nx, ny, nz = [geo[k, pl.ds(b, 1), :] for k in range(6)]
-        cx, cy, cz = [jnp.sum(v, axis=1, keepdims=True) * (1.0 / bp) for v in (px, py, pz)]
-        sx, sy, sz = lis[0] - cx, lis[1] - cy, lis[2] - cz
-        theta = jnp.sqrt(sx * sx + sy * sy + sz * sz) * turn
-        c1, s1 = sincos_turns(8.0 * theta)
-        cs = [None, (c1, s1)]
-        for a in range(2, half // 8):
-            (ca, sa), (cb, sb) = cs[a // 2], cs[a - a // 2]
-            cs.append((ca * cb - sa * sb, sa * cb + ca * sb))
-        for a in range(1, half // 8):
-            coarse[0, a] = cs[a][0]
-            coarse[1, a] = cs[a][1]
-        coarse[0, 0] = theta
-        for t in range(tiles):
-            th = jnp.broadcast_to(coarse[0, 0, t : t + 1, :], (8, 128)) * sub8
-            c, s = sincos_turns(th)
-            fine[0, t] = c
-            fine[1, t] = s
-        for r in range(0, tiles * 128, 16):
-            ox = lisb[0, r : r + 16, :] - px
-            oy = lisb[1, r : r + 16, :] - py
-            oz = lisb[2, r : r + 16, :] - pz
-            d2 = ox * ox + oy * oy + oz * oz
-            face = nx * ox + ny * oy + nz * oz
-            wts[r : r + 16, :] = (face * (1.0 / d2)).astype(jnp.bfloat16)
-        for q in range(tiles // 2):
-            prod[q % 2] = lax.dot_general(sp[b], wts[q * 256 : (q + 1) * 256, :], NT, preferred_element_type=jnp.float32)
-            for u in range(2):
-                t = 2 * q + u
-                bc, bs = fine[0, t], fine[1, t]
-                for a in range(half // 8):
-                    if a == 0:
-                        c, s = bc, bs
-                    else:
-                        ec = jnp.broadcast_to(coarse[0, a, t : t + 1, :], (8, 128))
-                        es = jnp.broadcast_to(coarse[1, a, t : t + 1, :], (8, 128))
-                        c = ec * bc - es * bs
-                        s = es * bc + ec * bs
-                    re = prod[q % 2, a * 8 : a * 8 + 8, u * 128 : u * 128 + 128]
-                    im = prod[q % 2, half + a * 8 : half + a * 8 + 8, u * 128 : u * 128 + 128]
-                    acc[0, a * 8 : a * 8 + 8, t * 128 : t * 128 + 128] += re * c + im * s
-                    acc[1, a * 8 : a * 8 + 8, t * 128 : t * 128 + 128] += im * c - re * s
+        for q, out in enumerate(outs):
+            for r in range(0, span, 16):
+                at = q * span + r
+                ox = lisb[0, at : at + 16, :] - px
+                oy = lisb[1, at : at + 16, :] - py
+                oz = lisb[2, at : at + 16, :] - pz
+                d2 = ox * ox + oy * oy + oz * oz
+                facing = nx * ox + ny * oy + nz * oz
+                out[pl.ds(pl.multiple_of(b * span + r, 16), 16), :] = (facing * (1.0 / d2)).astype(jnp.bfloat16)
         return 0
 
-    lax.fori_loop(0, count, block, 0)
-    shares = out.shape[0]
-    per = tiles // shares
-    for g in range(shares):
-        for k in range(2):
-            for t in range(per):
-                col = (g * per + t) * 128
-                out[g, k, t * 128 : (t + 1) * 128, :] = jnp.transpose(acc[k, :, col : col + 128])
-
-
-def panels(live, dens, rec, geo, cell, lis, table, shares):
-    slots, bp = cell.shape
-    rows = dens.shape[0]
-    tiles = lis.shape[1]
-    k2 = table.shape[0]
-    obs = tiles * 128
+    lax.fori_loop(0, (live[0] + BATCH - 1) // BATCH * BATCH, block, 0)
+
+
+def weights(live, geo, lis, chunks):
+    slots, bp = geo.shape[1:]
+    obs = lis.shape[1] * 128
     vm = pl.BlockSpec(memory_space=pltpu.VMEM)
     return pl.pallas_call(
-        panels_kernel,
-        out_shape=jax.ShapeDtypeStruct((shares, 2, obs // shares, k2 // 2), jnp.float32),
-        in_specs=[pl.BlockSpec(memory_space=pltpu.SMEM)] + [vm] * 6,
+        weights_kernel,
+        out_shape=[jax.ShapeDtypeStruct((slots * obs // chunks, bp), jnp.bfloat16)] * chunks,
+        in_specs=[pl.BlockSpec(memory_space=pltpu.SMEM), vm, vm],
+        out_specs=[vm] * chunks,
+        scratch_shapes=[pltpu.VMEM((3, obs, 128), jnp.float32)],
+        name="weights",
+        compiler_params=pltpu.CompilerParams(vmem_limit_bytes=14 * 1024 * 1024),
+    )(live, geo, lis)
+
+
+def spectra_kernel(live, dens, rec, cell, table, sp, dens3, held, onehot, src, sems):
+    slots, bp = cell.shape
+    rows = dens.shape[0] // 2
+    groups = slots // BATCH
+    total = (live[0] + BATCH - 1) // BATCH
+    span = BATCH * bp
+
+    def fetch(g):
+        at = pl.ds(pl.multiple_of(g * span, span), span)
+        return pltpu.make_async_copy(rec.at[at, :], held.at[at, :], sems.at[g])
+
+    for g in range(groups):
+        @pl.when(g < total)
+        def _():
+            fetch(g).start()
+
+    for h in range(2):
+        d = dens[pl.ds(h, rows, stride=2), :]
+        hi = d.astype(jnp.bfloat16)
+        left = d - hi.astype(jnp.float32)
+        mid = left.astype(jnp.bfloat16)
+        lo = (left - mid.astype(jnp.float32)).astype(jnp.bfloat16)
+        for k, part in enumerate((hi, mid, lo)):
+            dens3[k, :, h * 128 : (h + 1) * 128] = part
+    lane = lax.broadcasted_iota(jnp.int32, (bp, 128), 1).astype(jnp.float32)
+
+    def group(g, _):
+        lows = []
+        for j in range(BATCH):
+            cells = cell[pl.ds(g * BATCH + j, 1), :].astype(jnp.float32)
+            col = jnp.transpose(jnp.broadcast_to(cells, (128, 128)))
+            high = jnp.floor(col * (1.0 / 256.0))
+            low = col - 256.0 * high
+            lows.append(low)
+            for h in range(rows // 128):
+                hit = jnp.where(high == lane + float(128 * h), 1.0, 0.0).astype(jnp.bfloat16)
+                onehot[j * bp : (j + 1) * bp, h * 128 : (h + 1) * 128] = hit
+        hot = onehot[...]
+        picked = jnp.dot(hot, dens3[0], preferred_element_type=jnp.float32)
+        picked = picked + jnp.dot(hot, dens3[1], preferred_element_type=jnp.float32)
+        picked = picked + jnp.dot(hot, dens3[2], preferred_element_type=jnp.float32)
+        fetch(g).wait()
+        for j in range(BATCH):
+            own = picked[j * bp : (j + 1) * bp, :]
+            found = jnp.where(lows[j] == lane, own[:, 0:128], 0.0) + jnp.where(lows[j] == lane + 128.0, own[:, 128:256], 0.0)
+            sampled = jnp.sum(found, axis=1, keepdims=True)
+            record = held[pl.ds(pl.multiple_of(g * span + j * bp, bp), bp), :].astype(jnp.float32)
+            src[j * bp : (j + 1) * bp, :] = (record * sampled).astype(jnp.bfloat16)
+        for j in range(0, BATCH, 2):
+            both = lax.dot_general(table[...], src[j * bp : (j + 2) * bp, :], NT, preferred_element_type=jnp.float32)
+            both = both.astype(jnp.bfloat16)
+            sp[g * BATCH + j] = both[:, 0:bp]
+            sp[g * BATCH + j + 1] = both[:, bp : 2 * bp]
+        return 0
+
+    lax.fori_loop(0, total, group, 0)
+
+
+def spectra(live, dens, rec, cell, table, rows):
+    slots, bp = cell.shape
+    samples = rec.shape[1]
+    k2 = table.shape[0]
+    vm = pl.BlockSpec(memory_space=pltpu.VMEM)
+    return pl.pallas_call(
+        spectra_kernel,
+        grid=(1,),
+        out_shape=jax.ShapeDtypeStruct((slots, k2, bp), jnp.bfloat16),
+        in_specs=[
+            pl.BlockSpec(memory_space=pltpu.SMEM),
+            pl.BlockSpec((rows, 128), lambda i: (0, 0)),
+            pl.BlockSpec(memory_space=pl.ANY),
+            vm,
+            vm,
+        ],
         out_specs=vm,
         scratch_shapes=[
-            pltpu.VMEM((rows, 384), jnp.bfloat16),
-            pltpu.VMEM((3, obs, 128), jnp.float32),
-            pltpu.VMEM((slots, k2, bp), jnp.bfloat16),
-            pltpu.VMEM((obs, bp), jnp.bfloat16),
-            pltpu.VMEM((2, k2, 256), jnp.float32),
-            pltpu.VMEM((2, tiles, 8, 128), jnp.float32),
-            pltpu.VMEM((2, k2 // 16, tiles, 128), jnp.float32),
-            pltpu.VMEM((2, k2 // 2, obs), jnp.float32),
+            pltpu.VMEM((3, rows // 2, 256), jnp.bfloat16),
+            pltpu.VMEM(rec.shape, jnp.bfloat16),
+            pltpu.VMEM((BATCH * bp, rows // 2), jnp.bfloat16),
+            pltpu.VMEM((BATCH * bp, samples), jnp.bfloat16),
+            pltpu.SemaphoreType.DMA((slots // BATCH,)),
         ],
-        name="panels",
-        compiler_params=pltpu.CompilerParams(vmem_limit_bytes=48 * 1024 * 1024),
-    )(live, dens, rec, geo, cell, lis, table)
+        name="spectra",
+        compiler_params=pltpu.CompilerParams(vmem_limit_bytes=12 * 1024 * 1024),
+    )(live, dens, rec, cell, table)
+
+
+def observe_kernel(live, centre, sp, wts, lis, out, prod, acc):
+    slots, k2, bp = sp.shape
+    tiles = lis.shape[1]
+    half = k2 // 2
+    span = tiles * 128
+    total = (live[0] + BATCH - 1) // BATCH
+    acc[...] = jnp.zeros(acc.shape, jnp.float32)
+    orders = lax.broadcasted_iota(jnp.int32, (8, 128), 0).astype(jnp.float32) + 1.0
+    orders = orders * (WAVE_STEP / (2.0 * math.pi))
+
+    def group(g, _):
+        for pair in range(0, BATCH, 2):
+            waves = []
+            for j in range(2):
+                b = g * BATCH + pair + j
+                held = wts[pl.ds(pl.multiple_of(b * span, span), span), :]
+                prod[pair + j] = lax.dot_general(sp[b], held, NT, preferred_element_type=jnp.float32)
+            for t in range(tiles):
+                state = []
+                for j in range(2):
+                    b = g * BATCH + pair + j
+                    away = [jnp.broadcast_to(lis[k, t : t + 1, :], (8, 128)) - centre[k, b] for k in range(3)]
+                    reach = jnp.sqrt(away[0] * away[0] + away[1] * away[1] + away[2] * away[2])
+                    c, s = sincos_turns(reach * orders)
+                    ec = jnp.broadcast_to(c[7:8, :], (8, 128))
+                    es = jnp.broadcast_to(s[7:8, :], (8, 128))
+                    state.append([c, s, ec * c - es * s, es * c + ec * s, ec + ec])
+                for a in range(half // 8):
+                    re_sum = acc[0, a * 8 : a * 8 + 8, t * 128 : t * 128 + 128]
+                    im_sum = acc[1, a * 8 : a * 8 + 8, t * 128 : t * 128 + 128]
+                    for j in range(2):
+                        c, s, c_next, s_next, twice = state[j]
+                        re = prod[pair + j, a * 8 : a * 8 + 8, t * 128 : t * 128 + 128]
+                        im = prod[pair + j, half + a * 8 : half + a * 8 + 8, t * 128 : t * 128 + 128]
+                        re_sum = re_sum + (re * c + im * s)
+                        im_sum = im_sum + (im * c - re * s)
+                        state[j] = [c_next, s_next, twice * c_next - c, twice * s_next - s, twice]
+                    acc[0, a * 8 : a * 8 + 8, t * 128 : t * 128 + 128] = re_sum
+                    acc[1, a * 8 : a * 8 + 8, t * 128 : t * 128 + 128] = im_sum
+        return 0
+
+    lax.fori_loop(0, total, group, 0)
+    shares, _, per, _ = out.shape
+    each = 128 // per
+    for k in range(2):
+        for t in range(tiles):
+            turned = jnp.transpose(acc[k, :, t * 128 : (t + 1) * 128])
+            for e in range(each):
+                out[t * each + e, k, :, :] = turned[e * per : (e + 1) * per, :]
+
+
+def observe(live, centre, sp, wts, lis, shares):
+    slots, k2, bp = sp.shape
+    span = lis.shape[1] * 128
+    vm = pl.BlockSpec(memory_space=pltpu.VMEM)
+    sm = pl.BlockSpec(memory_space=pltpu.SMEM)
+    return pl.pallas_call(
+        observe_kernel,
+        out_shape=jax.ShapeDtypeStruct((shares, 2, span // shares, k2 // 2), jnp.float32),
+        in_specs=[sm, sm, vm, vm, vm],
+        out_specs=vm,
+        scratch_shapes=[
+            pltpu.VMEM((BATCH, k2, span), jnp.float32),
+            pltpu.VMEM((2, k2 // 2, span), jnp.float32),
+        ],
+        name="observe",
+        compiler_params=pltpu.CompilerParams(vmem_limit_bytes=8 * 1024 * 1024),
+    )(live, centre, sp, wts, lis)
 
 
 def swap(value, axis, bit):
@@ -461,20 +537,16 @@
     listener_angles,
     listener_range,
 ):
-    cells_x = state_section.shape[1]
-    cells_y = state_section.shape[2]
-    cells_z = state_section.shape[3]
+    cells_x, cells_y, cells_z = state_section.shape[1:]
     counts = (
         cells_x * lax.axis_size("gx"),
         cells_y * lax.axis_size("gy"),
         cells_z * lax.axis_size("gz"),
     )
     step_size = COURANT / max(counts)
-    updated = flow(state_old, state_section, counts, step_size)
-    slot_count = panel_cell.shape[0]
-    block_rows = panel_cell.shape[1]
+    slot_count, block_rows = panel_cell.shape
     samples = panel_record.shape[1]
-    density = updated[0].reshape(cells_x * cells_y, cells_z)
+    shares = lax.axis_size("gz")
     places = panel_places(
         panel_cell,
         lax.axis_index("gx"),
@@ -485,24 +557,25 @@
         cells_z,
         counts,
     )
-    normals = jnp.transpose(directions(panel_angles.reshape(2, slot_count, block_rows)), (1, 0, 2))
-    geometry = jnp.transpose(
-        jnp.concatenate([places, normals * (0.25 / math.pi)], axis=1), (1, 0, 2)
-    )
+    live = jnp.arange(slot_count, dtype=jnp.int32) < owned_blocks[0]
+    normals = directions(panel_angles.reshape(2, slot_count, block_rows))
+    normals = jnp.where(live[None, :, None], normals * (0.25 / math.pi), 0.0)
+    geometry = jnp.concatenate([jnp.transpose(places, (1, 0, 2)), normals], axis=0)
+    centres = jnp.transpose(jnp.mean(places, axis=2))
     listeners = 0.5 + listener_range[None, :] * directions(listener_angles)
+    listeners = jnp.transpose(listeners.reshape(3, shares, CHUNKS, -1), (0, 2, 1, 3))
     listeners = listeners.reshape(3, -1, 128)
-    shares = panels(
-        owned_blocks,
-        density,
-        panel_record,
-        geometry,
-        panel_cell,
-        listeners,
-        dft_table(samples, FREQS),
-        lax.axis_size("gz"),
-    )
-    spectra_out = reduce_spectra(shares)
-    return (updated, spectra_out)
+    parts = weights(owned_blocks, geometry, listeners, CHUNKS)
+    updated = flow(state_old, state_section, counts, step_size)
+    heard = spectra(
+        owned_blocks, updated.reshape(-1, cells_z), panel_record, panel_cell, dft_table(samples, FREQS), cells_x * cells_y
+    )
+    tiles = listeners.shape[1] // CHUNKS
+    pieces = []
+    for q in range(CHUNKS):
+        own = listeners[:, q * tiles : (q + 1) * tiles]
+        pieces.append(reduce_spectra(observe(owned_blocks, centres, heard, parts[q], own, shares)))
+    return (updated, jnp.concatenate(pieces, axis=1))
 
 
 def solution(mesh):

time: 137 us -> 114 us (0.83)
  waiting for transfers between devices: 36.3 us -> 12.4 us
  Pallas kernels: 48.5 us -> 32.7 us
  starting transfers between devices: 41.9 us -> 50.5 us
  local copies, waits for them, and re-layouts: 5.9 us -> 11.2 us
  other arithmetic: 2.16 us -> 4.71 us
    ppermute x5 -> x20, waiting for transfers between devices: 32.8 us -> 12.4 us  [swap(): return lax.ppermute(value, axis, [(i, i ^ bit) for i in range(size)])]
    pallas_call x1 -> x6, Pallas kernels: 16.7 us -> 7.38 us  [the longest x4 4.5 us: observe(): pl.pallas_call(observe_kernel, out_shape=jax.ShapeDtypeStruct((shares, 2,...]
    ppermute x5 -> x20, starting transfers between devices: 34.8 us -> 41.6 us  [swap(): return lax.ppermute(value, axis, [(i, i ^ bit) for i in range(size)])]
    pallas_call x3, Pallas kernels: 28.7 us -> 24 us  [line_call(): pl.pallas_call(kernel, out_shape=jax.ShapeDtypeStruct(operands[0].shape,...]
    unnamed x24 -> x38, local copies, waits for them, and re-layouts: 4.87 us -> 9.37 us
    ppermute x6, waiting for transfers between devices: 3.43 us -> 0.02 us  [neighbours(): return (lax.ppermute(last, axis, up), lax.ppermute(first, axis, down))]
    ppermute x6, starting transfers between devices: 7.11 us -> 8.9 us  [neighbours(): return (lax.ppermute(last, axis, up), lax.ppermute(first, axis, down))]
    pallas_call x1, Pallas kernels: 3.08 us -> 1.3 us  [pack(): pl.pallas_call(functools.partial(pack_kernel, cx=cx, cy=cy, cz=cz), out_s...]
  transfers between devices with their start and end apart: 11 -> 26, of which waited for: 7 -> 11; matrix products, arithmetic and copies ran while one was open for 1% -> 5% of each run, Pallas kernels for 14% -> 18%
where the time goes in v3:
time: 114 us; the launch traced here: 113 us
  starting transfers between devices  50.5 us (44%)
  Pallas kernels  32.7 us (29%)
  waiting for transfers between devices  12.4 us (11%)
  local copies, waits for them, and re-layouts  11.2 us (10%)
  other arithmetic  4.71 us (4%)
  between operations  1.71 us (2%)
    ppermute x20, starting transfers between devices, swap(): return lax.ppermute(value, axis, [(i, i ^ bit) for i in range(size)])  41.6 us
    pallas_call x3, Pallas kernels, line_call(): pl.pallas_call(kernel, out_shape=jax.ShapeDtypeStruct(operands[0].shape,...  24 us
    ppermute x20, waiting for transfers between devices, swap(): return lax.ppermute(value, axis, [(i, i ^ bit) for i in range(size)])  12.4 us
    unnamed x38, local copies, waits for them, and re-layouts  9.37 us
    ppermute x6, starting transfers between devices, neighbours(): return (lax.ppermute(last, axis, up), lax.ppermute(first, axis, down))  8.9 us
    pallas_call x4, Pallas kernels, observe(): pl.pallas_call(observe_kernel, out_shape=jax.ShapeDtypeStruct((shares, 2,...  4.5 us
    mul x2, other arithmetic, directions(): jnp.cos(polar_angle) * jnp.cos(azimuth)  2.81 us
  transfers between devices with their start and end apart: 26, of which 11 were waited for; matrix products, arithmetic and copies ran while one was open for 5% of the time, Pallas kernels for 18%

profile of v3, /device:TPU:0, one launch (start us, length us, event | category | flops | bytes accessed | tf_op | source)
XLA Modules:
  0.0 113.3 jit_solution(152032392202165642)
XLA Ops:
  4.3 3.0 %collective-permute-start = (f32[480,128]{1,0:T(8,128)}, f32[480,128]{1,0:T(8,128)}, u32[]{:S(2)}, u32[]{:S(2)}) collective-permute-start(f32[480,128]{1,0:T(8,128)} %get-tuple-element.13), channel_id=1, source_target_pairs={{0,16},{16,0},{1,17},{17,1},{2,18},{18,2},{3,19},{19,3},{4,20},{20... | collective-permute-start | bytes 737288 | tf_op jit(solution)/shard_map/ppermute | solution.py:229
  7.3 2.1 %collective-permute-start.2 = (f32[240,128]{1,0:T(8,128)}, f32[240,128]{1,0:T(8,128)}, u32[]{:S(2)}, u32[]{:S(2)}) collective-permute-start(f32[240,128]{1,0:T(8,128)} %get-tuple-element.15), channel_id=1, source_target_pairs={{0,4},{4,8},{8,12},{12,0},{1,5},{5,9},{9,13},{13,1},{2,6},{6,10},{... | collective-permute-start | bytes 368648 | tf_op jit(solution)/shard_map/ppermute | solution.py:229
  9.4 2.0 %collective-permute-start.3 = (f32[240,128]{1,0:T(8,128)}, f32[240,128]{1,0:T(8,128)}, u32[]{:S(2)}, u32[]{:S(2)}) collective-permute-start(f32[240,128]{1,0:T(8,128)} %get-tuple-element.16), channel_id=1, source_target_pairs={{4,0},{8,4},{12,8},{0,12},{5,1},{9,5},{13,9},{1,13},{6,2},{10,6},{... | collective-permute-start | bytes 368648 | tf_op jit(solution)/shard_map/ppermute | solution.py:229
  12.1 1.8 %cosine_multiply_fusion = (f32[1,4096]{1,0:T(1,128)S(1)}, f32[1,4096]{1,0:T(1,128)S(1)}, f32[1,4096]{1,0:T(1,128)S(1)}) fusion(f32[2,4096]{1,0:T(2,128)} %param.13), kind=kLoop, calls=%fused_computation.51 | loop fusion | flops 12288 | bytes 81920 | tf_op jit(solution)/shard_map/mul | solution.py:260
  17.6 1.8 %collective-permute-start.5 = (f32[60,128]{1,0:T(8,128)}, f32[60,128]{1,0:T(8,128)}, u32[]{:S(2)}, u32[]{:S(2)}) collective-permute-start(f32[60,128]{1,0:T(8,128)} %get-tuple-element.19), channel_id=1, source_target_pairs={{1,0},{2,1},{3,2},{0,3},{5,4},{6,5},{7,6},{4,7},{9,8},{10,9},{11,1... | collective-permute-start | bytes 92168 | tf_op jit(solution)/shard_map/ppermute | solution.py:229
  19.4 1.6 %weights.1 = (bf16[8192,128]{1,0:T(8,128)(2,1)S(1)}, bf16[8192,128]{1,0:T(8,128)(2,1)S(1)}, bf16[8192,128]{1,0:T(8,128)(2,1)S(1)}, bf16[8192,128]{1,0:T(8,128)(2,1)S(1)}) custom-call(s32[1]{0:T(128)} %copy.18.live, f32[6,32,128]{2,1,0:T(8,128)S(1)} %pad_maximum_fusion.1.geo, f32[3,8,128]{2,1,0:T(8,128)S(1)} %reshape.128.lis), custom_call_target="tpu_custom_call" | custom-call | tf_op jit(solution)/shard_map/weights/pallas_call | solution.py:337
  21.0 1.3 %copy-done.4 = bf16[8192,128]{1,0:T(8,128)(2,1)} copy-done((bf16[8192,128]{1,0:T(8,128)(2,1)}, bf16[8192,128]{1,0:T(8,128)(2,1)S(1)}, u32[]{:S(2)}) %copy-start.4) | copy-done | bytes 2097176
  22.3 1.3 %copy-done.6 = bf16[8192,128]{1,0:T(8,128)(2,1)} copy-done((bf16[8192,128]{1,0:T(8,128)(2,1)}, bf16[8192,128]{1,0:T(8,128)(2,1)S(1)}, u32[]{:S(2)}) %copy-start.6) | copy-done | bytes 2097176
  23.6 1.4 %copy-done.8 = bf16[8192,128]{1,0:T(8,128)(2,1)} copy-done((bf16[8192,128]{1,0:T(8,128)(2,1)}, bf16[8192,128]{1,0:T(8,128)(2,1)S(1)}, u32[]{:S(2)}) %copy-start.8) | copy-done | bytes 2097176
  26.3 8.0 %along_z.1.start = f32[2560,128]{1,0:T(8,128)S(1)} custom-call(f32[2560,128]{1,0:T(8,128)S(1)} %copy-done.11, f32[60,128]{1,0:T(8,128)S(1)} %collective-permute-done.4.left, f32[60,128]{1,0:T(8,128)} %collective-permute-done.5.right), custom_call_target="tpu_custom_call" | custom-call | tf_op jit(solution)/shard_map/along_z/pallas_call | solution.py:208
  34.4 7.8 %along_y.1.start = f32[2560,128]{1,0:T(8,128)S(1)} custom-call(f32[2560,128]{1,0:T(8,128)S(1)} %bitcast.49, f32[240,128]{1,0:T(8,128)} %collective-permute-done.2.left, f32[240,128]{1,0:T(8,128)} %collective-permute-done.3.right, f32[2560,128]{1,0:T(8,128)S(1)} %along_z.1.start), custom_call_target="tpu_custom_call" | custom-call | tf_op jit(solution)/shard_map/along_y/pallas_call | solution.py:208
  42.2 8.3 %along_x.1.dens = f32[2560,128]{1,0:T(8,128)} custom-call(f32[2560,128]{1,0:T(8,128)S(1)} %bitcast.50, f32[480,128]{1,0:T(8,128)} %collective-permute-done.left, f32[480,128]{1,0:T(8,128)} %collective-permute-done.1.right, f32[2560,128]{1,0:T(8,128)S(1)} %along_y.1.start, f32[2560,128]{1,0:T(8,128)S(1)} %bitcast.52), custom_call_target="tpu_custom_call" | custom-call | tf_op jit(solution)/shard_map/along_x/pallas_call | solution.py:208
  51.8 1.3 %spectra.1.sp = bf16[32,256,128]{2,1,0:T(8,128)(2,1)S(1)} custom-call(s32[1]{0:T(128)} %copy.18.live, f32[2560,128]{1,0:T(8,128)S(1)} %copy-done.2, bf16[4096,512]{1,0:T(8,128)(2,1)S(1)} %copy-done.3, s32[32,128]{1,0:T(8,128)S(1)} %copy-done.14, bf16[256,512]{1,0:T(8,128)(2,1)S(1)} %copy-done.13), custom_call_target="tpu_custom_call" | custom-call | tf_op jit(solution)/shard_map/spectra/pallas_call | solution.py:411
  54.6 18.6 %collective-permute-start.21 = (f32[2,2,64,128]{3,2,1,0:T(8,128)S(1)}, f32[2,2,64,128]{3,2,1,0:T(8,128)S(1)}, u32[]{:S(2)}, u32[]{:S(2)}) collective-permute-start(f32[2,2,64,128]{3,2,1,0:T(8,128)S(1)} %dynamic-slice_bitcast_fusion), channel_id=1, source_target_pairs={{0,1},{1,0},{2,3},{3,2},{4,5},{5,4},{6,7},{7,6},{8,9},{9,8},{10,11... | collective-permute-start | bytes 393224 | tf_op jit(solution)/shard_map/ppermute | solution.py:507
  74.4 3.1 %collective-permute-start.16 = (f32[2,2,64,128]{3,2,1,0:T(8,128)S(1)}, f32[2,2,64,128]{3,2,1,0:T(8,128)S(1)}, u32[]{:S(2)}, u32[]{:S(2)}) collective-permute-start(f32[2,2,64,128]{3,2,1,0:T(8,128)S(1)} %dynamic-slice_bitcast_fusion.1), channel_id=1, source_target_pairs={{0,1},{1,0},{2,3},{3,2},{4,5},{5,4},{6,7},{7,6},{8,9},{9,8},{10,11... | collective-permute-start | bytes 393224 | tf_op jit(solution)/shard_map/ppermute | solution.py:507
  78.6 3.1 %collective-permute-start.11 = (f32[2,2,64,128]{3,2,1,0:T(8,128)S(1)}, f32[2,2,64,128]{3,2,1,0:T(8,128)S(1)}, u32[]{:S(2)}, u32[]{:S(2)}) collective-permute-start(f32[2,2,64,128]{3,2,1,0:T(8,128)S(1)} %dynamic-slice_bitcast_fusion.2), channel_id=1, source_target_pairs={{0,1},{1,0},{2,3},{3,2},{4,5},{5,4},{6,7},{7,6},{8,9},{9,8},{10,11... | collective-permute-start | bytes 393224 | tf_op jit(solution)/shard_map/ppermute | solution.py:507
  82.9 3.0 %collective-permute-start.6 = (f32[2,2,64,128]{3,2,1,0:T(8,128)S(1)}, f32[2,2,64,128]{3,2,1,0:T(8,128)S(1)}, u32[]{:S(2)}, u32[]{:S(2)}) collective-permute-start(f32[2,2,64,128]{3,2,1,0:T(8,128)S(1)} %dynamic-slice_bitcast_fusion.3), channel_id=1, source_target_pairs={{0,1},{1,0},{2,3},{3,2},{4,5},{5,4},{6,7},{7,6},{8,9},{9,8},{10,11... | collective-permute-start | bytes 393224 | tf_op jit(solution)/shard_map/ppermute | solution.py:507
  86.0 2.1 %collective-permute-start.17 = (f32[1,2,64,128]{3,2,1,0:T(8,128)S(1)}, f32[1,2,64,128]{3,2,1,0:T(8,128)S(1)}, u32[]{:S(2)}, u32[]{:S(2)}) collective-permute-start(f32[1,2,64,128]{3,2,1,0:T(8,128)S(1)} %constant_dynamic-slice_fusion.1), channel_id=1, source_target_pairs={{0,2},{1,3},{2,0},{3,1},{4,6},{5,7},{6,4},{7,5},{8,10},{9,11},{10,... | collective-permute-start | bytes 196616 | tf_op jit(solution)/shard_map/ppermute | solution.py:507
  88.3 2.1 %collective-permute-start.7 = (f32[1,2,64,128]{3,2,1,0:T(8,128)S(1)}, f32[1,2,64,128]{3,2,1,0:T(8,128)S(1)}, u32[]{:S(2)}, u32[]{:S(2)}) collective-permute-start(f32[1,2,64,128]{3,2,1,0:T(8,128)S(1)} %constant_dynamic-slice_fusion.3), channel_id=1, source_target_pairs={{0,2},{1,3},{2,0},{3,1},{4,6},{5,7},{6,4},{7,5},{8,10},{9,11},{10,... | collective-permute-start | bytes 196616 | tf_op jit(solution)/shard_map/ppermute | solution.py:507
  98.1 1.4 %collective-permute-start.14 = (f32[2,64,128]{2,1,0:T(8,128)S(1)}, f32[2,64,128]{2,1,0:T(8,128)S(1)}, u32[]{:S(2)}, u32[]{:S(2)}) collective-permute-start(f32[2,64,128]{2,1,0:T(8,128)S(1)} %add.175), channel_id=1, source_target_pairs={{0,4},{4,0},{8,12},{12,8},{1,5},{5,1},{9,13},{13,9},{2,6},{6,2},{1... | collective-permute-start | bytes 196616 | tf_op jit(solution)/shard_map/ppermute | solution.py:507
  100.4 2.5 %collective-permute-done.19 = f32[2,64,128]{2,1,0:T(8,128)S(1)} collective-permute-done((f32[2,64,128]{2,1,0:T(8,128)S(1)}, f32[2,64,128]{2,1,0:T(8,128)S(1)}, u32[]{:S(2)}, u32[]{:S(2)}) %collective-permute-start.19) | collective-permute-done | bytes 65568 | tf_op jit(solution)/shard_map/ppermute | solution.py:507
  103.6 2.4 %collective-permute-start.15 = (f32[2,64,128]{2,1,0:T(8,128)S(1)}, f32[2,64,128]{2,1,0:T(8,128)S(1)}, u32[]{:S(2)}, u32[]{:S(2)}) collective-permute-start(f32[2,64,128]{2,1,0:T(8,128)S(1)} %add.176), channel_id=1, source_target_pairs={{0,8},{4,12},{8,0},{12,4},{1,9},{5,13},{9,1},{13,5},{2,10},{6,14},... | collective-permute-start | bytes 196616 | tf_op jit(solution)/shard_map/ppermute | solution.py:507
  106.6 3.1 %collective-permute-done.25 = f32[2,64,128]{2,1,0:T(8,128)S(1)} collective-permute-done((f32[2,64,128]{2,1,0:T(8,128)S(1)}, f32[2,64,128]{2,1,0:T(8,128)S(1)}, u32[]{:S(2)}, u32[]{:S(2)}) %collective-permute-start.25) | collective-permute-done | bytes 65568 | tf_op jit(solution)/shard_map/ppermute | solution.py:507
  109.8 1.4 %collective-permute-done.20 = f32[2,64,128]{2,1,0:T(8,128)S(1)} collective-permute-done((f32[2,64,128]{2,1,0:T(8,128)S(1)}, f32[2,64,128]{2,1,0:T(8,128)S(1)}, u32[]{:S(2)}, u32[]{:S(2)}) %collective-permute-start.20) | collective-permute-done | bytes 65568 | tf_op jit(solution)/shard_map/ppermute | solution.py:507
  (124 shorter events, 27.3 us)
Async XLA Ops:
  4.3 37.9 %collective-permute-start = (f32[480,128]{1,0:T(8,128)}, f32[480,128]{1,0:T(8,128)}, u32[]{:S(2)}, u32[]{:S(2)}) collective-permute-start(f32[480,128]{1,0:T(8,128)} %get-tuple-element.13), channel_id=1, source_target_pairs={{0,16},{16,0},{1,17},{17,1},{2,18},{18,2},{3,19},{19,3},{4,20},{20... | collective-permute-start | bytes 737288 | tf_op jit(solution)/shard_map/ppermute | solution.py:229
  7.3 34.9 %collective-permute-start.1 = (f32[480,128]{1,0:T(8,128)}, f32[480,128]{1,0:T(8,128)}, u32[]{:S(2)}, u32[]{:S(2)}) collective-permute-start(f32[480,128]{1,0:T(8,128)} %get-tuple-element.14), channel_id=1, source_target_pairs={{16,0},{0,16},{17,1},{1,17},{18,2},{2,18},{19,3},{3,19},{20,4},{4,... | collective-permute-start | bytes 737288 | tf_op jit(solution)/shard_map/ppermute | solution.py:229
  7.3 27.0 %collective-permute-start.2 = (f32[240,128]{1,0:T(8,128)}, f32[240,128]{1,0:T(8,128)}, u32[]{:S(2)}, u32[]{:S(2)}) collective-permute-start(f32[240,128]{1,0:T(8,128)} %get-tuple-element.15), channel_id=1, source_target_pairs={{0,4},{4,8},{8,12},{12,0},{1,5},{5,9},{9,13},{13,1},{2,6},{6,10},{... | collective-permute-start | bytes 368648 | tf_op jit(solution)/shard_map/ppermute | solution.py:229
  9.4 25.0 %collective-permute-start.3 = (f32[240,128]{1,0:T(8,128)}, f32[240,128]{1,0:T(8,128)}, u32[]{:S(2)}, u32[]{:S(2)}) collective-permute-start(f32[240,128]{1,0:T(8,128)} %get-tuple-element.16), channel_id=1, source_target_pairs={{4,0},{8,4},{12,8},{0,12},{5,1},{9,5},{13,9},{1,13},{6,2},{10,6},{... | collective-permute-start | bytes 368648 | tf_op jit(solution)/shard_map/ppermute | solution.py:229
  11.4 6.2 %collective-permute-start.4 = (f32[60,128]{1,0:T(8,128)S(1)}, f32[60,128]{1,0:T(8,128)S(1)}, u32[]{:S(2)}, u32[]{:S(2)}) collective-permute-start(f32[60,128]{1,0:T(8,128)S(1)} %get-tuple-element.18), channel_id=1, source_target_pairs={{0,1},{1,2},{2,3},{3,0},{4,5},{5,6},{6,7},{7,4},{8,9},{9,10},{10,1... | collective-permute-start | bytes 92168 | tf_op jit(solution)/shard_map/ppermute | solution.py:229
  17.6 7.4 %collective-permute-start.5 = (f32[60,128]{1,0:T(8,128)}, f32[60,128]{1,0:T(8,128)}, u32[]{:S(2)}, u32[]{:S(2)}) collective-permute-start(f32[60,128]{1,0:T(8,128)} %get-tuple-element.19), channel_id=1, source_target_pairs={{1,0},{2,1},{3,2},{0,3},{5,4},{6,5},{7,6},{4,7},{9,8},{10,9},{11,1... | collective-permute-start | bytes 92168 | tf_op jit(solution)/shard_map/ppermute | solution.py:229
  54.6 31.2 %collective-permute-start.21 = (f32[2,2,64,128]{3,2,1,0:T(8,128)S(1)}, f32[2,2,64,128]{3,2,1,0:T(8,128)S(1)}, u32[]{:S(2)}, u32[]{:S(2)}) collective-permute-start(f32[2,2,64,128]{3,2,1,0:T(8,128)S(1)} %dynamic-slice_bitcast_fusion), channel_id=1, source_target_pairs={{0,1},{1,0},{2,3},{3,2},{4,5},{5,4},{6,7},{7,6},{8,9},{9,8},{10,11... | collective-permute-start | bytes 393224 | tf_op jit(solution)/shard_map/ppermute | solution.py:507
  74.4 11.6 %collective-permute-start.16 = (f32[2,2,64,128]{3,2,1,0:T(8,128)S(1)}, f32[2,2,64,128]{3,2,1,0:T(8,128)S(1)}, u32[]{:S(2)}, u32[]{:S(2)}) collective-permute-start(f32[2,2,64,128]{3,2,1,0:T(8,128)S(1)} %dynamic-slice_bitcast_fusion.1), channel_id=1, source_target_pairs={{0,1},{1,0},{2,3},{3,2},{4,5},{5,4},{6,7},{7,6},{8,9},{9,8},{10,11... | collective-permute-start | bytes 393224 | tf_op jit(solution)/shard_map/ppermute | solution.py:507
  78.6 9.5 %collective-permute-start.11 = (f32[2,2,64,128]{3,2,1,0:T(8,128)S(1)}, f32[2,2,64,128]{3,2,1,0:T(8,128)S(1)}, u32[]{:S(2)}, u32[]{:S(2)}) collective-permute-start(f32[2,2,64,128]{3,2,1,0:T(8,128)S(1)} %dynamic-slice_bitcast_fusion.2), channel_id=1, source_target_pairs={{0,1},{1,0},{2,3},{3,2},{4,5},{5,4},{6,7},{7,6},{8,9},{9,8},{10,11... | collective-permute-start | bytes 393224 | tf_op jit(solution)/shard_map/ppermute | solution.py:507
  82.9 5.4 %collective-permute-start.6 = (f32[2,2,64,128]{3,2,1,0:T(8,128)S(1)}, f32[2,2,64,128]{3,2,1,0:T(8,128)S(1)}, u32[]{:S(2)}, u32[]{:S(2)}) collective-permute-start(f32[2,2,64,128]{3,2,1,0:T(8,128)S(1)} %dynamic-slice_bitcast_fusion.3), channel_id=1, source_target_pairs={{0,1},{1,0},{2,3},{3,2},{4,5},{5,4},{6,7},{7,6},{8,9},{9,8},{10,11... | collective-permute-start | bytes 393224 | tf_op jit(solution)/shard_map/ppermute | solution.py:507
  85.9 5.0 %collective-permute-start.22 = (f32[1,2,64,128]{3,2,1,0:T(8,128)S(1)}, f32[1,2,64,128]{3,2,1,0:T(8,128)S(1)}, u32[]{:S(2)}, u32[]{:S(2)}) collective-permute-start(f32[1,2,64,128]{3,2,1,0:T(8,128)S(1)} %constant_dynamic-slice_fusion), channel_id=1, source_target_pairs={{0,2},{1,3},{2,0},{3,1},{4,6},{5,7},{6,4},{7,5},{8,10},{9,11},{10,... | collective-permute-start | bytes 196616 | tf_op jit(solution)/shard_map/ppermute | solution.py:507
  86.0 6.3 %collective-permute-start.17 = (f32[1,2,64,128]{3,2,1,0:T(8,128)S(1)}, f32[1,2,64,128]{3,2,1,0:T(8,128)S(1)}, u32[]{:S(2)}, u32[]{:S(2)}) collective-permute-start(f32[1,2,64,128]{3,2,1,0:T(8,128)S(1)} %constant_dynamic-slice_fusion.1), channel_id=1, source_target_pairs={{0,2},{1,3},{2,0},{3,1},{4,6},{5,7},{6,4},{7,5},{8,10},{9,11},{10,... | collective-permute-start | bytes 196616 | tf_op jit(solution)/shard_map/ppermute | solution.py:507
  88.1 5.4 %collective-permute-start.12 = (f32[1,2,64,128]{3,2,1,0:T(8,128)S(1)}, f32[1,2,64,128]{3,2,1,0:T(8,128)S(1)}, u32[]{:S(2)}, u32[]{:S(2)}) collective-permute-start(f32[1,2,64,128]{3,2,1,0:T(8,128)S(1)} %constant_dynamic-slice_fusion.2), channel_id=1, source_target_pairs={{0,2},{1,3},{2,0},{3,1},{4,6},{5,7},{6,4},{7,5},{8,10},{9,11},{10,... | collective-permute-start | bytes 196616 | tf_op jit(solution)/shard_map/ppermute | solution.py:507
  88.3 6.2 %collective-permute-start.7 = (f32[1,2,64,128]{3,2,1,0:T(8,128)S(1)}, f32[1,2,64,128]{3,2,1,0:T(8,128)S(1)}, u32[]{:S(2)}, u32[]{:S(2)}) collective-permute-start(f32[1,2,64,128]{3,2,1,0:T(8,128)S(1)} %constant_dynamic-slice_fusion.3), channel_id=1, source_target_pairs={{0,2},{1,3},{2,0},{3,1},{4,6},{5,7},{6,4},{7,5},{8,10},{9,11},{10,... | collective-permute-start | bytes 196616 | tf_op jit(solution)/shard_map/ppermute | solution.py:507
  90.9 5.0 %collective-permute-start.23 = (f32[2,64,128]{2,1,0:T(8,128)S(1)}, f32[2,64,128]{2,1,0:T(8,128)S(1)}, u32[]{:S(2)}, u32[]{:S(2)}) collective-permute-start(f32[2,64,128]{2,1,0:T(8,128)S(1)} %add_bitcast_fusion), channel_id=1, source_target_pairs={{0,16},{16,0},{1,17},{17,1},{2,18},{18,2},{3,19},{19,3},{4,20},{20... | collective-permute-start | bytes 196616 | tf_op jit(solution)/shard_map/ppermute | solution.py:507
  92.3 5.0 %collective-permute-start.18 = (f32[2,64,128]{2,1,0:T(8,128)S(1)}, f32[2,64,128]{2,1,0:T(8,128)S(1)}, u32[]{:S(2)}, u32[]{:S(2)}) collective-permute-start(f32[2,64,128]{2,1,0:T(8,128)S(1)} %add_bitcast_fusion.1), channel_id=1, source_target_pairs={{0,16},{16,0},{1,17},{17,1},{2,18},{18,2},{3,19},{19,3},{4,20},{20... | collective-permute-start | bytes 196616 | tf_op jit(solution)/shard_map/ppermute | solution.py:507
  94.5 5.0 %collective-permute-start.8 = (f32[2,64,128]{2,1,0:T(8,128)S(1)}, f32[2,64,128]{2,1,0:T(8,128)S(1)}, u32[]{:S(2)}, u32[]{:S(2)}) collective-permute-start(f32[2,64,128]{2,1,0:T(8,128)S(1)} %add_bitcast_fusion.3), channel_id=1, source_target_pairs={{0,16},{16,0},{1,17},{17,1},{2,18},{18,2},{3,19},{19,3},{4,20},{20... | collective-permute-start | bytes 196616 | tf_op jit(solution)/shard_map/ppermute | solution.py:507
  97.3 5.5 %collective-permute-start.19 = (f32[2,64,128]{2,1,0:T(8,128)S(1)}, f32[2,64,128]{2,1,0:T(8,128)S(1)}, u32[]{:S(2)}, u32[]{:S(2)}) collective-permute-start(f32[2,64,128]{2,1,0:T(8,128)S(1)} %add.180), channel_id=1, source_target_pairs={{0,4},{4,0},{8,12},{12,8},{1,5},{5,1},{9,13},{13,9},{2,6},{6,2},{1... | collective-permute-start | bytes 196616 | tf_op jit(solution)/shard_map/ppermute | solution.py:507
  98.1 5.5 %collective-permute-start.14 = (f32[2,64,128]{2,1,0:T(8,128)S(1)}, f32[2,64,128]{2,1,0:T(8,128)S(1)}, u32[]{:S(2)}, u32[]{:S(2)}) collective-permute-start(f32[2,64,128]{2,1,0:T(8,128)S(1)} %add.175), channel_id=1, source_target_pairs={{0,4},{4,0},{8,12},{12,8},{1,5},{5,1},{9,13},{13,9},{2,6},{6,2},{1... | collective-permute-start | bytes 196616 | tf_op jit(solution)/shard_map/ppermute | solution.py:507
  99.5 6.4 %collective-permute-start.9 = (f32[2,64,128]{2,1,0:T(8,128)S(1)}, f32[2,64,128]{2,1,0:T(8,128)S(1)}, u32[]{:S(2)}, u32[]{:S(2)}) collective-permute-start(f32[2,64,128]{2,1,0:T(8,128)S(1)} %add.170), channel_id=1, source_target_pairs={{0,4},{4,0},{8,12},{12,8},{1,5},{5,1},{9,13},{13,9},{2,6},{6,2},{1... | collective-permute-start | bytes 196616 | tf_op jit(solution)/shard_map/ppermute | solution.py:507
  100.3 9.5 %collective-permute-start.25 = (f32[2,64,128]{2,1,0:T(8,128)S(1)}, f32[2,64,128]{2,1,0:T(8,128)S(1)}, u32[]{:S(2)}, u32[]{:S(2)}) collective-permute-start(f32[2,64,128]{2,1,0:T(8,128)S(1)} %add.186), channel_id=1, source_target_pairs={{0,8},{4,12},{8,0},{12,4},{1,9},{5,13},{9,1},{13,5},{2,10},{6,14},... | collective-permute-start | bytes 196616 | tf_op jit(solution)/shard_map/ppermute | solution.py:507
  102.9 8.3 %collective-permute-start.20 = (f32[2,64,128]{2,1,0:T(8,128)S(1)}, f32[2,64,128]{2,1,0:T(8,128)S(1)}, u32[]{:S(2)}, u32[]{:S(2)}) collective-permute-start(f32[2,64,128]{2,1,0:T(8,128)S(1)} %add.181), channel_id=1, source_target_pairs={{0,8},{4,12},{8,0},{12,4},{1,9},{5,13},{9,1},{13,5},{2,10},{6,14},... | collective-permute-start | bytes 196616 | tf_op jit(solution)/shard_map/ppermute | solution.py:507
  103.6 8.3 %collective-permute-start.15 = (f32[2,64,128]{2,1,0:T(8,128)S(1)}, f32[2,64,128]{2,1,0:T(8,128)S(1)}, u32[]{:S(2)}, u32[]{:S(2)}) collective-permute-start(f32[2,64,128]{2,1,0:T(8,128)S(1)} %add.176), channel_id=1, source_target_pairs={{0,8},{4,12},{8,0},{12,4},{1,9},{5,13},{9,1},{13,5},{2,10},{6,14},... | collective-permute-start | bytes 196616 | tf_op jit(solution)/shard_map/ppermute | solution.py:507
  105.9 6.6 %collective-permute-start.10 = (f32[2,64,128]{2,1,0:T(8,128)S(1)}, f32[2,64,128]{2,1,0:T(8,128)S(1)}, u32[]{:S(2)}, u32[]{:S(2)}) collective-permute-start(f32[2,64,128]{2,1,0:T(8,128)S(1)} %add.171), channel_id=1, source_target_pairs={{0,8},{4,12},{8,0},{12,4},{1,9},{5,13},{9,1},{13,5},{2,10},{6,14},... | collective-permute-start | bytes 196616 | tf_op jit(solution)/shard_map/ppermute | solution.py:507
  (21 other events, 136.4 us)

commit v4 on v3

--- a/solution.py
+++ b/solution.py
@@ -12,6 +12,7 @@
 FREQS = 128
 BATCH = 4
 CHUNKS = 4
+TIED = True
 NT = (((1,), (1,)), ((), ()))
 
 
@@ -22,7 +23,7 @@
 COURANT = 0.08
 
 
-def pack_kernel(state, turned, zlo, zhi, ylo, yhi, xlo, xhi, *, cx, cy, cz):
+def pack_kernel(state, turned, zlo, zhi, ylo, yhi, xends, *, cx, cy, cz):
     plane = cx * cy
     groups = plane // 128
     for c in range(5):
@@ -34,21 +35,21 @@
             yhi[(c * 3 + k) * cx : (c * 3 + k + 1) * cx, :] = state[pl.ds(c * plane + cy - 3 + k, cx, stride=cy), :]
             zlo[(c * 3 + k) * groups : (c * 3 + k + 1) * groups, :] = turned[pl.ds(c * plane + k, groups, stride=128), :]
             zhi[(c * 3 + k) * groups : (c * 3 + k + 1) * groups, :] = turned[pl.ds(c * plane + cz - 3 + k, groups, stride=128), :]
-        xlo[c * 3 * cy : (c + 1) * 3 * cy, :] = state[c * plane : c * plane + 3 * cy, :]
-        xhi[c * 3 * cy : (c + 1) * 3 * cy, :] = state[c * plane + (cx - 3) * cy : (c + 1) * plane, :]
+        xends[c * 3 * cy : (c + 1) * 3 * cy, :] = state[c * plane : c * plane + 3 * cy, :]
+        xends[(5 + c) * 3 * cy : (6 + c) * 3 * cy, :] = state[c * plane + (cx - 3) * cy : (c + 1) * plane, :]
 
 
 def pack(state, cx, cy, cz):
     groups = cx * cy // 128
-    rows = [state.shape[0]] + [15 * groups] * 2 + [15 * cx] * 2 + [15 * cy] * 2
+    rows = [state.shape[0]] + [15 * groups] * 2 + [15 * cx] * 2 + [30 * cy]
     vm = pl.BlockSpec(memory_space=pltpu.VMEM)
     return pl.pallas_call(
         functools.partial(pack_kernel, cx=cx, cy=cy, cz=cz),
         out_shape=[jax.ShapeDtypeStruct((r, 128), jnp.float32) for r in rows],
         in_specs=[vm],
-        out_specs=[vm] * 7,
+        out_specs=[vm] * 6,
         name="pack",
-        compiler_params=pltpu.CompilerParams(vmem_limit_bytes=10 * 1024 * 1024),
+        compiler_params=pltpu.CompilerParams(vmem_limit_bytes=2 * 1024 * 1024),
     )(state)
 
 
@@ -94,7 +95,7 @@
             flux[pl.ds(4 * span + at, 8), :] = (energy + pressure) * u
         return 0
 
-    lax.fori_loop(0, length, fluxes, 0, unroll=2)
+    lax.fori_loop(0, length, fluxes, 0, unroll=5 if tiles == 1 else 2)
 
     def waves(i, _):
         for w in range(tiles):
@@ -105,7 +106,7 @@
             wave[pl.ds(at, 8), :] = top
         return 0
 
-    lax.fori_loop(0, n + 1, waves, 0)
+    lax.fori_loop(0, n + 1, waves, 0, unroll={1: 5, 2: 3}.get(tiles, 1))
 
     def line(index, _):
         c = index // tiles
@@ -185,14 +186,14 @@
     line_kernel_body(cells, flux, speed, wave, emit, n=cy, width=cx, axis=1)
 
 
-def x_kernel(state, left, right, start, old, out, cells, flux, speed, wave, *, cx, cy, scale):
+def x_kernel(state, ends, start, old, out, density, cells, flux, speed, wave, *, cx, cy, scale):
     plane = cx * cy
     length = cx + 6
     for c in range(5):
         base = c * length * cy
-        cells[base : base + 3 * cy, :] = left[c * 3 * cy : (c + 1) * 3 * cy, :]
+        cells[base : base + 3 * cy, :] = ends[(5 + c) * 3 * cy : (6 + c) * 3 * cy, :]
         cells[base + 3 * cy : base + (cx + 3) * cy, :] = state[c * plane : (c + 1) * plane, :]
-        cells[base + (cx + 3) * cy : base + length * cy, :] = right[c * 3 * cy : (c + 1) * 3 * cy, :]
+        cells[base + (cx + 3) * cy : base + length * cy, :] = ends[c * 3 * cy : (c + 1) * 3 * cy, :]
 
     def emit(c, w, i, value):
         rows = pl.ds(pl.multiple_of(c * plane + i * cy + w * 8, 8), 8)
@@ -200,16 +201,17 @@
         out[rows, :] = (0.75 * old[rows, :] + 0.25 * state[rows, :]) - change
 
     line_kernel_body(cells, flux, speed, wave, emit, n=cx, width=cy, axis=0)
-
-
-def line_call(kernel, operands, n, width, name, more=()):
+    density[...] = out[0:plane, :]
+
+
+def line_call(kernel, operands, n, width, name, more=(), results=()):
     length = n + 6
     vm = pl.BlockSpec(memory_space=pltpu.VMEM)
     return pl.pallas_call(
         kernel,
-        out_shape=jax.ShapeDtypeStruct(operands[0].shape, jnp.float32),
+        out_shape=[jax.ShapeDtypeStruct(shape, jnp.float32) for shape in (operands[0].shape, *results)],
         in_specs=[vm] * len(operands),
-        out_specs=vm,
+        out_specs=[vm] * (1 + len(results)),
         scratch_shapes=[
             pltpu.VMEM((5 * length * width, 128), jnp.float32),
             pltpu.VMEM((5 * length * width, 128), jnp.float32),
@@ -218,7 +220,7 @@
         ]
         + list(more),
         name=name,
-        compiler_params=pltpu.CompilerParams(vmem_limit_bytes=14 * 1024 * 1024),
+        compiler_params=pltpu.CompilerParams(vmem_limit_bytes=6 * 1024 * 1024),
     )(*operands)
 
 
@@ -233,45 +235,26 @@
     shape = state_section.shape
     cx, cy, cz = shape[1:]
     state = state_section.reshape(-1, cz)
-    turned, zlo, zhi, ylo, yhi, xlo, xhi = pack(state, cx, cy, cz)
+    turned, zlo, zhi, ylo, yhi, xends = pack(state, cx, cy, cz)
+    if lax.axis_size("gx") == 2:
+        ends = swap(xends, "gx", 1)
+    else:
+        ends = jnp.concatenate(neighbours(xends[: xends.shape[0] // 2], xends[xends.shape[0] // 2 :], "gx")[::-1])
     zl, zr = neighbours(zlo, zhi, "gz")
     yl, yr = neighbours(ylo, yhi, "gy")
-    xl, xr = neighbours(xlo, xhi, "gx")
     scales = [0.25 * step_size * n / 12.0 for n in counts]
     plane = cx * cy
-    part = line_call(
+    (part,) = line_call(
         functools.partial(z_kernel, cx=cx, cy=cy, cz=cz, scale=scales[2]),
         (turned, zl, zr), cz // 2, plane // 64, "along_z",
         (pltpu.VMEM((5 * plane, 128), jnp.float32),),
     )
-    part = line_call(functools.partial(y_kernel, cx=cx, cy=cy, scale=scales[1]), (state, yl, yr, part), cy, cx, "along_y")
-    updated = line_call(
+    (part,) = line_call(functools.partial(y_kernel, cx=cx, cy=cy, scale=scales[1]), (state, yl, yr, part), cy, cx, "along_y")
+    updated, density = line_call(
         functools.partial(x_kernel, cx=cx, cy=cy, scale=scales[0]),
-        (state, xl, xr, part, state_old.reshape(-1, cz)), cx, cy, "along_x",
+        (state, ends, part, state_old.reshape(-1, cz)), cx, cy, "along_x", (), ((plane, cz),),
     )
-    return updated.reshape(shape)
-
-
-def directions(angles):
-    polar_angle = 0.5 * angles[0]
-    azimuth = angles[1]
-    return jnp.stack(
-        [
-            jnp.cos(polar_angle) * jnp.cos(azimuth),
-            jnp.cos(polar_angle) * jnp.sin(azimuth),
-            jnp.sin(polar_angle),
-        ]
-    )
-
-
-def panel_places(cell_rows, block_x, block_y, block_z, cells_x, cells_y, cells_z, counts):
-    along_x = cell_rows // (cells_y * cells_z)
-    along_y = cell_rows // cells_z % cells_y
-    along_z = cell_rows % cells_z
-    place_x = ((block_x * cells_x + along_x).astype(jnp.float32) + 0.5) / counts[0]
-    place_y = ((block_y * cells_y + along_y).astype(jnp.float32) + 0.5) / counts[1]
-    place_z = ((block_z * cells_z + along_z).astype(jnp.float32) + 0.5) / counts[2]
-    return jnp.stack([place_x, place_y, place_z], axis=1)
+    return updated.reshape(shape), density
 
 
 def dft_table(sample_count, freq_count):
@@ -283,9 +266,7 @@
     return jnp.asarray(both, jnp.bfloat16)
 
 
-def sincos_turns(turns):
-    r = turns - jnp.round(turns)
-    x = r * math.pi
+def double_angle(x):
     x2 = x * x
     s = 1.0 / 6227020800.0
     s = s * x2 - 1.0 / 39916800.0
@@ -305,10 +286,35 @@
     return 1.0 - s2 * s, s2 * c
 
 
-def weights_kernel(live, geo, lis, *refs):
-    outs, lisb = refs[:-1], refs[-1]
+def sincos_turns(turns):
+    return double_angle((turns - jnp.round(turns)) * math.pi)
+
+
+def direction(polar, azimuth):
+    cos_p, sin_p = double_angle(0.25 * polar)
+    cos_a, sin_a = double_angle(0.5 * azimuth)
+    return cos_p * cos_a, cos_p * sin_a, sin_p
+
+
+def weights_kernel(live, corner, cell, angles, raw, out, centre, lis, geo, lisb, *, sizes, counts):
+    slots, bp = cell.shape
     tiles = lis.shape[1]
-    span = tiles * 128 // len(outs)
+    span = tiles * 128 // CHUNKS
+    cells = cell[...].astype(jnp.float32)
+    along_x = jnp.floor((cells + 0.5) * (1.0 / (sizes[1] * sizes[2])))
+    rest = cells - along_x * float(sizes[1] * sizes[2])
+    along_y = jnp.floor((rest + 0.5) * (1.0 / sizes[2]))
+    along_z = rest - along_y * float(sizes[2])
+    for k, along in enumerate((along_x, along_y, along_z)):
+        place = ((along + corner[k].astype(jnp.float32)) + 0.5) / float(counts[k])
+        geo[k] = place
+        mean = jnp.sum(place, axis=1, keepdims=True) * (1.0 / bp)
+        centre[k] = jnp.broadcast_to(mean, (slots, 128))
+    shown = lax.broadcasted_iota(jnp.int32, (slots, bp), 0) < live[0]
+    for k, part in enumerate(direction(angles[0], angles[1])):
+        geo[3 + k] = jnp.where(shown, part * (0.25 / math.pi), 0.0)
+    for k, part in enumerate(direction(raw[0], raw[1])):
+        lis[k] = 0.5 + raw[2] * part
     for k in range(3):
         for t in range(tiles):
             row = lis[k, t : t + 1, :]
@@ -316,7 +322,7 @@
 
     def block(b, _):
         px, py, pz, nx, ny, nz = [geo[k, pl.ds(b, 1), :] for k in range(6)]
-        for q, out in enumerate(outs):
+        for q in range(CHUNKS):
             for r in range(0, span, 16):
                 at = q * span + r
                 ox = lisb[0, at : at + 16, :] - px
@@ -324,25 +330,31 @@
                 oz = lisb[2, at : at + 16, :] - pz
                 d2 = ox * ox + oy * oy + oz * oz
                 facing = nx * ox + ny * oy + nz * oz
-                out[pl.ds(pl.multiple_of(b * span + r, 16), 16), :] = (facing * (1.0 / d2)).astype(jnp.bfloat16)
+                row = pl.multiple_of(q * slots * span + b * span + r, 16)
+                out[pl.ds(row, 16), :] = (facing * (1.0 / d2)).astype(jnp.bfloat16)
         return 0
 
     lax.fori_loop(0, (live[0] + BATCH - 1) // BATCH * BATCH, block, 0)
 
 
-def weights(live, geo, lis, chunks):
-    slots, bp = geo.shape[1:]
-    obs = lis.shape[1] * 128
+def weights(live, corner, cell, angles, raw, sizes, counts):
+    slots, bp = cell.shape
+    obs = raw.shape[1] * 128
     vm = pl.BlockSpec(memory_space=pltpu.VMEM)
+    sm = pl.BlockSpec(memory_space=pltpu.SMEM)
     return pl.pallas_call(
-        weights_kernel,
-        out_shape=[jax.ShapeDtypeStruct((slots * obs // chunks, bp), jnp.bfloat16)] * chunks,
-        in_specs=[pl.BlockSpec(memory_space=pltpu.SMEM), vm, vm],
-        out_specs=[vm] * chunks,
-        scratch_shapes=[pltpu.VMEM((3, obs, 128), jnp.float32)],
+        functools.partial(weights_kernel, sizes=sizes, counts=counts),
+        out_shape=[
+            jax.ShapeDtypeStruct((slots * obs, bp), jnp.bfloat16),
+            jax.ShapeDtypeStruct((3, slots, 128), jnp.float32),
+            jax.ShapeDtypeStruct(raw.shape, jnp.float32),
+        ],
+        in_specs=[sm, sm, vm, vm, vm],
+        out_specs=[vm] * 3,
+        scratch_shapes=[pltpu.VMEM((6, slots, bp), jnp.float32), pltpu.VMEM((3, obs, 128), jnp.float32)],
         name="weights",
-        compiler_params=pltpu.CompilerParams(vmem_limit_bytes=14 * 1024 * 1024),
-    )(live, geo, lis)
+        compiler_params=pltpu.CompilerParams(vmem_limit_bytes=4 * 1024 * 1024),
+    )(live, corner, cell, angles, raw)
 
 
 def spectra_kernel(live, dens, rec, cell, table, sp, dens3, held, onehot, src, sems):
@@ -403,18 +415,18 @@
     lax.fori_loop(0, total, group, 0)
 
 
-def spectra(live, dens, rec, cell, table, rows):
+def spectra(live, dens, rec, cell, table):
+    rows = dens.shape[0]
     slots, bp = cell.shape
     samples = rec.shape[1]
     k2 = table.shape[0]
     vm = pl.BlockSpec(memory_space=pltpu.VMEM)
     return pl.pallas_call(
         spectra_kernel,
-        grid=(1,),
         out_shape=jax.ShapeDtypeStruct((slots, k2, bp), jnp.bfloat16),
         in_specs=[
             pl.BlockSpec(memory_space=pltpu.SMEM),
-            pl.BlockSpec((rows, 128), lambda i: (0, 0)),
+            vm,
             pl.BlockSpec(memory_space=pl.ANY),
             vm,
             vm,
@@ -428,13 +440,13 @@
             pltpu.SemaphoreType.DMA((slots // BATCH,)),
         ],
         name="spectra",
-        compiler_params=pltpu.CompilerParams(vmem_limit_bytes=12 * 1024 * 1024),
+        compiler_params=pltpu.CompilerParams(vmem_limit_bytes=8 * 1024 * 1024),
     )(live, dens, rec, cell, table)
 
 
-def observe_kernel(live, centre, sp, wts, lis, out, prod, acc):
+def observe_kernel(live, centre, sp, wts, lis, out, prod, acc, *, chunk):
     slots, k2, bp = sp.shape
-    tiles = lis.shape[1]
+    tiles = lis.shape[1] // CHUNKS
     half = k2 // 2
     span = tiles * 128
     total = (live[0] + BATCH - 1) // BATCH
@@ -447,13 +459,14 @@
             waves = []
             for j in range(2):
                 b = g * BATCH + pair + j
-                held = wts[pl.ds(pl.multiple_of(b * span, span), span), :]
+                held = wts[pl.ds(pl.multiple_of(chunk * slots * span + b * span, span), span), :]
                 prod[pair + j] = lax.dot_general(sp[b], held, NT, preferred_element_type=jnp.float32)
             for t in range(tiles):
                 state = []
                 for j in range(2):
                     b = g * BATCH + pair + j
-                    away = [jnp.broadcast_to(lis[k, t : t + 1, :], (8, 128)) - centre[k, b] for k in range(3)]
+                    u = chunk * tiles + t
+                    away = [jnp.broadcast_to(lis[k, u : u + 1, :] - centre[k, pl.ds(b, 1), :], (8, 128)) for k in range(3)]
                     reach = jnp.sqrt(away[0] * away[0] + away[1] * away[1] + away[2] * away[2])
                     c, s = sincos_turns(reach * orders)
                     ec = jnp.broadcast_to(c[7:8, :], (8, 128))
@@ -483,22 +496,22 @@
                 out[t * each + e, k, :, :] = turned[e * per : (e + 1) * per, :]
 
 
-def observe(live, centre, sp, wts, lis, shares):
+def observe(chunk, live, centre, sp, wts, lis, shares):
     slots, k2, bp = sp.shape
-    span = lis.shape[1] * 128
+    span = lis.shape[1] * 128 // CHUNKS
     vm = pl.BlockSpec(memory_space=pltpu.VMEM)
     sm = pl.BlockSpec(memory_space=pltpu.SMEM)
     return pl.pallas_call(
-        observe_kernel,
+        functools.partial(observe_kernel, chunk=chunk),
         out_shape=jax.ShapeDtypeStruct((shares, 2, span // shares, k2 // 2), jnp.float32),
-        in_specs=[sm, sm, vm, vm, vm],
+        in_specs=[sm, vm, vm, vm, vm],
         out_specs=vm,
         scratch_shapes=[
             pltpu.VMEM((BATCH, k2, span), jnp.float32),
             pltpu.VMEM((2, k2 // 2, span), jnp.float32),
         ],
         name="observe",
-        compiler_params=pltpu.CompilerParams(vmem_limit_bytes=8 * 1024 * 1024),
+        compiler_params=pltpu.CompilerParams(vmem_limit_bytes=3 * 1024 * 1024),
     )(live, centre, sp, wts, lis)
 
 
@@ -507,24 +520,24 @@
     return lax.ppermute(value, axis, [(i, i ^ bit) for i in range(size)])
 
 
-def reduce_spectra(shares):
-    size = shares.shape[0]
-    here = lax.axis_index("gz")
-    bit = 1
-    while bit < size:
-        pairs = shares.reshape((shares.shape[0] // 2, 2) + shares.shape[1:])
-        up = (here // bit) % 2
-        mine = lax.dynamic_index_in_dim(pairs, up, 1, keepdims=False)
-        theirs = lax.dynamic_index_in_dim(pairs, 1 - up, 1, keepdims=False)
-        shares = mine + swap(theirs, "gz", bit)
-        bit *= 2
-    total = shares[0]
-    for axis in ("gx", "gy"):
+def stages():
+    steps = []
+    for axis in ("gz", "gx", "gy"):
         bit = 1
         while bit < lax.axis_size(axis):
-            total = total + swap(total, axis, bit)
+            steps.append((axis, bit))
             bit *= 2
-    return total
+    return steps
+
+
+def exchange(value, axis, bit):
+    if axis != "gz":
+        return value + swap(value, axis, bit)
+    up = (lax.axis_index("gz") // bit) % 2
+    pairs = value.reshape((value.shape[0] // 2, 2) + value.shape[1:])
+    mine = lax.dynamic_index_in_dim(pairs, up, 1, keepdims=False)
+    theirs = lax.dynamic_index_in_dim(pairs, 1 - up, 1, keepdims=False)
+    return mine + swap(theirs, "gz", bit)
 
 
 def local(
@@ -537,44 +550,35 @@
     listener_angles,
     listener_range,
 ):
-    cells_x, cells_y, cells_z = state_section.shape[1:]
-    counts = (
-        cells_x * lax.axis_size("gx"),
-        cells_y * lax.axis_size("gy"),
-        cells_z * lax.axis_size("gz"),
-    )
+    sizes = state_section.shape[1:]
+    axes = ("gx", "gy", "gz")
+    counts = tuple(n * lax.axis_size(axis) for n, axis in zip(sizes, axes))
     step_size = COURANT / max(counts)
     slot_count, block_rows = panel_cell.shape
     samples = panel_record.shape[1]
     shares = lax.axis_size("gz")
-    places = panel_places(
-        panel_cell,
-        lax.axis_index("gx"),
-        lax.axis_index("gy"),
-        lax.axis_index("gz"),
-        cells_x,
-        cells_y,
-        cells_z,
-        counts,
-    )
-    live = jnp.arange(slot_count, dtype=jnp.int32) < owned_blocks[0]
-    normals = directions(panel_angles.reshape(2, slot_count, block_rows))
-    normals = jnp.where(live[None, :, None], normals * (0.25 / math.pi), 0.0)
-    geometry = jnp.concatenate([jnp.transpose(places, (1, 0, 2)), normals], axis=0)
-    centres = jnp.transpose(jnp.mean(places, axis=2))
-    listeners = 0.5 + listener_range[None, :] * directions(listener_angles)
-    listeners = jnp.transpose(listeners.reshape(3, shares, CHUNKS, -1), (0, 2, 1, 3))
-    listeners = listeners.reshape(3, -1, 128)
-    parts = weights(owned_blocks, geometry, listeners, CHUNKS)
-    updated = flow(state_old, state_section, counts, step_size)
-    heard = spectra(
-        owned_blocks, updated.reshape(-1, cells_z), panel_record, panel_cell, dft_table(samples, FREQS), cells_x * cells_y
-    )
-    tiles = listeners.shape[1] // CHUNKS
+    corner = jnp.stack([lax.axis_index(axis) * n for n, axis in zip(sizes, axes)]).astype(jnp.int32)
+    raw = jnp.concatenate([listener_angles, listener_range[None]], axis=0)
+    raw = jnp.transpose(raw.reshape(3, shares, CHUNKS, -1), (0, 2, 1, 3)).reshape(3, -1, 128)
+    angles = panel_angles.reshape(2, slot_count, block_rows)
+    wts, centres, listeners = weights(owned_blocks, corner, panel_cell, angles, raw, sizes, counts)
+    updated, density = flow(state_old, state_section, counts, step_size)
+    heard = spectra(owned_blocks, density, panel_record, panel_cell, dft_table(samples, FREQS))
+    steps = stages()
     pieces = []
+    live = owned_blocks
     for q in range(CHUNKS):
-        own = listeners[:, q * tiles : (q + 1) * tiles]
-        pieces.append(reduce_spectra(observe(owned_blocks, centres, heard, parts[q], own, shares)))
+        if TIED and q >= 2:
+            pieces = [exchange(v, *steps[n]) if n < len(steps) else v for v, n in zip(pieces, range(q - 2, -1, -1))] + pieces[q - 1 :]
+            tied = lax.optimization_barrier((live, *pieces[: q - 1]))
+            live, pieces = tied[0], list(tied[1:]) + pieces[q - 1 :]
+        pieces.append(observe(q, live, centres, heard, wts, listeners, shares))
+    for n in range(len(steps) + CHUNKS):
+        for q in range(CHUNKS):
+            done = max(CHUNKS - 2 - q, 0) if TIED else 0
+            if done + n < len(steps):
+                pieces[q] = exchange(pieces[q], *steps[done + n])
+    pieces = [v.reshape((2, -1, FREQS)) for v in pieces]
     return (updated, jnp.concatenate(pieces, axis=1))
 
 

time: 114 us -> 95.8 us (0.84)
  local copies, waits for them, and re-layouts: 11.2 us -> 1.73 us
  starting transfers between devices: 50.5 us -> 57 us
  Pallas kernels: 32.7 us -> 26.3 us
  waiting for transfers between devices: 12.4 us -> 8.19 us
  other arithmetic: 4.71 us -> 1.02 us
    ppermute x20 -> x21, starting transfers between devices: 41.6 us -> 51.4 us  [swap(): return lax.ppermute(value, axis, [(i, i ^ bit) for i in range(size)])]
    unnamed x38 -> x19, local copies, waits for them, and re-layouts: 9.37 us -> 1.36 us
    pallas_call x9, Pallas kernels: 31.4 us -> 25.7 us  [the longest x3 20 us: line_call(): pl.pallas_call(kernel, out_shape=[jax.ShapeDtypeStruct(shape, jnp.float32...]
    ppermute x20 -> x21, waiting for transfers between devices: 12.4 us -> 8.18 us  [swap(): return lax.ppermute(value, axis, [(i, i ^ bit) for i in range(size)])]
    ppermute x6 -> x4, starting transfers between devices: 8.9 us -> 5.57 us  [neighbours(): return (lax.ppermute(last, axis, up), lax.ppermute(first, axis, down))]
    mul x2 -> x0, other arithmetic: 2.81 us -> none  [directions(): jnp.cos(polar_angle) * jnp.cos(azimuth)]
  transfers between devices with their start and end apart: 26 -> 25, of which waited for: 11 -> 10; matrix products, arithmetic and copies ran while one was open for 5% -> 1% of each run, Pallas kernels for 18% -> 16%
where the time goes in v4:
time: 95.8 us
  starting transfers between devices  57 us (59%)
  Pallas kernels  26.3 us (27%)
  waiting for transfers between devices  8.19 us (9%)
  local copies, waits for them, and re-layouts  1.73 us (2%)
  between operations  1.67 us (2%)
  other arithmetic  1.02 us (1%)
    ppermute x21, starting transfers between devices, swap(): return lax.ppermute(value, axis, [(i, i ^ bit) for i in range(size)])  51.4 us
    pallas_call x3, Pallas kernels, line_call(): pl.pallas_call(kernel, out_shape=[jax.ShapeDtypeStruct(shape, jnp.float32...  20 us
    ppermute x21, waiting for transfers between devices, swap(): return lax.ppermute(value, axis, [(i, i ^ bit) for i in range(size)])  8.18 us
    ppermute x4, starting transfers between devices, neighbours(): return (lax.ppermute(last, axis, up), lax.ppermute(first, axis, down))  5.57 us
    pallas_call x4, Pallas kernels, observe(): pl.pallas_call(functools.partial(observe_kernel, chunk=chunk), out_shape=...  2.23 us
    pallas_call x1, Pallas kernels, weights(): pl.pallas_call(functools.partial(weights_kernel, sizes=sizes, counts=coun...  2.14 us
  transfers between devices with their start and end apart: 25, of which 10 were waited for; matrix products, arithmetic and copies ran while one was open for 1% of the time, Pallas kernels for 16%

profile of v4, /device:TPU:0, one launch (start us, length us, event | category | flops | bytes accessed | tf_op | source)
XLA Modules:
  0.0 95.8 jit_solution(7406189708923158295)
XLA Ops:
  0.6 1.3 %copy-done = f32[5,16,32,128]{3,2,1,0:T(8,128)S(1)} copy-done((f32[5,16,32,128]{3,2,1,0:T(8,128)S(1)}, f32[5,16,32,128]{3,2,1,0:T(8,128)}, u32[]{:S(2)}) %copy-start) | copy-done | bytes 1310744
  2.5 3.0 %collective-permute-start = (f32[960,128]{1,0:T(8,128)S(1)}, f32[960,128]{1,0:T(8,128)S(1)}, u32[]{:S(2)}, u32[]{:S(2)}) collective-permute-start(f32[960,128]{1,0:T(8,128)S(1)} %get-tuple-element.18), channel_id=1, source_target_pairs={{0,16},{16,0},{1,17},{17,1},{2,18},{18,2},{3,19},{19,3},{4,20},{20... | collective-permute-start | bytes 1474568 | tf_op jit(solution)/shard_map/ppermute | solution.py:520
  5.5 1.7 %collective-permute-start.4 = (f32[60,128]{1,0:T(8,128)S(1)}, f32[60,128]{1,0:T(8,128)S(1)}, u32[]{:S(2)}, u32[]{:S(2)}) collective-permute-start(f32[60,128]{1,0:T(8,128)S(1)} %get-tuple-element.23), channel_id=1, source_target_pairs={{1,0},{2,1},{3,2},{0,3},{5,4},{6,5},{7,6},{4,7},{9,8},{10,9},{11,1... | collective-permute-start | bytes 92168 | tf_op jit(solution)/shard_map/ppermute | solution.py:231
  7.3 1.6 %collective-permute-start.1 = (f32[240,128]{1,0:T(8,128)S(1)}, f32[240,128]{1,0:T(8,128)S(1)}, u32[]{:S(2)}, u32[]{:S(2)}) collective-permute-start(f32[240,128]{1,0:T(8,128)S(1)} %get-tuple-element.19), channel_id=1, source_target_pairs={{0,4},{4,8},{8,12},{12,0},{1,5},{5,9},{9,13},{13,1},{2,6},{6,10},{... | collective-permute-start | bytes 368648 | tf_op jit(solution)/shard_map/ppermute | solution.py:231
  8.8 2.2 %collective-permute-start.2 = (f32[240,128]{1,0:T(8,128)S(1)}, f32[240,128]{1,0:T(8,128)S(1)}, u32[]{:S(2)}, u32[]{:S(2)}) collective-permute-start(f32[240,128]{1,0:T(8,128)S(1)} %get-tuple-element.20), channel_id=1, source_target_pairs={{4,0},{8,4},{12,8},{0,12},{5,1},{9,5},{13,9},{1,13},{6,2},{10,6},{... | collective-permute-start | bytes 368648 | tf_op jit(solution)/shard_map/ppermute | solution.py:231
  12.1 2.1 %weights.1 = (bf16[32768,128]{1,0:T(8,128)(2,1)S(1)}, f32[3,32,128]{2,1,0:T(8,128)S(1)}, f32[3,8,128]{2,1,0:T(8,128)S(1)}) custom-call(s32[1]{0:T(128)S(6)} %copy.17.live, s32[3]{0:T(128)S(1)} %pad_add_fusion.corner, s32[32,128]{1,0:T(8,128)S(1)} %copy-done.5, f32[2,32,128]{2,1,0:T(8,128)S(1)} %bitcast.52, f32[3,8,128]{2,1,0:T(8,128)S(1)} %reshape.71.raw), custom_call_target="tpu_custom_call" | custom-call | tf_op jit(solution)/shard_map/weights/pallas_call | solution.py:345
  14.3 6.4 %along_z.1.start = f32[2560,128]{1,0:T(8,128)S(1)} custom-call(f32[2560,128]{1,0:T(8,128)S(1)} %get-tuple-element.21.turned, f32[60,128]{1,0:T(8,128)S(1)} %collective-permute-done.3.left, f32[60,128]{1,0:T(8,128)S(1)} %collective-permute-done.4.right), custom_call_target="tpu_custom_call" | custom-call | tf_op jit(solution)/shard_map/along_z/pallas_call | solution.py:210
  20.8 6.5 %along_y.1.start = f32[2560,128]{1,0:T(8,128)S(1)} custom-call(f32[2560,128]{1,0:T(8,128)S(1)} %bitcast.41, f32[240,128]{1,0:T(8,128)S(1)} %collective-permute-done.1.left, f32[240,128]{1,0:T(8,128)S(1)} %collective-permute-done.2.right, f32[2560,128]{1,0:T(8,128)S(1)} %along_z.1.start), custom_call_target="tpu_custom_call" | custom-call | tf_op jit(solution)/shard_map/along_y/pallas_call | solution.py:210
  27.4 7.1 %along_x.1 = (f32[2560,128]{1,0:T(8,128)}, f32[512,128]{1,0:T(8,128)S(1)}) custom-call(f32[2560,128]{1,0:T(8,128)S(1)} %bitcast.42, f32[960,128]{1,0:T(8,128)S(1)} %collective-permute-done.ends, f32[2560,128]{1,0:T(8,128)S(1)} %along_y.1.start, f32[2560,128]{1,0:T(8,128)S(1)} %bitcast.43), custom_call_target="tpu_custom_call" | custom-call | tf_op jit(solution)/shard_map/along_x/pallas_call | solution.py:210
  34.5 1.3 %spectra.1.sp = bf16[32,256,128]{2,1,0:T(8,128)(2,1)S(1)} custom-call(s32[1]{0:T(128)S(6)} %copy.17.live, f32[512,128]{1,0:T(8,128)S(1)} %get-tuple-element.26.dens, bf16[4096,512]{1,0:T(8,128)(2,1)S(1)} %copy-done.2, s32[32,128]{1,0:T(8,128)S(1)} %copy-done.5, bf16[256,512]{1,0:T(8,128)(2,1)S(1)} %copy-done.4), custom_call_target="tpu_custom_call" | custom-call | tf_op jit(solution)/shard_map/spectra/pallas_call | solution.py:424
  39.5 1.6 %collective-permute-start.21 = (f32[1,2,64,128]{3,2,1,0:T(8,128)S(1)}, f32[1,2,64,128]{3,2,1,0:T(8,128)S(1)}, u32[]{:S(2)}, u32[]{:S(2)}) collective-permute-start(f32[1,2,64,128]{3,2,1,0:T(8,128)S(1)} %constant_dynamic-slice_fusion), channel_id=1, source_target_pairs={{0,2},{1,3},{2,0},{3,1},{4,6},{5,7},{6,4},{7,5},{8,10},{9,11},{10,... | collective-permute-start | bytes 196616 | tf_op jit(solution)/shard_map/ppermute | solution.py:520
  41.8 1.6 %collective-permute-start.6 = (f32[1,2,64,128]{3,2,1,0:T(8,128)S(1)}, f32[1,2,64,128]{3,2,1,0:T(8,128)S(1)}, u32[]{:S(2)}, u32[]{:S(2)}) collective-permute-start(f32[1,2,64,128]{3,2,1,0:T(8,128)S(1)} %constant_dynamic-slice_fusion.3), channel_id=1, source_target_pairs={{0,2},{1,3},{2,0},{3,1},{4,6},{5,7},{6,4},{7,5},{8,10},{9,11},{10,... | collective-permute-start | bytes 196616 | tf_op jit(solution)/shard_map/ppermute | solution.py:520
  44.1 27.5 %collective-permute-start.22 = (f32[1,2,64,128]{3,2,1,0:T(8,128)S(1)}, f32[1,2,64,128]{3,2,1,0:T(8,128)S(1)}, u32[]{:S(2)}, u32[]{:S(2)}) collective-permute-start(f32[1,2,64,128]{3,2,1,0:T(8,128)S(1)} %dynamic-slice_add_fusion), channel_id=1, source_target_pairs={{0,16},{16,0},{1,17},{17,1},{2,18},{18,2},{3,19},{19,3},{4,20},{20... | collective-permute-start | bytes 196616 | tf_op jit(solution)/shard_map/ppermute | solution.py:520
  71.6 2.5 %collective-permute-start.11 = (f32[1,2,64,128]{3,2,1,0:T(8,128)S(1)}, f32[1,2,64,128]{3,2,1,0:T(8,128)S(1)}, u32[]{:S(2)}, u32[]{:S(2)}) collective-permute-start(f32[1,2,64,128]{3,2,1,0:T(8,128)S(1)} %constant_dynamic-slice_fusion.2), channel_id=1, source_target_pairs={{0,2},{1,3},{2,0},{3,1},{4,6},{5,7},{6,4},{7,5},{8,10},{9,11},{10,... | collective-permute-start | bytes 196616 | tf_op jit(solution)/shard_map/ppermute | solution.py:520
  74.1 2.0 %collective-permute-start.17 = (f32[1,2,64,128]{3,2,1,0:T(8,128)S(1)}, f32[1,2,64,128]{3,2,1,0:T(8,128)S(1)}, u32[]{:S(2)}, u32[]{:S(2)}) collective-permute-start(f32[1,2,64,128]{3,2,1,0:T(8,128)S(1)} %dynamic-slice_add_fusion.1), channel_id=1, source_target_pairs={{0,16},{16,0},{1,17},{17,1},{2,18},{18,2},{3,19},{19,3},{4,20},{20... | collective-permute-start | bytes 196616 | tf_op jit(solution)/shard_map/ppermute | solution.py:520
  76.4 2.4 %collective-permute-start.12 = (f32[1,2,64,128]{3,2,1,0:T(8,128)S(1)}, f32[1,2,64,128]{3,2,1,0:T(8,128)S(1)}, u32[]{:S(2)}, u32[]{:S(2)}) collective-permute-start(f32[1,2,64,128]{3,2,1,0:T(8,128)S(1)} %dynamic-slice_add_fusion.2), channel_id=1, source_target_pairs={{0,16},{16,0},{1,17},{17,1},{2,18},{18,2},{3,19},{19,3},{4,20},{20... | collective-permute-start | bytes 196616 | tf_op jit(solution)/shard_map/ppermute | solution.py:520
  79.2 1.8 %collective-permute-start.18 = (f32[1,2,64,128]{3,2,1,0:T(8,128)S(1)}, f32[1,2,64,128]{3,2,1,0:T(8,128)S(1)}, u32[]{:S(2)}, u32[]{:S(2)}) collective-permute-start(f32[1,2,64,128]{3,2,1,0:T(8,128)S(1)} %add.121), channel_id=1, source_target_pairs={{0,4},{4,0},{8,12},{12,8},{1,5},{5,1},{9,13},{13,9},{2,6},{6,2},{1... | collective-permute-start | bytes 196616 | tf_op jit(solution)/shard_map/ppermute | solution.py:520
  81.4 1.8 %collective-permute-start.13 = (f32[1,2,64,128]{3,2,1,0:T(8,128)S(1)}, f32[1,2,64,128]{3,2,1,0:T(8,128)S(1)}, u32[]{:S(2)}, u32[]{:S(2)}) collective-permute-start(f32[1,2,64,128]{3,2,1,0:T(8,128)S(1)} %add.116), channel_id=1, source_target_pairs={{0,4},{4,0},{8,12},{12,8},{1,5},{5,1},{9,13},{13,9},{2,6},{6,2},{1... | collective-permute-start | bytes 196616 | tf_op jit(solution)/shard_map/ppermute | solution.py:520
  83.5 1.3 %collective-permute-done.18 = f32[1,2,64,128]{3,2,1,0:T(8,128)S(1)} collective-permute-done((f32[1,2,64,128]{3,2,1,0:T(8,128)S(1)}, f32[1,2,64,128]{3,2,1,0:T(8,128)S(1)}, u32[]{:S(2)}, u32[]{:S(2)}) %collective-permute-start.18) | collective-permute-done | bytes 65568 | tf_op jit(solution)/shard_map/ppermute | solution.py:520
  84.8 1.7 %collective-permute-start.19 = (f32[1,2,64,128]{3,2,1,0:T(8,128)S(1)}, f32[1,2,64,128]{3,2,1,0:T(8,128)S(1)}, u32[]{:S(2)}, u32[]{:S(2)}) collective-permute-start(f32[1,2,64,128]{3,2,1,0:T(8,128)S(1)} %add.122), channel_id=1, source_target_pairs={{0,8},{4,12},{8,0},{12,4},{1,9},{5,13},{9,1},{13,5},{2,10},{6,14},... | collective-permute-start | bytes 196616 | tf_op jit(solution)/shard_map/ppermute | solution.py:520
  86.5 1.4 %collective-permute-start.10 = (f32[1,2,64,128]{3,2,1,0:T(8,128)S(1)}, f32[1,2,64,128]{3,2,1,0:T(8,128)S(1)}, u32[]{:S(2)}, u32[]{:S(2)}) collective-permute-start(f32[1,2,64,128]{3,2,1,0:T(8,128)S(1)} %add.113), channel_id=1, source_target_pairs={{0,8},{4,12},{8,0},{12,4},{1,9},{5,13},{9,1},{13,5},{2,10},{6,14},... | collective-permute-start | bytes 196616 | tf_op jit(solution)/shard_map/ppermute | solution.py:520
  87.9 1.7 %collective-permute-start.14 = (f32[1,2,64,128]{3,2,1,0:T(8,128)S(1)}, f32[1,2,64,128]{3,2,1,0:T(8,128)S(1)}, u32[]{:S(2)}, u32[]{:S(2)}) collective-permute-start(f32[1,2,64,128]{3,2,1,0:T(8,128)S(1)} %add.117), channel_id=1, source_target_pairs={{0,8},{4,12},{8,0},{12,4},{1,9},{5,13},{9,1},{13,5},{2,10},{6,14},... | collective-permute-start | bytes 196616 | tf_op jit(solution)/shard_map/ppermute | solution.py:520
  89.6 2.4 %collective-permute-done.24 = f32[1,2,64,128]{3,2,1,0:T(8,128)S(1)} collective-permute-done((f32[1,2,64,128]{3,2,1,0:T(8,128)S(1)}, f32[1,2,64,128]{3,2,1,0:T(8,128)S(1)}, u32[]{:S(2)}, u32[]{:S(2)}) %collective-permute-start.24) | collective-permute-done | bytes 65568 | tf_op jit(solution)/shard_map/ppermute | solution.py:520
  92.0 1.7 %collective-permute-done.19 = f32[1,2,64,128]{3,2,1,0:T(8,128)S(1)} collective-permute-done((f32[1,2,64,128]{3,2,1,0:T(8,128)S(1)}, f32[1,2,64,128]{3,2,1,0:T(8,128)S(1)}, u32[]{:S(2)}, u32[]{:S(2)}) %collective-permute-start.19) | collective-permute-done | bytes 65568 | tf_op jit(solution)/shard_map/ppermute | solution.py:520
  (91 shorter events, 9.4 us)
Async XLA Ops:
  2.5 24.9 %collective-permute-start = (f32[960,128]{1,0:T(8,128)S(1)}, f32[960,128]{1,0:T(8,128)S(1)}, u32[]{:S(2)}, u32[]{:S(2)}) collective-permute-start(f32[960,128]{1,0:T(8,128)S(1)} %get-tuple-element.18), channel_id=1, source_target_pairs={{0,16},{16,0},{1,17},{17,1},{2,18},{18,2},{3,19},{19,3},{4,20},{20... | collective-permute-start | bytes 1474568 | tf_op jit(solution)/shard_map/ppermute | solution.py:520
  5.5 8.8 %collective-permute-start.3 = (f32[60,128]{1,0:T(8,128)S(1)}, f32[60,128]{1,0:T(8,128)S(1)}, u32[]{:S(2)}, u32[]{:S(2)}) collective-permute-start(f32[60,128]{1,0:T(8,128)S(1)} %get-tuple-element.22), channel_id=1, source_target_pairs={{0,1},{1,2},{2,3},{3,0},{4,5},{5,6},{6,7},{7,4},{8,9},{9,10},{10,1... | collective-permute-start | bytes 92168 | tf_op jit(solution)/shard_map/ppermute | solution.py:231
  5.5 8.8 %collective-permute-start.4 = (f32[60,128]{1,0:T(8,128)S(1)}, f32[60,128]{1,0:T(8,128)S(1)}, u32[]{:S(2)}, u32[]{:S(2)}) collective-permute-start(f32[60,128]{1,0:T(8,128)S(1)} %get-tuple-element.23), channel_id=1, source_target_pairs={{1,0},{2,1},{3,2},{0,3},{5,4},{6,5},{7,6},{4,7},{9,8},{10,9},{11,1... | collective-permute-start | bytes 92168 | tf_op jit(solution)/shard_map/ppermute | solution.py:231
  7.3 13.5 %collective-permute-start.1 = (f32[240,128]{1,0:T(8,128)S(1)}, f32[240,128]{1,0:T(8,128)S(1)}, u32[]{:S(2)}, u32[]{:S(2)}) collective-permute-start(f32[240,128]{1,0:T(8,128)S(1)} %get-tuple-element.19), channel_id=1, source_target_pairs={{0,4},{4,8},{8,12},{12,0},{1,5},{5,9},{9,13},{13,1},{2,6},{6,10},{... | collective-permute-start | bytes 368648 | tf_op jit(solution)/shard_map/ppermute | solution.py:231
  8.8 11.9 %collective-permute-start.2 = (f32[240,128]{1,0:T(8,128)S(1)}, f32[240,128]{1,0:T(8,128)S(1)}, u32[]{:S(2)}, u32[]{:S(2)}) collective-permute-start(f32[240,128]{1,0:T(8,128)S(1)} %get-tuple-element.20), channel_id=1, source_target_pairs={{4,0},{8,4},{12,8},{0,12},{5,1},{9,5},{13,9},{1,13},{6,2},{10,6},{... | collective-permute-start | bytes 368648 | tf_op jit(solution)/shard_map/ppermute | solution.py:231
  38.2 2.9 %collective-permute-start.15 = (f32[2,2,64,128]{3,2,1,0:T(8,128)S(1)}, f32[2,2,64,128]{3,2,1,0:T(8,128)S(1)}, u32[]{:S(2)}, u32[]{:S(2)}) collective-permute-start(f32[2,2,64,128]{3,2,1,0:T(8,128)S(1)} %dynamic-slice_bitcast_fusion.1), channel_id=1, source_target_pairs={{0,1},{1,0},{2,3},{3,2},{4,5},{5,4},{6,7},{7,6},{8,9},{9,8},{10,11... | collective-permute-start | bytes 393224 | tf_op jit(solution)/shard_map/ppermute | solution.py:520
  38.8 3.0 %collective-permute-start.5 = (f32[2,2,64,128]{3,2,1,0:T(8,128)S(1)}, f32[2,2,64,128]{3,2,1,0:T(8,128)S(1)}, u32[]{:S(2)}, u32[]{:S(2)}) collective-permute-start(f32[2,2,64,128]{3,2,1,0:T(8,128)S(1)} %dynamic-slice_bitcast_fusion.3), channel_id=1, source_target_pairs={{0,1},{1,0},{2,3},{3,2},{4,5},{5,4},{6,7},{7,6},{8,9},{9,8},{10,11... | collective-permute-start | bytes 393224 | tf_op jit(solution)/shard_map/ppermute | solution.py:520
  38.9 4.5 %collective-permute-start.7 = (f32[2,2,64,128]{3,2,1,0:T(8,128)S(1)}, f32[2,2,64,128]{3,2,1,0:T(8,128)S(1)}, u32[]{:S(2)}, u32[]{:S(2)}) collective-permute-start(f32[2,2,64,128]{3,2,1,0:T(8,128)S(1)} %dynamic-slice_bitcast_fusion.2), channel_id=1, source_target_pairs={{0,1},{1,0},{2,3},{3,2},{4,5},{5,4},{6,7},{7,6},{8,9},{9,8},{10,11... | collective-permute-start | bytes 393224 | tf_op jit(solution)/shard_map/ppermute | solution.py:520
  39.5 4.5 %collective-permute-start.21 = (f32[1,2,64,128]{3,2,1,0:T(8,128)S(1)}, f32[1,2,64,128]{3,2,1,0:T(8,128)S(1)}, u32[]{:S(2)}, u32[]{:S(2)}) collective-permute-start(f32[1,2,64,128]{3,2,1,0:T(8,128)S(1)} %constant_dynamic-slice_fusion), channel_id=1, source_target_pairs={{0,2},{1,3},{2,0},{3,1},{4,6},{5,7},{6,4},{7,5},{8,10},{9,11},{10,... | collective-permute-start | bytes 196616 | tf_op jit(solution)/shard_map/ppermute | solution.py:520
  41.2 32.9 %collective-permute-start.16 = (f32[1,2,64,128]{3,2,1,0:T(8,128)S(1)}, f32[1,2,64,128]{3,2,1,0:T(8,128)S(1)}, u32[]{:S(2)}, u32[]{:S(2)}) collective-permute-start(f32[1,2,64,128]{3,2,1,0:T(8,128)S(1)} %constant_dynamic-slice_fusion.1), channel_id=1, source_target_pairs={{0,2},{1,3},{2,0},{3,1},{4,6},{5,7},{6,4},{7,5},{8,10},{9,11},{10,... | collective-permute-start | bytes 196616 | tf_op jit(solution)/shard_map/ppermute | solution.py:520
  41.8 29.7 %collective-permute-start.6 = (f32[1,2,64,128]{3,2,1,0:T(8,128)S(1)}, f32[1,2,64,128]{3,2,1,0:T(8,128)S(1)}, u32[]{:S(2)}, u32[]{:S(2)}) collective-permute-start(f32[1,2,64,128]{3,2,1,0:T(8,128)S(1)} %constant_dynamic-slice_fusion.3), channel_id=1, source_target_pairs={{0,2},{1,3},{2,0},{3,1},{4,6},{5,7},{6,4},{7,5},{8,10},{9,11},{10,... | collective-permute-start | bytes 196616 | tf_op jit(solution)/shard_map/ppermute | solution.py:520
  44.1 34.7 %collective-permute-start.22 = (f32[1,2,64,128]{3,2,1,0:T(8,128)S(1)}, f32[1,2,64,128]{3,2,1,0:T(8,128)S(1)}, u32[]{:S(2)}, u32[]{:S(2)}) collective-permute-start(f32[1,2,64,128]{3,2,1,0:T(8,128)S(1)} %dynamic-slice_add_fusion), channel_id=1, source_target_pairs={{0,16},{16,0},{1,17},{17,1},{2,18},{18,2},{3,19},{19,3},{4,20},{20... | collective-permute-start | bytes 196616 | tf_op jit(solution)/shard_map/ppermute | solution.py:520
  71.6 4.8 %collective-permute-start.11 = (f32[1,2,64,128]{3,2,1,0:T(8,128)S(1)}, f32[1,2,64,128]{3,2,1,0:T(8,128)S(1)}, u32[]{:S(2)}, u32[]{:S(2)}) collective-permute-start(f32[1,2,64,128]{3,2,1,0:T(8,128)S(1)} %constant_dynamic-slice_fusion.2), channel_id=1, source_target_pairs={{0,2},{1,3},{2,0},{3,1},{4,6},{5,7},{6,4},{7,5},{8,10},{9,11},{10,... | collective-permute-start | bytes 196616 | tf_op jit(solution)/shard_map/ppermute | solution.py:520
  74.1 5.0 %collective-permute-start.17 = (f32[1,2,64,128]{3,2,1,0:T(8,128)S(1)}, f32[1,2,64,128]{3,2,1,0:T(8,128)S(1)}, u32[]{:S(2)}, u32[]{:S(2)}) collective-permute-start(f32[1,2,64,128]{3,2,1,0:T(8,128)S(1)} %dynamic-slice_add_fusion.1), channel_id=1, source_target_pairs={{0,16},{16,0},{1,17},{17,1},{2,18},{18,2},{3,19},{19,3},{4,20},{20... | collective-permute-start | bytes 196616 | tf_op jit(solution)/shard_map/ppermute | solution.py:520
  76.1 4.9 %collective-permute-start.8 = (f32[1,2,64,128]{3,2,1,0:T(8,128)S(1)}, f32[1,2,64,128]{3,2,1,0:T(8,128)S(1)}, u32[]{:S(2)}, u32[]{:S(2)}) collective-permute-start(f32[1,2,64,128]{3,2,1,0:T(8,128)S(1)} %dynamic-slice_add_fusion.3), channel_id=1, source_target_pairs={{0,16},{16,0},{1,17},{17,1},{2,18},{18,2},{3,19},{19,3},{4,20},{20... | collective-permute-start | bytes 196616 | tf_op jit(solution)/shard_map/ppermute | solution.py:520
  76.4 5.0 %collective-permute-start.12 = (f32[1,2,64,128]{3,2,1,0:T(8,128)S(1)}, f32[1,2,64,128]{3,2,1,0:T(8,128)S(1)}, u32[]{:S(2)}, u32[]{:S(2)}) collective-permute-start(f32[1,2,64,128]{3,2,1,0:T(8,128)S(1)} %dynamic-slice_add_fusion.2), channel_id=1, source_target_pairs={{0,16},{16,0},{1,17},{17,1},{2,18},{18,2},{3,19},{19,3},{4,20},{20... | collective-permute-start | bytes 196616 | tf_op jit(solution)/shard_map/ppermute | solution.py:520
  78.8 4.6 %collective-permute-start.23 = (f32[1,2,64,128]{3,2,1,0:T(8,128)S(1)}, f32[1,2,64,128]{3,2,1,0:T(8,128)S(1)}, u32[]{:S(2)}, u32[]{:S(2)}) collective-permute-start(f32[1,2,64,128]{3,2,1,0:T(8,128)S(1)} %add.126), channel_id=1, source_target_pairs={{0,4},{4,0},{8,12},{12,8},{1,5},{5,1},{9,13},{13,9},{2,6},{6,2},{1... | collective-permute-start | bytes 196616 | tf_op jit(solution)/shard_map/ppermute | solution.py:520
  79.2 5.7 %collective-permute-start.18 = (f32[1,2,64,128]{3,2,1,0:T(8,128)S(1)}, f32[1,2,64,128]{3,2,1,0:T(8,128)S(1)}, u32[]{:S(2)}, u32[]{:S(2)}) collective-permute-start(f32[1,2,64,128]{3,2,1,0:T(8,128)S(1)} %add.121), channel_id=1, source_target_pairs={{0,4},{4,0},{8,12},{12,8},{1,5},{5,1},{9,13},{13,9},{2,6},{6,2},{1... | collective-permute-start | bytes 196616 | tf_op jit(solution)/shard_map/ppermute | solution.py:520
  81.0 5.5 %collective-permute-start.9 = (f32[1,2,64,128]{3,2,1,0:T(8,128)S(1)}, f32[1,2,64,128]{3,2,1,0:T(8,128)S(1)}, u32[]{:S(2)}, u32[]{:S(2)}) collective-permute-start(f32[1,2,64,128]{3,2,1,0:T(8,128)S(1)} %add.112), channel_id=1, source_target_pairs={{0,4},{4,0},{8,12},{12,8},{1,5},{5,1},{9,13},{13,9},{2,6},{6,2},{1... | collective-permute-start | bytes 196616 | tf_op jit(solution)/shard_map/ppermute | solution.py:520
  81.4 6.5 %collective-permute-start.13 = (f32[1,2,64,128]{3,2,1,0:T(8,128)S(1)}, f32[1,2,64,128]{3,2,1,0:T(8,128)S(1)}, u32[]{:S(2)}, u32[]{:S(2)}) collective-permute-start(f32[1,2,64,128]{3,2,1,0:T(8,128)S(1)} %add.116), channel_id=1, source_target_pairs={{0,4},{4,0},{8,12},{12,8},{1,5},{5,1},{9,13},{13,9},{2,6},{6,2},{1... | collective-permute-start | bytes 196616 | tf_op jit(solution)/shard_map/ppermute | solution.py:520
  83.4 8.5 %collective-permute-start.24 = (f32[1,2,64,128]{3,2,1,0:T(8,128)S(1)}, f32[1,2,64,128]{3,2,1,0:T(8,128)S(1)}, u32[]{:S(2)}, u32[]{:S(2)}) collective-permute-start(f32[1,2,64,128]{3,2,1,0:T(8,128)S(1)} %add.127), channel_id=1, source_target_pairs={{0,8},{4,12},{8,0},{12,4},{1,9},{5,13},{9,1},{13,5},{2,10},{6,14},... | collective-permute-start | bytes 196616 | tf_op jit(solution)/shard_map/ppermute | solution.py:520
  84.8 8.9 %collective-permute-start.19 = (f32[1,2,64,128]{3,2,1,0:T(8,128)S(1)}, f32[1,2,64,128]{3,2,1,0:T(8,128)S(1)}, u32[]{:S(2)}, u32[]{:S(2)}) collective-permute-start(f32[1,2,64,128]{3,2,1,0:T(8,128)S(1)} %add.122), channel_id=1, source_target_pairs={{0,8},{4,12},{8,0},{12,4},{1,9},{5,13},{9,1},{13,5},{2,10},{6,14},... | collective-permute-start | bytes 196616 | tf_op jit(solution)/shard_map/ppermute | solution.py:520
  86.5 7.9 %collective-permute-start.10 = (f32[1,2,64,128]{3,2,1,0:T(8,128)S(1)}, f32[1,2,64,128]{3,2,1,0:T(8,128)S(1)}, u32[]{:S(2)}, u32[]{:S(2)}) collective-permute-start(f32[1,2,64,128]{3,2,1,0:T(8,128)S(1)} %add.113), channel_id=1, source_target_pairs={{0,8},{4,12},{8,0},{12,4},{1,9},{5,13},{9,1},{13,5},{2,10},{6,14},... | collective-permute-start | bytes 196616 | tf_op jit(solution)/shard_map/ppermute | solution.py:520
  87.9 7.2 %collective-permute-start.14 = (f32[1,2,64,128]{3,2,1,0:T(8,128)S(1)}, f32[1,2,64,128]{3,2,1,0:T(8,128)S(1)}, u32[]{:S(2)}, u32[]{:S(2)}) collective-permute-start(f32[1,2,64,128]{3,2,1,0:T(8,128)S(1)} %add.117), channel_id=1, source_target_pairs={{0,8},{4,12},{8,0},{12,4},{1,9},{5,13},{9,1},{13,5},{2,10},{6,14},... | collective-permute-start | bytes 196616 | tf_op jit(solution)/shard_map/ppermute | solution.py:520
  (10 other events, 75.3 us)

commit v5 on v4

--- a/solution.py
+++ b/solution.py
@@ -11,8 +11,8 @@
 
 FREQS = 128
 BATCH = 4
-CHUNKS = 4
-TIED = True
+CHUNKS = 2
+PARTS = 3
 NT = (((1,), (1,)), ((), ()))
 
 
@@ -357,21 +357,11 @@
     )(live, corner, cell, angles, raw)
 
 
-def spectra_kernel(live, dens, rec, cell, table, sp, dens3, held, onehot, src, sems):
+def spectra_kernel(live, dens, rec, cell, table, sp, dens3, onehot, src):
     slots, bp = cell.shape
     rows = dens.shape[0] // 2
-    groups = slots // BATCH
     total = (live[0] + BATCH - 1) // BATCH
     span = BATCH * bp
-
-    def fetch(g):
-        at = pl.ds(pl.multiple_of(g * span, span), span)
-        return pltpu.make_async_copy(rec.at[at, :], held.at[at, :], sems.at[g])
-
-    for g in range(groups):
-        @pl.when(g < total)
-        def _():
-            fetch(g).start()
 
     for h in range(2):
         d = dens[pl.ds(h, rows, stride=2), :]
@@ -398,12 +388,11 @@
         picked = jnp.dot(hot, dens3[0], preferred_element_type=jnp.float32)
         picked = picked + jnp.dot(hot, dens3[1], preferred_element_type=jnp.float32)
         picked = picked + jnp.dot(hot, dens3[2], preferred_element_type=jnp.float32)
-        fetch(g).wait()
         for j in range(BATCH):
             own = picked[j * bp : (j + 1) * bp, :]
             found = jnp.where(lows[j] == lane, own[:, 0:128], 0.0) + jnp.where(lows[j] == lane + 128.0, own[:, 128:256], 0.0)
             sampled = jnp.sum(found, axis=1, keepdims=True)
-            record = held[pl.ds(pl.multiple_of(g * span + j * bp, bp), bp), :].astype(jnp.float32)
+            record = rec[pl.ds(pl.multiple_of(g * span + j * bp, bp), bp), :].astype(jnp.float32)
             src[j * bp : (j + 1) * bp, :] = (record * sampled).astype(jnp.bfloat16)
         for j in range(0, BATCH, 2):
             both = lax.dot_general(table[...], src[j * bp : (j + 2) * bp, :], NT, preferred_element_type=jnp.float32)
@@ -427,36 +416,40 @@
         in_specs=[
             pl.BlockSpec(memory_space=pltpu.SMEM),
             vm,
-            pl.BlockSpec(memory_space=pl.ANY),
+            vm,
             vm,
             vm,
         ],
         out_specs=vm,
         scratch_shapes=[
             pltpu.VMEM((3, rows // 2, 256), jnp.bfloat16),
-            pltpu.VMEM(rec.shape, jnp.bfloat16),
             pltpu.VMEM((BATCH * bp, rows // 2), jnp.bfloat16),
             pltpu.VMEM((BATCH * bp, samples), jnp.bfloat16),
-            pltpu.SemaphoreType.DMA((slots // BATCH,)),
         ],
         name="spectra",
-        compiler_params=pltpu.CompilerParams(vmem_limit_bytes=8 * 1024 * 1024),
+        compiler_params=pltpu.CompilerParams(vmem_limit_bytes=3 * 1024 * 1024),
     )(live, dens, rec, cell, table)
 
 
-def observe_kernel(live, centre, sp, wts, lis, out, prod, acc, *, chunk):
+def observe_kernel(live, centre, sp, wts, lis, *refs, chunk, part, parts, ties):
     slots, k2, bp = sp.shape
     tiles = lis.shape[1] // CHUNKS
     half = k2 // 2
     span = tiles * 128
+    before, refs = (refs[0], refs[1 + ties :]) if part > 0 else (None, refs[ties:])
+    out, prod, acc = refs if part == parts - 1 else (None, refs[1], refs[0])
     total = (live[0] + BATCH - 1) // BATCH
-    acc[...] = jnp.zeros(acc.shape, jnp.float32)
+    turns = (total - part + parts - 1) // parts
+    if before is None:
+        acc[...] = jnp.zeros(acc.shape, jnp.float32)
+    else:
+        acc[...] = before[...]
     orders = lax.broadcasted_iota(jnp.int32, (8, 128), 0).astype(jnp.float32) + 1.0
     orders = orders * (WAVE_STEP / (2.0 * math.pi))
 
-    def group(g, _):
+    def group(turn, _):
+        g = turn * parts + part
         for pair in range(0, BATCH, 2):
-            waves = []
             for j in range(2):
                 b = g * BATCH + pair + j
                 held = wts[pl.ds(pl.multiple_of(chunk * slots * span + b * span, span), span), :]
@@ -486,7 +479,9 @@
                     acc[1, a * 8 : a * 8 + 8, t * 128 : t * 128 + 128] = im_sum
         return 0
 
-    lax.fori_loop(0, total, group, 0)
+    lax.fori_loop(0, turns, group, 0)
+    if out is None:
+        return
     shares, _, per, _ = out.shape
     each = 128 // per
     for k in range(2):
@@ -496,23 +491,24 @@
                 out[t * each + e, k, :, :] = turned[e * per : (e + 1) * per, :]
 
 
-def observe(chunk, live, centre, sp, wts, lis, shares):
+def observe(chunk, part, parts, live, centre, sp, wts, lis, shares, before=None, ties=()):
     slots, k2, bp = sp.shape
     span = lis.shape[1] * 128 // CHUNKS
     vm = pl.BlockSpec(memory_space=pltpu.VMEM)
     sm = pl.BlockSpec(memory_space=pltpu.SMEM)
+    sums = (2, k2 // 2, span)
+    last = part == parts - 1
+    scratch = [pltpu.VMEM((BATCH, k2, span), jnp.float32)]
     return pl.pallas_call(
-        functools.partial(observe_kernel, chunk=chunk),
-        out_shape=jax.ShapeDtypeStruct((shares, 2, span // shares, k2 // 2), jnp.float32),
-        in_specs=[sm, vm, vm, vm, vm],
+        functools.partial(observe_kernel, chunk=chunk, part=part, parts=parts, ties=len(ties)),
+        out_shape=jax.ShapeDtypeStruct((shares, 2, span // shares, k2 // 2) if last else sums, jnp.float32),
+        in_specs=[sm, vm, vm, vm, vm] + [vm] * (part > 0) + [pl.BlockSpec(memory_space=pl.ANY)] * len(ties),
         out_specs=vm,
-        scratch_shapes=[
-            pltpu.VMEM((BATCH, k2, span), jnp.float32),
-            pltpu.VMEM((2, k2 // 2, span), jnp.float32),
-        ],
+        scratch_shapes=scratch + [pltpu.VMEM(sums, jnp.float32)] * last,
         name="observe",
-        compiler_params=pltpu.CompilerParams(vmem_limit_bytes=3 * 1024 * 1024),
-    )(live, centre, sp, wts, lis)
+        cost_estimate=pl.CostEstimate(flops=4_000_000_000, transcendentals=0, bytes_accessed=1_000_000),
+        compiler_params=pltpu.CompilerParams(vmem_limit_bytes=4 * 1024 * 1024),
+    )(live, centre, sp, wts, lis, *([before] if part > 0 else []), *ties)
 
 
 def swap(value, axis, bit):
@@ -521,23 +517,29 @@
 
 
 def stages():
-    steps = []
-    for axis in ("gz", "gx", "gy"):
-        bit = 1
-        while bit < lax.axis_size(axis):
-            steps.append((axis, bit))
-            bit *= 2
-    return steps
-
-
-def exchange(value, axis, bit):
-    if axis != "gz":
+    def bits(axis):
+        return [1 << k for k in range(lax.axis_size(axis).bit_length() - 1)]
+
+    steps = [("halve", axis, bit) for axis in ("gz", "gx") for bit in bits(axis)]
+    steps += [("sum", "gy", bit) for bit in bits("gy")]
+    return steps + [("gather", "gx", bit) for bit in bits("gx")[::-1]]
+
+
+def exchange(value, kind, axis, bit):
+    if kind == "sum":
         return value + swap(value, axis, bit)
-    up = (lax.axis_index("gz") // bit) % 2
-    pairs = value.reshape((value.shape[0] // 2, 2) + value.shape[1:])
-    mine = lax.dynamic_index_in_dim(pairs, up, 1, keepdims=False)
-    theirs = lax.dynamic_index_in_dim(pairs, 1 - up, 1, keepdims=False)
-    return mine + swap(theirs, "gz", bit)
+    up = (lax.axis_index(axis) // bit) % 2
+    if kind == "gather":
+        theirs = swap(value, axis, bit)
+        first = jnp.where(up == 0, value, theirs)
+        return jnp.concatenate([first, jnp.where(up == 0, theirs, value)], axis=2)
+    if axis == "gz":
+        pairs, dim = value.reshape((value.shape[0] // 2, 2) + value.shape[1:]), 1
+    else:
+        pairs, dim = value.reshape(value.shape[:2] + (2, value.shape[2] // 2) + value.shape[3:]), 2
+    mine = lax.dynamic_index_in_dim(pairs, up, dim, keepdims=False)
+    theirs = lax.dynamic_index_in_dim(pairs, 1 - up, dim, keepdims=False)
+    return mine + swap(theirs, axis, bit)
 
 
 def local(
@@ -565,19 +567,27 @@
     updated, density = flow(state_old, state_section, counts, step_size)
     heard = spectra(owned_blocks, density, panel_record, panel_cell, dft_table(samples, FREQS))
     steps = stages()
-    pieces = []
-    live = owned_blocks
+    known = (owned_blocks, centres, heard, wts, listeners, shares)
+    pieces, done = [], []
     for q in range(CHUNKS):
-        if TIED and q >= 2:
-            pieces = [exchange(v, *steps[n]) if n < len(steps) else v for v, n in zip(pieces, range(q - 2, -1, -1))] + pieces[q - 1 :]
-            tied = lax.optimization_barrier((live, *pieces[: q - 1]))
-            live, pieces = tied[0], list(tied[1:]) + pieces[q - 1 :]
-        pieces.append(observe(q, live, centres, heard, wts, listeners, shares))
-    for n in range(len(steps) + CHUNKS):
-        for q in range(CHUNKS):
-            done = max(CHUNKS - 2 - q, 0) if TIED else 0
-            if done + n < len(steps):
-                pieces[q] = exchange(pieces[q], *steps[done + n])
+        parts = 1 if q == 0 else PARTS
+        sums = None
+        for part in range(parts):
+            ties = []
+            if part > 0:
+                for k in range(len(pieces)):
+                    if done[k] < len(steps):
+                        pieces[k] = exchange(pieces[k], *steps[done[k]])
+                        done[k] += 1
+                        ties.append(pieces[k])
+            sums = observe(q, part, parts, *known, sums, ties)
+        pieces.append(sums)
+        done.append(0)
+    while min(done) < len(steps):
+        for k in range(len(pieces)):
+            if done[k] < len(steps):
+                pieces[k] = exchange(pieces[k], *steps[done[k]])
+                done[k] += 1
     pieces = [v.reshape((2, -1, FREQS)) for v in pieces]
     return (updated, jnp.concatenate(pieces, axis=1))
 

time: 95.8 us -> 90.6 us (0.946); the launches traced: 95.8 us -> 89 us
  starting transfers between devices: 57 us -> 46.1 us
  waiting for transfers between devices: 8.19 us -> 12.7 us
    ppermute x21 -> x13, starting transfers between devices: 51.4 us -> 40.6 us  [swap(): return lax.ppermute(value, axis, [(i, i ^ bit) for i in range(size)])]
    ppermute x21 -> x13, waiting for transfers between devices: 8.18 us -> 12.7 us  [swap(): return lax.ppermute(value, axis, [(i, i ^ bit) for i in range(size)])]
  transfers between devices with their start and end apart: 25 -> 17, of which waited for: 10 -> 9; matrix products, arithmetic and copies ran while one was open for 1% -> 0% of each run, Pallas kernels for 16% -> 18%
where the time goes in v5:
time: 90.6 us; the launch traced here: 89 us
  starting transfers between devices  46.1 us (51%)
  Pallas kernels  26 us (29%)
  waiting for transfers between devices  12.7 us (14%)
  between operations  1.66 us (2%)
  local copies, waits for them, and re-layouts  1.49 us (2%)
  other arithmetic  1 us (1%)
    ppermute x13, starting transfers between devices, swap(): return lax.ppermute(value, axis, [(i, i ^ bit) for i in range(size)])  40.6 us
    pallas_call x3, Pallas kernels, line_call(): pl.pallas_call(kernel, out_shape=[jax.ShapeDtypeStruct(shape, jnp.float32...  20 us
    ppermute x13, waiting for transfers between devices, swap(): return lax.ppermute(value, axis, [(i, i ^ bit) for i in range(size)])  12.7 us
    ppermute x4, starting transfers between devices, neighbours(): return (lax.ppermute(last, axis, up), lax.ppermute(first, axis, down))  5.57 us
    pallas_call x4, Pallas kernels, observe(): pl.pallas_call(functools.partial(observe_kernel, chunk=chunk, part=part,...  2.29 us
    pallas_call x1, Pallas kernels, weights(): pl.pallas_call(functools.partial(weights_kernel, sizes=sizes, counts=coun...  2.14 us
  transfers between devices with their start and end apart: 17, of which 9 were waited for; matrix products, arithmetic and copies ran while one was open for 0% of the time, Pallas kernels for 18%

profile of v5, /device:TPU:0, one launch (start us, length us, event | category | flops | bytes accessed | tf_op | source)
XLA Modules:
  0.0 89.0 jit_solution(9606843240875278148)
XLA Ops:
  0.6 1.3 %copy-done = f32[5,16,32,128]{3,2,1,0:T(8,128)S(1)} copy-done((f32[5,16,32,128]{3,2,1,0:T(8,128)S(1)}, f32[5,16,32,128]{3,2,1,0:T(8,128)}, u32[]{:S(2)}) %copy-start) | copy-done | bytes 1310744
  2.5 3.0 %collective-permute-start = (f32[960,128]{1,0:T(8,128)S(1)}, f32[960,128]{1,0:T(8,128)S(1)}, u32[]{:S(2)}, u32[]{:S(2)}) collective-permute-start(f32[960,128]{1,0:T(8,128)S(1)} %get-tuple-element.13), channel_id=1, source_target_pairs={{0,16},{16,0},{1,17},{17,1},{2,18},{18,2},{3,19},{19,3},{4,20},{20... | collective-permute-start | bytes 1474568 | tf_op jit(solution)/shard_map/ppermute | solution.py:516
  5.5 1.7 %collective-permute-start.4 = (f32[60,128]{1,0:T(8,128)S(1)}, f32[60,128]{1,0:T(8,128)S(1)}, u32[]{:S(2)}, u32[]{:S(2)}) collective-permute-start(f32[60,128]{1,0:T(8,128)S(1)} %get-tuple-element.18), channel_id=1, source_target_pairs={{1,0},{2,1},{3,2},{0,3},{5,4},{6,5},{7,6},{4,7},{9,8},{10,9},{11,1... | collective-permute-start | bytes 92168 | tf_op jit(solution)/shard_map/ppermute | solution.py:231
  7.3 1.6 %collective-permute-start.1 = (f32[240,128]{1,0:T(8,128)S(1)}, f32[240,128]{1,0:T(8,128)S(1)}, u32[]{:S(2)}, u32[]{:S(2)}) collective-permute-start(f32[240,128]{1,0:T(8,128)S(1)} %get-tuple-element.14), channel_id=1, source_target_pairs={{0,4},{4,8},{8,12},{12,0},{1,5},{5,9},{9,13},{13,1},{2,6},{6,10},{... | collective-permute-start | bytes 368648 | tf_op jit(solution)/shard_map/ppermute | solution.py:231
  8.8 2.2 %collective-permute-start.2 = (f32[240,128]{1,0:T(8,128)S(1)}, f32[240,128]{1,0:T(8,128)S(1)}, u32[]{:S(2)}, u32[]{:S(2)}) collective-permute-start(f32[240,128]{1,0:T(8,128)S(1)} %get-tuple-element.15), channel_id=1, source_target_pairs={{4,0},{8,4},{12,8},{0,12},{5,1},{9,5},{13,9},{1,13},{6,2},{10,6},{... | collective-permute-start | bytes 368648 | tf_op jit(solution)/shard_map/ppermute | solution.py:231
  12.0 2.1 %weights.1 = (bf16[32768,128]{1,0:T(8,128)(2,1)S(1)}, f32[3,32,128]{2,1,0:T(8,128)S(1)}, f32[3,8,128]{2,1,0:T(8,128)S(1)}) custom-call(s32[1]{0:T(128)S(6)} %copy.23.live, s32[3]{0:T(128)S(1)} %pad_add_fusion.corner, s32[32,128]{1,0:T(8,128)S(1)} %copy-done.5, f32[2,32,128]{2,1,0:T(8,128)S(1)} %bitcast.52, f32[3,8,128]{2,1,0:T(8,128)S(1)} %bitcast.53), custom_call_target="tpu_custom_call" | custom-call | tf_op jit(solution)/shard_map/weights/pallas_call | solution.py:345
  14.1 6.4 %along_z.1.start = f32[2560,128]{1,0:T(8,128)S(1)} custom-call(f32[2560,128]{1,0:T(8,128)S(1)} %get-tuple-element.16.turned, f32[60,128]{1,0:T(8,128)S(1)} %collective-permute-done.3.left, f32[60,128]{1,0:T(8,128)S(1)} %collective-permute-done.4.right), custom_call_target="tpu_custom_call" | custom-call | tf_op jit(solution)/shard_map/along_z/pallas_call | solution.py:210
  20.6 6.5 %along_y.1.start = f32[2560,128]{1,0:T(8,128)S(1)} custom-call(f32[2560,128]{1,0:T(8,128)S(1)} %bitcast.43, f32[240,128]{1,0:T(8,128)S(1)} %collective-permute-done.1.left, f32[240,128]{1,0:T(8,128)S(1)} %collective-permute-done.2.right, f32[2560,128]{1,0:T(8,128)S(1)} %along_z.1.start), custom_call_target="tpu_custom_call" | custom-call | tf_op jit(solution)/shard_map/along_y/pallas_call | solution.py:210
  27.2 7.1 %along_x.1 = (f32[2560,128]{1,0:T(8,128)}, f32[512,128]{1,0:T(8,128)S(1)}) custom-call(f32[2560,128]{1,0:T(8,128)S(1)} %bitcast.44, f32[960,128]{1,0:T(8,128)S(1)} %collective-permute-done.ends, f32[2560,128]{1,0:T(8,128)S(1)} %along_y.1.start, f32[2560,128]{1,0:T(8,128)S(1)} %bitcast.45), custom_call_target="tpu_custom_call" | custom-call | tf_op jit(solution)/shard_map/along_x/pallas_call | solution.py:210
  34.3 1.1 %spectra.1.sp = bf16[32,256,128]{2,1,0:T(8,128)(2,1)S(1)} custom-call(s32[1]{0:T(128)S(6)} %copy.23.live, f32[512,128]{1,0:T(8,128)S(1)} %get-tuple-element.21.dens, bf16[4096,512]{1,0:T(8,128)(2,1)S(1)} %copy-done.2, s32[32,128]{1,0:T(8,128)S(1)} %copy-done.5, bf16[256,512]{1,0:T(8,128)(2,1)S(1)} %copy-done.4), custom_call_target="tpu_custom_call" | custom-call | tf_op jit(solution)/shard_map/spectra/pallas_call | solution.py:413
  35.3 1.1 %observe.4 = f32[4,2,128,128]{3,2,1,0:T(8,128)S(1)} custom-call(s32[1]{0:T(128)S(6)} %copy.23.live, f32[3,32,128]{2,1,0:T(8,128)S(1)} %get-tuple-element.20.centre, bf16[32,256,128]{2,1,0:T(8,128)(2,1)S(1)} %spectra.1.sp, bf16[32768,128]{1,0:T(8,128)(2,1)S(1)} %get-tuple-element.22.wts, f32[3,8,128]{2,1,0:T(8,128)S(1)} %get-tuple-element.23.lis), custom_call_target="tpu_custom_call" | custom-call | flops 4000000000 | bytes 1000000 | tf_op jit(solution)/shard_map/observe/pallas_call | solution.py:502
  36.5 5.3 %collective-permute-start.5 = (f32[2,2,128,128]{3,2,1,0:T(8,128)S(1)}, f32[2,2,128,128]{3,2,1,0:T(8,128)S(1)}, u32[]{:S(2)}, u32[]{:S(2)}) collective-permute-start(f32[2,2,128,128]{3,2,1,0:T(8,128)S(1)} %dynamic-slice_bitcast_fusion.1), channel_id=1, source_target_pairs={{0,1},{1,0},{2,3},{3,2},{4,5},{5,4},{6,7},{7,6},{8,9},{9,8},{10,11... | collective-permute-start | bytes 786440 | tf_op jit(solution)/shard_map/ppermute | solution.py:516
  43.1 5.7 %collective-permute-done.6 = f32[1,2,128,128]{3,2,1,0:T(8,128)S(1)} collective-permute-done((f32[1,2,128,128]{3,2,1,0:T(8,128)S(1)}, f32[1,2,128,128]{3,2,1,0:T(8,128)S(1)}, u32[]{:S(2)}, u32[]{:S(2)}) %collective-permute-start.6) | collective-permute-done | bytes 131104 | tf_op jit(solution)/shard_map/ppermute | solution.py:516
  49.5 1.2 %collective-permute-done.11 = f32[2,2,128,128]{3,2,1,0:T(8,128)S(1)} collective-permute-done((f32[2,2,128,128]{3,2,1,0:T(8,128)S(1)}, f32[2,2,128,128]{3,2,1,0:T(8,128)S(1)}, u32[]{:S(2)}, u32[]{:S(2)}) %collective-permute-start.11) | collective-permute-done | bytes 262176 | tf_op jit(solution)/shard_map/ppermute | solution.py:516
  51.1 4.0 %collective-permute-start.7 = (f32[1,2,64,128]{3,2,1,0:T(8,128)S(1)}, f32[1,2,64,128]{3,2,1,0:T(8,128)S(1)}, u32[]{:S(2)}, u32[]{:S(2)}) collective-permute-start(f32[1,2,64,128]{3,2,1,0:T(8,128)S(1)} %dynamic-slice_bitcast_fusion.3), channel_id=1, source_target_pairs={{0,16},{16,0},{1,17},{17,1},{2,18},{18,2},{3,19},{19,3},{4,20},{20... | collective-permute-start | bytes 196616 | tf_op jit(solution)/shard_map/ppermute | solution.py:516
  55.1 1.5 %collective-permute-done.12 = f32[1,2,128,128]{3,2,1,0:T(8,128)S(1)} collective-permute-done((f32[1,2,128,128]{3,2,1,0:T(8,128)S(1)}, f32[1,2,128,128]{3,2,1,0:T(8,128)S(1)}, u32[]{:S(2)}, u32[]{:S(2)}) %collective-permute-start.12) | collective-permute-done | bytes 131104 | tf_op jit(solution)/shard_map/ppermute | solution.py:516
  56.6 4.2 %collective-permute-start.13 = (f32[1,2,64,128]{3,2,1,0:T(8,128)S(1)}, f32[1,2,64,128]{3,2,1,0:T(8,128)S(1)}, u32[]{:S(2)}, u32[]{:S(2)}) collective-permute-start(f32[1,2,64,128]{3,2,1,0:T(8,128)S(1)} %dynamic-slice_bitcast_fusion.2), channel_id=1, source_target_pairs={{0,16},{16,0},{1,17},{17,1},{2,18},{18,2},{3,19},{19,3},{4,20},{20... | collective-permute-start | bytes 196616 | tf_op jit(solution)/shard_map/ppermute | solution.py:516
  60.9 12.6 %collective-permute-start.8 = (f32[1,2,64,128]{3,2,1,0:T(8,128)S(1)}, f32[1,2,64,128]{3,2,1,0:T(8,128)S(1)}, u32[]{:S(2)}, u32[]{:S(2)}) collective-permute-start(f32[1,2,64,128]{3,2,1,0:T(8,128)S(1)} %bitcast_add_fusion.3), channel_id=1, source_target_pairs={{0,4},{4,0},{8,12},{12,8},{1,5},{5,1},{9,13},{13,9},{2,6},{6,2},{1... | collective-permute-start | bytes 196616 | tf_op jit(solution)/shard_map/ppermute | solution.py:516
  73.5 2.2 %collective-permute-start.14 = (f32[1,2,64,128]{3,2,1,0:T(8,128)S(1)}, f32[1,2,64,128]{3,2,1,0:T(8,128)S(1)}, u32[]{:S(2)}, u32[]{:S(2)}) collective-permute-start(f32[1,2,64,128]{3,2,1,0:T(8,128)S(1)} %bitcast_add_fusion.2), channel_id=1, source_target_pairs={{0,4},{4,0},{8,12},{12,8},{1,5},{5,1},{9,13},{13,9},{2,6},{6,2},{1... | collective-permute-start | bytes 196616 | tf_op jit(solution)/shard_map/ppermute | solution.py:516
  76.2 1.9 %collective-permute-start.9 = (f32[1,2,64,128]{3,2,1,0:T(8,128)S(1)}, f32[1,2,64,128]{3,2,1,0:T(8,128)S(1)}, u32[]{:S(2)}, u32[]{:S(2)}) collective-permute-start(f32[1,2,64,128]{3,2,1,0:T(8,128)S(1)} %add.90), channel_id=1, source_target_pairs={{0,8},{4,12},{8,0},{12,4},{1,9},{5,13},{9,1},{13,5},{2,10},{6,14},... | collective-permute-start | bytes 196616 | tf_op jit(solution)/shard_map/ppermute | solution.py:516
  78.7 2.2 %collective-permute-start.15 = (f32[1,2,64,128]{3,2,1,0:T(8,128)S(1)}, f32[1,2,64,128]{3,2,1,0:T(8,128)S(1)}, u32[]{:S(2)}, u32[]{:S(2)}) collective-permute-start(f32[1,2,64,128]{3,2,1,0:T(8,128)S(1)} %add.95), channel_id=1, source_target_pairs={{0,8},{4,12},{8,0},{12,4},{1,9},{5,13},{9,1},{13,5},{2,10},{6,14},... | collective-permute-start | bytes 196616 | tf_op jit(solution)/shard_map/ppermute | solution.py:516
  81.5 2.5 %collective-permute-start.10 = (f32[1,2,64,128]{3,2,1,0:T(8,128)S(1)}, f32[1,2,64,128]{3,2,1,0:T(8,128)S(1)}, u32[]{:S(2)}, u32[]{:S(2)}) collective-permute-start(f32[1,2,64,128]{3,2,1,0:T(8,128)S(1)} %add.91), channel_id=1, source_target_pairs={{0,16},{16,0},{1,17},{17,1},{2,18},{18,2},{3,19},{19,3},{4,20},{20... | collective-permute-start | bytes 196616 | tf_op jit(solution)/shard_map/ppermute | solution.py:516
  83.9 1.8 %collective-permute-start.16 = (f32[1,2,64,128]{3,2,1,0:T(8,128)S(1)}, f32[1,2,64,128]{3,2,1,0:T(8,128)S(1)}, u32[]{:S(2)}, u32[]{:S(2)}) collective-permute-start(f32[1,2,64,128]{3,2,1,0:T(8,128)S(1)} %add.96), channel_id=1, source_target_pairs={{0,16},{16,0},{1,17},{17,1},{2,18},{18,2},{3,19},{19,3},{4,20},{20... | collective-permute-start | bytes 196616 | tf_op jit(solution)/shard_map/ppermute | solution.py:516
  86.2 2.1 %collective-permute-done.16 = f32[1,2,64,128]{3,2,1,0:T(8,128)S(1)} collective-permute-done((f32[1,2,64,128]{3,2,1,0:T(8,128)S(1)}, f32[1,2,64,128]{3,2,1,0:T(8,128)S(1)}, u32[]{:S(2)}, u32[]{:S(2)}) %collective-permute-start.16) | collective-permute-done | bytes 65568 | tf_op jit(solution)/shard_map/ppermute | solution.py:516
  (64 shorter events, 6.0 us)
Async XLA Ops:
  2.0 9.1 %copy-start.7 = (f32[2,1024]{1,0:T(2,128)S(1)}, f32[2,1024]{1,0:T(2,128)}, u32[]{:S(2)}) copy-start(f32[2,1024]{1,0:T(2,128)} %param.15) | copy-start | bytes 24580
  2.0 9.2 %copy-start.8 = (f32[1024]{0:T(1024)S(1)}, f32[1024]{0:T(1024)}, u32[]{:S(2)}) copy-start(f32[1024]{0:T(1024)} %param.16) | copy-start | bytes 12292
  2.0 10.0 %copy-start.6 = (f32[2,4096]{1,0:T(2,128)S(1)}, f32[2,4096]{1,0:T(2,128)}, u32[]{:S(2)}) copy-start(f32[2,4096]{1,0:T(2,128)} %param.13) | copy-start | bytes 98308
  2.0 10.0 %copy-start.5 = (s32[32,128]{1,0:T(8,128)S(1)}, s32[32,128]{1,0:T(8,128)}, u32[]{:S(2)}) copy-start(s32[32,128]{1,0:T(8,128)} %cell.3) | copy-start | bytes 49156
  2.5 24.7 %collective-permute-start = (f32[960,128]{1,0:T(8,128)S(1)}, f32[960,128]{1,0:T(8,128)S(1)}, u32[]{:S(2)}, u32[]{:S(2)}) collective-permute-start(f32[960,128]{1,0:T(8,128)S(1)} %get-tuple-element.13), channel_id=1, source_target_pairs={{0,16},{16,0},{1,17},{17,1},{2,18},{18,2},{3,19},{19,3},{4,20},{20... | collective-permute-start | bytes 1474568 | tf_op jit(solution)/shard_map/ppermute | solution.py:516
  5.5 8.6 %collective-permute-start.3 = (f32[60,128]{1,0:T(8,128)S(1)}, f32[60,128]{1,0:T(8,128)S(1)}, u32[]{:S(2)}, u32[]{:S(2)}) collective-permute-start(f32[60,128]{1,0:T(8,128)S(1)} %get-tuple-element.17), channel_id=1, source_target_pairs={{0,1},{1,2},{2,3},{3,0},{4,5},{5,6},{6,7},{7,4},{8,9},{9,10},{10,1... | collective-permute-start | bytes 92168 | tf_op jit(solution)/shard_map/ppermute | solution.py:231
  5.5 8.6 %collective-permute-start.4 = (f32[60,128]{1,0:T(8,128)S(1)}, f32[60,128]{1,0:T(8,128)S(1)}, u32[]{:S(2)}, u32[]{:S(2)}) collective-permute-start(f32[60,128]{1,0:T(8,128)S(1)} %get-tuple-element.18), channel_id=1, source_target_pairs={{1,0},{2,1},{3,2},{0,3},{5,4},{6,5},{7,6},{4,7},{9,8},{10,9},{11,1... | collective-permute-start | bytes 92168 | tf_op jit(solution)/shard_map/ppermute | solution.py:231
  7.3 13.3 %collective-permute-start.1 = (f32[240,128]{1,0:T(8,128)S(1)}, f32[240,128]{1,0:T(8,128)S(1)}, u32[]{:S(2)}, u32[]{:S(2)}) collective-permute-start(f32[240,128]{1,0:T(8,128)S(1)} %get-tuple-element.14), channel_id=1, source_target_pairs={{0,4},{4,8},{8,12},{12,0},{1,5},{5,9},{9,13},{13,1},{2,6},{6,10},{... | collective-permute-start | bytes 368648 | tf_op jit(solution)/shard_map/ppermute | solution.py:231
  8.8 11.8 %collective-permute-start.2 = (f32[240,128]{1,0:T(8,128)S(1)}, f32[240,128]{1,0:T(8,128)S(1)}, u32[]{:S(2)}, u32[]{:S(2)}) collective-permute-start(f32[240,128]{1,0:T(8,128)S(1)} %get-tuple-element.15), channel_id=1, source_target_pairs={{4,0},{8,4},{12,8},{0,12},{5,1},{9,5},{13,9},{1,13},{6,2},{10,6},{... | collective-permute-start | bytes 368648 | tf_op jit(solution)/shard_map/ppermute | solution.py:231
  20.6 6.6 %copy-start.3 = (f32[5,16,32,128]{3,2,1,0:T(8,128)S(1)}, f32[5,16,32,128]{3,2,1,0:T(8,128)}, u32[]{:S(2)}) copy-start(f32[5,16,32,128]{3,2,1,0:T(8,128)} %param.9) | copy-start | bytes 3932164
  20.6 13.7 %copy-start.4 = (bf16[256,512]{1,0:T(8,128)(2,1)S(1)}, bf16[256,512]{1,0:T(8,128)(2,1)}, u32[]{:S(2)}) copy-start(bf16[256,512]{1,0:T(8,128)(2,1)} %constant.124.clone.table) | copy-start | bytes 786436
  27.2 7.1 %copy-start.2 = (bf16[4096,512]{1,0:T(8,128)(2,1)S(1)}, bf16[4096,512]{1,0:T(8,128)(2,1)}, u32[]{:S(2)}) copy-start(bf16[4096,512]{1,0:T(8,128)(2,1)} %rec.1) | copy-start | bytes 12582916
  36.5 6.5 %collective-permute-start.5 = (f32[2,2,128,128]{3,2,1,0:T(8,128)S(1)}, f32[2,2,128,128]{3,2,1,0:T(8,128)S(1)}, u32[]{:S(2)}, u32[]{:S(2)}) collective-permute-start(f32[2,2,128,128]{3,2,1,0:T(8,128)S(1)} %dynamic-slice_bitcast_fusion.1), channel_id=1, source_target_pairs={{0,1},{1,0},{2,3},{3,2},{4,5},{5,4},{6,7},{7,6},{8,9},{9,8},{10,11... | collective-permute-start | bytes 786440 | tf_op jit(solution)/shard_map/ppermute | solution.py:516
  43.0 5.8 %collective-permute-start.6 = (f32[1,2,128,128]{3,2,1,0:T(8,128)S(1)}, f32[1,2,128,128]{3,2,1,0:T(8,128)S(1)}, u32[]{:S(2)}, u32[]{:S(2)}) collective-permute-start(f32[1,2,128,128]{3,2,1,0:T(8,128)S(1)} %constant_dynamic-slice_fusion.1), channel_id=1, source_target_pairs={{0,2},{1,3},{2,0},{3,1},{4,6},{5,7},{6,4},{7,5},{8,10},{9,11},{10,... | collective-permute-start | bytes 393224 | tf_op jit(solution)/shard_map/ppermute | solution.py:516
  49.1 1.6 %collective-permute-start.11 = (f32[2,2,128,128]{3,2,1,0:T(8,128)S(1)}, f32[2,2,128,128]{3,2,1,0:T(8,128)S(1)}, u32[]{:S(2)}, u32[]{:S(2)}) collective-permute-start(f32[2,2,128,128]{3,2,1,0:T(8,128)S(1)} %dynamic-slice_bitcast_fusion), channel_id=1, source_target_pairs={{0,1},{1,0},{2,3},{3,2},{4,5},{5,4},{6,7},{7,6},{8,9},{9,8},{10,11... | collective-permute-start | bytes 786440 | tf_op jit(solution)/shard_map/ppermute | solution.py:516
  50.8 5.8 %collective-permute-start.12 = (f32[1,2,128,128]{3,2,1,0:T(8,128)S(1)}, f32[1,2,128,128]{3,2,1,0:T(8,128)S(1)}, u32[]{:S(2)}, u32[]{:S(2)}) collective-permute-start(f32[1,2,128,128]{3,2,1,0:T(8,128)S(1)} %constant_dynamic-slice_fusion), channel_id=1, source_target_pairs={{0,2},{1,3},{2,0},{3,1},{4,6},{5,7},{6,4},{7,5},{8,10},{9,11},{10,... | collective-permute-start | bytes 393224 | tf_op jit(solution)/shard_map/ppermute | solution.py:516
  51.1 9.7 %collective-permute-start.7 = (f32[1,2,64,128]{3,2,1,0:T(8,128)S(1)}, f32[1,2,64,128]{3,2,1,0:T(8,128)S(1)}, u32[]{:S(2)}, u32[]{:S(2)}) collective-permute-start(f32[1,2,64,128]{3,2,1,0:T(8,128)S(1)} %dynamic-slice_bitcast_fusion.3), channel_id=1, source_target_pairs={{0,16},{16,0},{1,17},{17,1},{2,18},{18,2},{3,19},{19,3},{4,20},{20... | collective-permute-start | bytes 196616 | tf_op jit(solution)/shard_map/ppermute | solution.py:516
  56.6 16.8 %collective-permute-start.13 = (f32[1,2,64,128]{3,2,1,0:T(8,128)S(1)}, f32[1,2,64,128]{3,2,1,0:T(8,128)S(1)}, u32[]{:S(2)}, u32[]{:S(2)}) collective-permute-start(f32[1,2,64,128]{3,2,1,0:T(8,128)S(1)} %dynamic-slice_bitcast_fusion.2), channel_id=1, source_target_pairs={{0,16},{16,0},{1,17},{17,1},{2,18},{18,2},{3,19},{19,3},{4,20},{20... | collective-permute-start | bytes 196616 | tf_op jit(solution)/shard_map/ppermute | solution.py:516
  60.9 15.3 %collective-permute-start.8 = (f32[1,2,64,128]{3,2,1,0:T(8,128)S(1)}, f32[1,2,64,128]{3,2,1,0:T(8,128)S(1)}, u32[]{:S(2)}, u32[]{:S(2)}) collective-permute-start(f32[1,2,64,128]{3,2,1,0:T(8,128)S(1)} %bitcast_add_fusion.3), channel_id=1, source_target_pairs={{0,4},{4,0},{8,12},{12,8},{1,5},{5,1},{9,13},{13,9},{2,6},{6,2},{1... | collective-permute-start | bytes 196616 | tf_op jit(solution)/shard_map/ppermute | solution.py:516
  73.5 5.2 %collective-permute-start.14 = (f32[1,2,64,128]{3,2,1,0:T(8,128)S(1)}, f32[1,2,64,128]{3,2,1,0:T(8,128)S(1)}, u32[]{:S(2)}, u32[]{:S(2)}) collective-permute-start(f32[1,2,64,128]{3,2,1,0:T(8,128)S(1)} %bitcast_add_fusion.2), channel_id=1, source_target_pairs={{0,4},{4,0},{8,12},{12,8},{1,5},{5,1},{9,13},{13,9},{2,6},{6,2},{1... | collective-permute-start | bytes 196616 | tf_op jit(solution)/shard_map/ppermute | solution.py:516
  76.2 5.2 %collective-permute-start.9 = (f32[1,2,64,128]{3,2,1,0:T(8,128)S(1)}, f32[1,2,64,128]{3,2,1,0:T(8,128)S(1)}, u32[]{:S(2)}, u32[]{:S(2)}) collective-permute-start(f32[1,2,64,128]{3,2,1,0:T(8,128)S(1)} %add.90), channel_id=1, source_target_pairs={{0,8},{4,12},{8,0},{12,4},{1,9},{5,13},{9,1},{13,5},{2,10},{6,14},... | collective-permute-start | bytes 196616 | tf_op jit(solution)/shard_map/ppermute | solution.py:516
  78.7 5.3 %collective-permute-start.15 = (f32[1,2,64,128]{3,2,1,0:T(8,128)S(1)}, f32[1,2,64,128]{3,2,1,0:T(8,128)S(1)}, u32[]{:S(2)}, u32[]{:S(2)}) collective-permute-start(f32[1,2,64,128]{3,2,1,0:T(8,128)S(1)} %add.95), channel_id=1, source_target_pairs={{0,8},{4,12},{8,0},{12,4},{1,9},{5,13},{9,1},{13,5},{2,10},{6,14},... | collective-permute-start | bytes 196616 | tf_op jit(solution)/shard_map/ppermute | solution.py:516
  81.5 4.7 %collective-permute-start.10 = (f32[1,2,64,128]{3,2,1,0:T(8,128)S(1)}, f32[1,2,64,128]{3,2,1,0:T(8,128)S(1)}, u32[]{:S(2)}, u32[]{:S(2)}) collective-permute-start(f32[1,2,64,128]{3,2,1,0:T(8,128)S(1)} %add.91), channel_id=1, source_target_pairs={{0,16},{16,0},{1,17},{17,1},{2,18},{18,2},{3,19},{19,3},{4,20},{20... | collective-permute-start | bytes 196616 | tf_op jit(solution)/shard_map/ppermute | solution.py:516
  83.9 4.3 %collective-permute-start.16 = (f32[1,2,64,128]{3,2,1,0:T(8,128)S(1)}, f32[1,2,64,128]{3,2,1,0:T(8,128)S(1)}, u32[]{:S(2)}, u32[]{:S(2)}) collective-permute-start(f32[1,2,64,128]{3,2,1,0:T(8,128)S(1)} %add.96), channel_id=1, source_target_pairs={{0,16},{16,0},{1,17},{17,1},{2,18},{18,2},{3,19},{19,3},{4,20},{20... | collective-permute-start | bytes 196616 | tf_op jit(solution)/shard_map/ppermute | solution.py:516
  (2 other events, 7.8 us)

commit v6 on v5

--- a/solution.py
+++ b/solution.py
@@ -296,7 +296,15 @@
     return cos_p * cos_a, cos_p * sin_a, sin_p
 
 
-def weights_kernel(live, corner, cell, angles, raw, out, centre, lis, geo, lisb, *, sizes, counts):
+def three(value):
+    high = value.astype(jnp.bfloat16).astype(jnp.float32)
+    middle = (value - high).astype(jnp.bfloat16).astype(jnp.float32)
+    return high, middle, ((value - high) - middle).astype(jnp.bfloat16).astype(jnp.float32)
+
+
+def weights_kernel(
+    live, corner, cell, angles, raw, out, centre, lis, geo, lisb, pan, row_side, sides, col_side, cols, *, sizes, counts
+):
     slots, bp = cell.shape
     tiles = lis.shape[1]
     span = tiles * 128 // CHUNKS
@@ -305,36 +313,69 @@
     rest = cells - along_x * float(sizes[1] * sizes[2])
     along_y = jnp.floor((rest + 0.5) * (1.0 / sizes[2]))
     along_z = rest - along_y * float(sizes[2])
+    offsets = []
     for k, along in enumerate((along_x, along_y, along_z)):
         place = ((along + corner[k].astype(jnp.float32)) + 0.5) / float(counts[k])
-        geo[k] = place
         mean = jnp.sum(place, axis=1, keepdims=True) * (1.0 / bp)
         centre[k] = jnp.broadcast_to(mean, (slots, 128))
+        offsets.append(place - 0.5)
     shown = lax.broadcasted_iota(jnp.int32, (slots, bp), 0) < live[0]
+    along_normal = 0.0
     for k, part in enumerate(direction(angles[0], angles[1])):
-        geo[3 + k] = jnp.where(shown, part * (0.25 / math.pi), 0.0)
+        geo[k] = jnp.where(shown, part * (0.25 / math.pi), 0.0)
+        along_normal = along_normal + geo[k] * offsets[k]
+    geo[3] = along_normal
+    shifts = []
     for k, part in enumerate(direction(raw[0], raw[1])):
-        lis[k] = 0.5 + raw[2] * part
+        shift = raw[2] * part
+        lis[k] = 0.5 + shift
+        shifts.append(shift)
+        for t in range(tiles):
+            lisb[k, t * 128 : (t + 1) * 128, :] = jnp.transpose(jnp.broadcast_to(shift[t : t + 1, :], (128, 128)))
+    one = jnp.ones((tiles, 128), jnp.float32)
+    left, right = [], []
     for k in range(3):
+        for n, part in enumerate(three(-2.0 * offsets[k])):
+            pan[3 * k + n] = part
+        high, middle, low = three(shifts[k])
+        left += [high, high, high, middle, middle, low]
+        right += [3 * k, 3 * k + 1, 3 * k + 2, 3 * k, 3 * k + 1, 3 * k]
+    for n, part in enumerate(three(offsets[0] * offsets[0] + offsets[1] * offsets[1] + offsets[2] * offsets[2])):
+        pan[9 + n] = part
+    pan[12] = jnp.ones((slots, bp), jnp.float32)
+    left += [*three(shifts[0] * shifts[0] + shifts[1] * shifts[1] + shifts[2] * shifts[2]), one, one, one]
+    right += [12, 12, 12, 9, 10, 11]
+    row_side[...] = jnp.zeros(row_side.shape, jnp.float32)
+    col_side[...] = jnp.zeros(col_side.shape, jnp.float32)
+    cols[...] = jnp.zeros(cols.shape, jnp.bfloat16)
+    for n, part in enumerate(left):
         for t in range(tiles):
-            row = lis[k, t : t + 1, :]
-            lisb[k, t * 128 : (t + 1) * 128, :] = jnp.transpose(jnp.broadcast_to(row, (128, 128)))
-
-    def block(b, _):
-        px, py, pz, nx, ny, nz = [geo[k, pl.ds(b, 1), :] for k in range(6)]
+            row_side[n : n + 1, t * 128 : (t + 1) * 128] = part[t : t + 1, :]
+    for t in range(tiles):
+        sides[t * 128 : (t + 1) * 128, :] = jnp.transpose(row_side[:, t * 128 : (t + 1) * 128]).astype(jnp.bfloat16)
+
+    def pair(turn, _):
+        first = turn * 2
+        for j in range(2):
+            for n, source in enumerate(right):
+                col_side[n : n + 1, j * bp : (j + 1) * bp] = pan[source, pl.ds(first + j, 1), :]
+        cols[0:32, :] = col_side[...].astype(jnp.bfloat16)
+        parts = [[geo[k, pl.ds(first + j, 1), :] for k in range(4)] for j in range(2)]
         for q in range(CHUNKS):
-            for r in range(0, span, 16):
+            for r in range(0, span, 128):
                 at = q * span + r
-                ox = lisb[0, at : at + 16, :] - px
-                oy = lisb[1, at : at + 16, :] - py
-                oz = lisb[2, at : at + 16, :] - pz
-                d2 = ox * ox + oy * oy + oz * oz
-                facing = nx * ox + ny * oy + nz * oz
-                row = pl.multiple_of(q * slots * span + b * span + r, 16)
-                out[pl.ds(row, 16), :] = (facing * (1.0 / d2)).astype(jnp.bfloat16)
+                d2 = jnp.dot(sides[at : at + 128, :], cols[...], preferred_element_type=jnp.float32)
+                for w in range(0, 128, 16):
+                    lx, ly, lz = [lisb[k, at + w : at + w + 16, :] for k in range(3)]
+                    for j in range(2):
+                        nx, ny, nz, shift = parts[j]
+                        facing = (nx * lx + ny * ly) + (nz * lz - shift)
+                        row = pl.multiple_of(q * slots * span + (first + j) * span + r + w, 16)
+                        value = facing * (1.0 / d2[w : w + 16, j * bp : (j + 1) * bp])
+                        out[pl.ds(row, 16), :] = value.astype(jnp.bfloat16)
         return 0
 
-    lax.fori_loop(0, (live[0] + BATCH - 1) // BATCH * BATCH, block, 0)
+    lax.fori_loop(0, (live[0] + BATCH - 1) // BATCH * (BATCH // 2), pair, 0)
 
 
 def weights(live, corner, cell, angles, raw, sizes, counts):
@@ -351,7 +392,15 @@
         ],
         in_specs=[sm, sm, vm, vm, vm],
         out_specs=[vm] * 3,
-        scratch_shapes=[pltpu.VMEM((6, slots, bp), jnp.float32), pltpu.VMEM((3, obs, 128), jnp.float32)],
+        scratch_shapes=[
+            pltpu.VMEM((4, slots, bp), jnp.float32),
+            pltpu.VMEM((3, obs, 128), jnp.float32),
+            pltpu.VMEM((13, slots, bp), jnp.float32),
+            pltpu.VMEM((128, obs), jnp.float32),
+            pltpu.VMEM((obs, 128), jnp.bfloat16),
+            pltpu.VMEM((32, 2 * bp), jnp.float32),
+            pltpu.VMEM((128, 2 * bp), jnp.bfloat16),
+        ],
         name="weights",
         compiler_params=pltpu.CompilerParams(vmem_limit_bytes=4 * 1024 * 1024),
     )(live, corner, cell, angles, raw)
@@ -449,12 +498,12 @@
 
     def group(turn, _):
         g = turn * parts + part
-        for pair in range(0, BATCH, 2):
+        for h, pair in [(h, pair) for h in range(0, span, 256) for pair in range(0, BATCH, 2)]:
             for j in range(2):
                 b = g * BATCH + pair + j
-                held = wts[pl.ds(pl.multiple_of(chunk * slots * span + b * span, span), span), :]
-                prod[pair + j] = lax.dot_general(sp[b], held, NT, preferred_element_type=jnp.float32)
-            for t in range(tiles):
+                held = wts[pl.ds(pl.multiple_of(chunk * slots * span + b * span + h, 256), 256), :]
+                prod[pair + j, :, h : h + 256] = lax.dot_general(sp[b], held, NT, preferred_element_type=jnp.float32)
+            for t in range(h // 128, h // 128 + 2):
                 state = []
                 for j in range(2):
                     b = g * BATCH + pair + j

time: 90.6 us -> 88.9 us (0.981); the launches traced: 89 us -> 88.8 us
  starting transfers between devices: 46.1 us -> 17.9 us
  Pallas kernels: 26 us -> 46.4 us
  waiting for transfers between devices: 12.7 us -> 20.2 us
    ppermute x13, starting transfers between devices: 40.6 us -> 12.3 us  [swap(): return lax.ppermute(value, axis, [(i, i ^ bit) for i in range(size)])]
    pallas_call x4, Pallas kernels: 2.29 us -> 11.9 us  [observe(): pl.pallas_call(functools.partial(observe_kernel, chunk=chunk, part=part,...]
    ppermute x13, waiting for transfers between devices: 12.7 us -> 20.2 us  [swap(): return lax.ppermute(value, axis, [(i, i ^ bit) for i in range(size)])]
    pallas_call x1, Pallas kernels: 1.05 us -> 6.91 us  [spectra(): pl.pallas_call(spectra_kernel, out_shape=jax.ShapeDtypeStruct((slots, k2,...]
    pallas_call x1, Pallas kernels: 2.14 us -> 7.1 us  [weights(): pl.pallas_call(functools.partial(weights_kernel, sizes=sizes, counts=coun...]
  transfers between devices with their start and end apart: 17 -> 17, of which waited for: 9 -> 8; matrix products, arithmetic and copies ran while one was open for 0% -> 0% of each run, Pallas kernels for 18% -> 28%
where the time goes in v6:
time: 88.9 us; the launch traced here: 88.8 us
  Pallas kernels  46.4 us (52%)
  waiting for transfers between devices  20.2 us (23%)
  starting transfers between devices  17.9 us (20%)
  between operations  1.76 us (2%)
  local copies, waits for them, and re-layouts  1.5 us (2%)
  other arithmetic  1.01 us (1%)
    ppermute x13, waiting for transfers between devices, swap(): return lax.ppermute(value, axis, [(i, i ^ bit) for i in range(size)])  20.2 us
    pallas_call x3, Pallas kernels, line_call(): pl.pallas_call(kernel, out_shape=[jax.ShapeDtypeStruct(shape, jnp.float32...  20 us
    ppermute x13, starting transfers between devices, swap(): return lax.ppermute(value, axis, [(i, i ^ bit) for i in range(size)])  12.3 us
    pallas_call x4, Pallas kernels, observe(): pl.pallas_call(functools.partial(observe_kernel, chunk=chunk, part=part,...  11.9 us
    pallas_call x1, Pallas kernels, weights(): pl.pallas_call(functools.partial(weights_kernel, sizes=sizes, counts=coun...  7.1 us
    pallas_call x1, Pallas kernels, spectra(): pl.pallas_call(spectra_kernel, out_shape=jax.ShapeDtypeStruct((slots, k2,...  6.91 us
    ppermute x4, starting transfers between devices, neighbours(): return (lax.ppermute(last, axis, up), lax.ppermute(first, axis, down))  5.57 us
  transfers between devices with their start and end apart: 17, of which 8 were waited for; matrix products, arithmetic and copies ran while one was open for 0% of the time, Pallas kernels for 28%

profile of v6, /device:TPU:0, one launch (start us, length us, event | category | flops | bytes accessed | tf_op | source)
XLA Modules:
  0.0 88.8 jit_solution(9688302403583974307)
XLA Ops:
  0.6 1.3 %copy-done = f32[5,16,32,128]{3,2,1,0:T(8,128)S(1)} copy-done((f32[5,16,32,128]{3,2,1,0:T(8,128)S(1)}, f32[5,16,32,128]{3,2,1,0:T(8,128)}, u32[]{:S(2)}) %copy-start) | copy-done | bytes 1310744
  2.5 3.0 %collective-permute-start = (f32[960,128]{1,0:T(8,128)S(1)}, f32[960,128]{1,0:T(8,128)S(1)}, u32[]{:S(2)}, u32[]{:S(2)}) collective-permute-start(f32[960,128]{1,0:T(8,128)S(1)} %get-tuple-element.13), channel_id=1, source_target_pairs={{0,16},{16,0},{1,17},{17,1},{2,18},{18,2},{3,19},{19,3},{4,20},{20... | collective-permute-start | bytes 1474568 | tf_op jit(solution)/shard_map/ppermute | solution.py:565
  5.5 1.7 %collective-permute-start.4 = (f32[60,128]{1,0:T(8,128)S(1)}, f32[60,128]{1,0:T(8,128)S(1)}, u32[]{:S(2)}, u32[]{:S(2)}) collective-permute-start(f32[60,128]{1,0:T(8,128)S(1)} %get-tuple-element.18), channel_id=1, source_target_pairs={{1,0},{2,1},{3,2},{0,3},{5,4},{6,5},{7,6},{4,7},{9,8},{10,9},{11,1... | collective-permute-start | bytes 92168 | tf_op jit(solution)/shard_map/ppermute | solution.py:231
  7.3 1.6 %collective-permute-start.1 = (f32[240,128]{1,0:T(8,128)S(1)}, f32[240,128]{1,0:T(8,128)S(1)}, u32[]{:S(2)}, u32[]{:S(2)}) collective-permute-start(f32[240,128]{1,0:T(8,128)S(1)} %get-tuple-element.14), channel_id=1, source_target_pairs={{0,4},{4,8},{8,12},{12,0},{1,5},{5,9},{9,13},{13,1},{2,6},{6,10},{... | collective-permute-start | bytes 368648 | tf_op jit(solution)/shard_map/ppermute | solution.py:231
  8.8 2.2 %collective-permute-start.2 = (f32[240,128]{1,0:T(8,128)S(1)}, f32[240,128]{1,0:T(8,128)S(1)}, u32[]{:S(2)}, u32[]{:S(2)}) collective-permute-start(f32[240,128]{1,0:T(8,128)S(1)} %get-tuple-element.15), channel_id=1, source_target_pairs={{4,0},{8,4},{12,8},{0,12},{5,1},{9,5},{13,9},{1,13},{6,2},{10,6},{... | collective-permute-start | bytes 368648 | tf_op jit(solution)/shard_map/ppermute | solution.py:231
  12.0 7.1 %weights.1 = (bf16[32768,128]{1,0:T(8,128)(2,1)S(1)}, f32[3,32,128]{2,1,0:T(8,128)S(1)}, f32[3,8,128]{2,1,0:T(8,128)S(1)}) custom-call(s32[1]{0:T(128)S(6)} %copy.23.live, s32[3]{0:T(128)S(1)} %pad_add_fusion.corner, s32[32,128]{1,0:T(8,128)S(1)} %copy-done.5, f32[2,32,128]{2,1,0:T(8,128)S(1)} %bitcast.52, f32[3,8,128]{2,1,0:T(8,128)S(1)} %bitcast.53), custom_call_target="tpu_custom_call" | custom-call | tf_op jit(solution)/shard_map/weights/pallas_call | solution.py:386
  19.1 6.4 %along_z.1.start = f32[2560,128]{1,0:T(8,128)S(1)} custom-call(f32[2560,128]{1,0:T(8,128)S(1)} %get-tuple-element.16.turned, f32[60,128]{1,0:T(8,128)S(1)} %collective-permute-done.3.left, f32[60,128]{1,0:T(8,128)S(1)} %collective-permute-done.4.right), custom_call_target="tpu_custom_call" | custom-call | tf_op jit(solution)/shard_map/along_z/pallas_call | solution.py:210
  25.6 6.5 %along_y.1.start = f32[2560,128]{1,0:T(8,128)S(1)} custom-call(f32[2560,128]{1,0:T(8,128)S(1)} %bitcast.43, f32[240,128]{1,0:T(8,128)S(1)} %collective-permute-done.1.left, f32[240,128]{1,0:T(8,128)S(1)} %collective-permute-done.2.right, f32[2560,128]{1,0:T(8,128)S(1)} %along_z.1.start), custom_call_target="tpu_custom_call" | custom-call | tf_op jit(solution)/shard_map/along_y/pallas_call | solution.py:210
  32.2 7.1 %along_x.1 = (f32[2560,128]{1,0:T(8,128)}, f32[512,128]{1,0:T(8,128)S(1)}) custom-call(f32[2560,128]{1,0:T(8,128)S(1)} %bitcast.44, f32[960,128]{1,0:T(8,128)S(1)} %collective-permute-done.ends, f32[2560,128]{1,0:T(8,128)S(1)} %along_y.1.start, f32[2560,128]{1,0:T(8,128)S(1)} %bitcast.45), custom_call_target="tpu_custom_call" | custom-call | tf_op jit(solution)/shard_map/along_x/pallas_call | solution.py:210
  39.2 6.9 %spectra.1.sp = bf16[32,256,128]{2,1,0:T(8,128)(2,1)S(1)} custom-call(s32[1]{0:T(128)S(6)} %copy.23.live, f32[512,128]{1,0:T(8,128)S(1)} %get-tuple-element.21.dens, bf16[4096,512]{1,0:T(8,128)(2,1)S(1)} %copy-done.2, s32[32,128]{1,0:T(8,128)S(1)} %copy-done.5, bf16[256,512]{1,0:T(8,128)(2,1)S(1)} %copy-done.4), custom_call_target="tpu_custom_call" | custom-call | tf_op jit(solution)/shard_map/spectra/pallas_call | solution.py:462
  46.2 5.7 %observe.4 = f32[4,2,128,128]{3,2,1,0:T(8,128)S(1)} custom-call(s32[1]{0:T(128)S(6)} %copy.23.live, f32[3,32,128]{2,1,0:T(8,128)S(1)} %get-tuple-element.20.centre, bf16[32,256,128]{2,1,0:T(8,128)(2,1)S(1)} %spectra.1.sp, bf16[32768,128]{1,0:T(8,128)(2,1)S(1)} %get-tuple-element.22.wts, f32[3,8,128]{2,1,0:T(8,128)S(1)} %get-tuple-element.23.lis), custom_call_target="tpu_custom_call" | custom-call | flops 4000000000 | bytes 1000000 | tf_op jit(solution)/shard_map/observe/pallas_call | solution.py:551
  52.0 2.6 %observe.5.refs_0_ = f32[2,128,512]{2,1,0:T(8,128)S(1)} custom-call(s32[1]{0:T(128)S(6)} %copy.23.live, f32[3,32,128]{2,1,0:T(8,128)S(1)} %get-tuple-element.20.centre, bf16[32,256,128]{2,1,0:T(8,128)(2,1)S(1)} %spectra.1.sp, bf16[32768,128]{1,0:T(8,128)(2,1)S(1)} %get-tuple-element.22.wts, f32[3,8,128]{2,1,0:T(8,128)S(1)} %get-tuple-element.23.lis), custom_call_target="tpu_custom_call" | custom-call | flops 4000000000 | bytes 1000000 | tf_op jit(solution)/shard_map/observe/pallas_call | solution.py:551
  54.8 1.7 %observe.6.refs_0_ = f32[2,128,512]{2,1,0:T(8,128)S(1)} custom-call(s32[1]{0:T(128)S(6)} %copy.23.live, f32[3,32,128]{2,1,0:T(8,128)S(1)} %get-tuple-element.20.centre, bf16[32,256,128]{2,1,0:T(8,128)(2,1)S(1)} %spectra.1.sp, bf16[32768,128]{1,0:T(8,128)(2,1)S(1)} %get-tuple-element.22.wts, f32[3,8,128]{2,1,0:T(8,128)S(1)} %get-tuple-element.23.lis, ...), custom_call_target="tpu_custom_call" | custom-call | flops 4000000000 | bytes 1000000 | tf_op jit(solution)/shard_map/observe/pallas_call | solution.py:551
  56.5 3.3 %collective-permute-done.6 = f32[1,2,128,128]{3,2,1,0:T(8,128)S(1)} collective-permute-done((f32[1,2,128,128]{3,2,1,0:T(8,128)S(1)}, f32[1,2,128,128]{3,2,1,0:T(8,128)S(1)}, u32[]{:S(2)}, u32[]{:S(2)}) %collective-permute-start.6) | collective-permute-done | bytes 131104 | tf_op jit(solution)/shard_map/ppermute | solution.py:565
  59.8 1.8 %observe.7 = f32[4,2,128,128]{3,2,1,0:T(8,128)S(1)} custom-call(s32[1]{0:T(128)S(6)} %copy.23.live, f32[3,32,128]{2,1,0:T(8,128)S(1)} %get-tuple-element.20.centre, bf16[32,256,128]{2,1,0:T(8,128)(2,1)S(1)} %spectra.1.sp, bf16[32768,128]{1,0:T(8,128)(2,1)S(1)} %get-tuple-element.22.wts, f32[3,8,128]{2,1,0:T(8,128)S(1)} %get-tuple-element.23.lis, ...), custom_call_target="tpu_custom_call" | custom-call | flops 4000000000 | bytes 1000000 | tf_op jit(solution)/shard_map/observe/pallas_call | solution.py:551
  61.7 1.5 %collective-permute-done.11 = f32[2,2,128,128]{3,2,1,0:T(8,128)S(1)} collective-permute-done((f32[2,2,128,128]{3,2,1,0:T(8,128)S(1)}, f32[2,2,128,128]{3,2,1,0:T(8,128)S(1)}, u32[]{:S(2)}, u32[]{:S(2)}) %collective-permute-start.11) | collective-permute-done | bytes 262176 | tf_op jit(solution)/shard_map/ppermute | solution.py:565
  63.5 5.4 %collective-permute-done.12 = f32[1,2,128,128]{3,2,1,0:T(8,128)S(1)} collective-permute-done((f32[1,2,128,128]{3,2,1,0:T(8,128)S(1)}, f32[1,2,128,128]{3,2,1,0:T(8,128)S(1)}, u32[]{:S(2)}, u32[]{:S(2)}) %collective-permute-start.12) | collective-permute-done | bytes 131104 | tf_op jit(solution)/shard_map/ppermute | solution.py:565
  69.1 4.1 %collective-permute-done.13 = f32[1,2,64,128]{3,2,1,0:T(8,128)S(1)} collective-permute-done((f32[1,2,64,128]{3,2,1,0:T(8,128)S(1)}, f32[1,2,64,128]{3,2,1,0:T(8,128)S(1)}, u32[]{:S(2)}, u32[]{:S(2)}) %collective-permute-start.13) | collective-permute-done | bytes 65568 | tf_op jit(solution)/shard_map/ppermute | solution.py:565
  73.4 5.1 %collective-permute-start.9 = (f32[1,2,64,128]{3,2,1,0:T(8,128)S(1)}, f32[1,2,64,128]{3,2,1,0:T(8,128)S(1)}, u32[]{:S(2)}, u32[]{:S(2)}) collective-permute-start(f32[1,2,64,128]{3,2,1,0:T(8,128)S(1)} %add.90), channel_id=1, source_target_pairs={{0,8},{4,12},{8,0},{12,4},{1,9},{5,13},{9,1},{13,5},{2,10},{6,14},... | collective-permute-start | bytes 196616 | tf_op jit(solution)/shard_map/ppermute | solution.py:565
  78.5 2.3 %collective-permute-start.15 = (f32[1,2,64,128]{3,2,1,0:T(8,128)S(1)}, f32[1,2,64,128]{3,2,1,0:T(8,128)S(1)}, u32[]{:S(2)}, u32[]{:S(2)}) collective-permute-start(f32[1,2,64,128]{3,2,1,0:T(8,128)S(1)} %add.95), channel_id=1, source_target_pairs={{0,8},{4,12},{8,0},{12,4},{1,9},{5,13},{9,1},{13,5},{2,10},{6,14},... | collective-permute-start | bytes 196616 | tf_op jit(solution)/shard_map/ppermute | solution.py:565
  80.8 1.7 %collective-permute-done.9 = f32[1,2,64,128]{3,2,1,0:T(8,128)S(1)} collective-permute-done((f32[1,2,64,128]{3,2,1,0:T(8,128)S(1)}, f32[1,2,64,128]{3,2,1,0:T(8,128)S(1)}, u32[]{:S(2)}, u32[]{:S(2)}) %collective-permute-start.9) | collective-permute-done | bytes 65568 | tf_op jit(solution)/shard_map/ppermute | solution.py:565
  83.7 0.9 collective-permute-start.16
  84.6 2.2 %collective-permute-done.10 = f32[1,2,64,128]{3,2,1,0:T(8,128)S(1)} collective-permute-done((f32[1,2,64,128]{3,2,1,0:T(8,128)S(1)}, f32[1,2,64,128]{3,2,1,0:T(8,128)S(1)}, u32[]{:S(2)}, u32[]{:S(2)}) %collective-permute-start.10) | collective-permute-done | bytes 65568 | tf_op jit(solution)/shard_map/ppermute | solution.py:565
  86.8 1.3 %collective-permute-done.16 = f32[1,2,64,128]{3,2,1,0:T(8,128)S(1)} collective-permute-done((f32[1,2,64,128]{3,2,1,0:T(8,128)S(1)}, f32[1,2,64,128]{3,2,1,0:T(8,128)S(1)}, u32[]{:S(2)}, u32[]{:S(2)}) %collective-permute-start.16) | collective-permute-done | bytes 65568 | tf_op jit(solution)/shard_map/ppermute | solution.py:565
  (64 shorter events, 3.6 us)
Async XLA Ops:
  2.0 9.1 %copy-start.7 = (f32[2,1024]{1,0:T(2,128)S(1)}, f32[2,1024]{1,0:T(2,128)}, u32[]{:S(2)}) copy-start(f32[2,1024]{1,0:T(2,128)} %param.15) | copy-start | bytes 24580
  2.0 9.2 %copy-start.8 = (f32[1024]{0:T(1024)S(1)}, f32[1024]{0:T(1024)}, u32[]{:S(2)}) copy-start(f32[1024]{0:T(1024)} %param.16) | copy-start | bytes 12292
  2.0 10.0 %copy-start.6 = (f32[2,4096]{1,0:T(2,128)S(1)}, f32[2,4096]{1,0:T(2,128)}, u32[]{:S(2)}) copy-start(f32[2,4096]{1,0:T(2,128)} %param.13) | copy-start | bytes 98308
  2.0 10.0 %copy-start.5 = (s32[32,128]{1,0:T(8,128)S(1)}, s32[32,128]{1,0:T(8,128)}, u32[]{:S(2)}) copy-start(s32[32,128]{1,0:T(8,128)} %cell.3) | copy-start | bytes 49156
  2.5 29.6 %collective-permute-start = (f32[960,128]{1,0:T(8,128)S(1)}, f32[960,128]{1,0:T(8,128)S(1)}, u32[]{:S(2)}, u32[]{:S(2)}) collective-permute-start(f32[960,128]{1,0:T(8,128)S(1)} %get-tuple-element.13), channel_id=1, source_target_pairs={{0,16},{16,0},{1,17},{17,1},{2,18},{18,2},{3,19},{19,3},{4,20},{20... | collective-permute-start | bytes 1474568 | tf_op jit(solution)/shard_map/ppermute | solution.py:565
  5.5 13.5 %collective-permute-start.3 = (f32[60,128]{1,0:T(8,128)S(1)}, f32[60,128]{1,0:T(8,128)S(1)}, u32[]{:S(2)}, u32[]{:S(2)}) collective-permute-start(f32[60,128]{1,0:T(8,128)S(1)} %get-tuple-element.17), channel_id=1, source_target_pairs={{0,1},{1,2},{2,3},{3,0},{4,5},{5,6},{6,7},{7,4},{8,9},{9,10},{10,1... | collective-permute-start | bytes 92168 | tf_op jit(solution)/shard_map/ppermute | solution.py:231
  5.5 13.6 %collective-permute-start.4 = (f32[60,128]{1,0:T(8,128)S(1)}, f32[60,128]{1,0:T(8,128)S(1)}, u32[]{:S(2)}, u32[]{:S(2)}) collective-permute-start(f32[60,128]{1,0:T(8,128)S(1)} %get-tuple-element.18), channel_id=1, source_target_pairs={{1,0},{2,1},{3,2},{0,3},{5,4},{6,5},{7,6},{4,7},{9,8},{10,9},{11,1... | collective-permute-start | bytes 92168 | tf_op jit(solution)/shard_map/ppermute | solution.py:231
  7.3 18.3 %collective-permute-start.1 = (f32[240,128]{1,0:T(8,128)S(1)}, f32[240,128]{1,0:T(8,128)S(1)}, u32[]{:S(2)}, u32[]{:S(2)}) collective-permute-start(f32[240,128]{1,0:T(8,128)S(1)} %get-tuple-element.14), channel_id=1, source_target_pairs={{0,4},{4,8},{8,12},{12,0},{1,5},{5,9},{9,13},{13,1},{2,6},{6,10},{... | collective-permute-start | bytes 368648 | tf_op jit(solution)/shard_map/ppermute | solution.py:231
  8.8 16.7 %collective-permute-start.2 = (f32[240,128]{1,0:T(8,128)S(1)}, f32[240,128]{1,0:T(8,128)S(1)}, u32[]{:S(2)}, u32[]{:S(2)}) collective-permute-start(f32[240,128]{1,0:T(8,128)S(1)} %get-tuple-element.15), channel_id=1, source_target_pairs={{4,0},{8,4},{12,8},{0,12},{5,1},{9,5},{13,9},{1,13},{6,2},{10,6},{... | collective-permute-start | bytes 368648 | tf_op jit(solution)/shard_map/ppermute | solution.py:231
  25.5 6.6 %copy-start.3 = (f32[5,16,32,128]{3,2,1,0:T(8,128)S(1)}, f32[5,16,32,128]{3,2,1,0:T(8,128)}, u32[]{:S(2)}) copy-start(f32[5,16,32,128]{3,2,1,0:T(8,128)} %param.9) | copy-start | bytes 3932164
  25.6 13.7 %copy-start.4 = (bf16[256,512]{1,0:T(8,128)(2,1)S(1)}, bf16[256,512]{1,0:T(8,128)(2,1)}, u32[]{:S(2)}) copy-start(bf16[256,512]{1,0:T(8,128)(2,1)} %constant.124.clone.table) | copy-start | bytes 786436
  32.2 7.1 %copy-start.2 = (bf16[4096,512]{1,0:T(8,128)(2,1)S(1)}, bf16[4096,512]{1,0:T(8,128)(2,1)}, u32[]{:S(2)}) copy-start(bf16[4096,512]{1,0:T(8,128)(2,1)} %rec.1) | copy-start | bytes 12582916
  51.9 2.7 %collective-permute-start.5 = (f32[2,2,128,128]{3,2,1,0:T(8,128)S(1)}, f32[2,2,128,128]{3,2,1,0:T(8,128)S(1)}, u32[]{:S(2)}, u32[]{:S(2)}) collective-permute-start(f32[2,2,128,128]{3,2,1,0:T(8,128)S(1)} %dynamic-slice_bitcast_fusion.1), channel_id=1, source_target_pairs={{0,1},{1,0},{2,3},{3,2},{4,5},{5,4},{6,7},{7,6},{8,9},{9,8},{10,11... | collective-permute-start | bytes 786440 | tf_op jit(solution)/shard_map/ppermute | solution.py:565
  54.7 5.1 %collective-permute-start.6 = (f32[1,2,128,128]{3,2,1,0:T(8,128)S(1)}, f32[1,2,128,128]{3,2,1,0:T(8,128)S(1)}, u32[]{:S(2)}, u32[]{:S(2)}) collective-permute-start(f32[1,2,128,128]{3,2,1,0:T(8,128)S(1)} %constant_dynamic-slice_fusion.1), channel_id=1, source_target_pairs={{0,2},{1,3},{2,0},{3,1},{4,6},{5,7},{6,4},{7,5},{8,10},{9,11},{10,... | collective-permute-start | bytes 393224 | tf_op jit(solution)/shard_map/ppermute | solution.py:565
  61.6 1.6 %collective-permute-start.11 = (f32[2,2,128,128]{3,2,1,0:T(8,128)S(1)}, f32[2,2,128,128]{3,2,1,0:T(8,128)S(1)}, u32[]{:S(2)}, u32[]{:S(2)}) collective-permute-start(f32[2,2,128,128]{3,2,1,0:T(8,128)S(1)} %dynamic-slice_bitcast_fusion), channel_id=1, source_target_pairs={{0,1},{1,0},{2,3},{3,2},{4,5},{5,4},{6,7},{7,6},{8,9},{9,8},{10,11... | collective-permute-start | bytes 786440 | tf_op jit(solution)/shard_map/ppermute | solution.py:565
  63.3 5.6 %collective-permute-start.12 = (f32[1,2,128,128]{3,2,1,0:T(8,128)S(1)}, f32[1,2,128,128]{3,2,1,0:T(8,128)S(1)}, u32[]{:S(2)}, u32[]{:S(2)}) collective-permute-start(f32[1,2,128,128]{3,2,1,0:T(8,128)S(1)} %constant_dynamic-slice_fusion), channel_id=1, source_target_pairs={{0,2},{1,3},{2,0},{3,1},{4,6},{5,7},{6,4},{7,5},{8,10},{9,11},{10,... | collective-permute-start | bytes 393224 | tf_op jit(solution)/shard_map/ppermute | solution.py:565
  63.4 5.6 %collective-permute-start.7 = (f32[1,2,64,128]{3,2,1,0:T(8,128)S(1)}, f32[1,2,64,128]{3,2,1,0:T(8,128)S(1)}, u32[]{:S(2)}, u32[]{:S(2)}) collective-permute-start(f32[1,2,64,128]{3,2,1,0:T(8,128)S(1)} %dynamic-slice_bitcast_fusion.3), channel_id=1, source_target_pairs={{0,16},{16,0},{1,17},{17,1},{2,18},{18,2},{3,19},{19,3},{4,20},{20... | collective-permute-start | bytes 196616 | tf_op jit(solution)/shard_map/ppermute | solution.py:565
  69.0 4.3 %collective-permute-start.13 = (f32[1,2,64,128]{3,2,1,0:T(8,128)S(1)}, f32[1,2,64,128]{3,2,1,0:T(8,128)S(1)}, u32[]{:S(2)}, u32[]{:S(2)}) collective-permute-start(f32[1,2,64,128]{3,2,1,0:T(8,128)S(1)} %dynamic-slice_bitcast_fusion.2), channel_id=1, source_target_pairs={{0,16},{16,0},{1,17},{17,1},{2,18},{18,2},{3,19},{19,3},{4,20},{20... | collective-permute-start | bytes 196616 | tf_op jit(solution)/shard_map/ppermute | solution.py:565
  69.1 4.3 %collective-permute-start.8 = (f32[1,2,64,128]{3,2,1,0:T(8,128)S(1)}, f32[1,2,64,128]{3,2,1,0:T(8,128)S(1)}, u32[]{:S(2)}, u32[]{:S(2)}) collective-permute-start(f32[1,2,64,128]{3,2,1,0:T(8,128)S(1)} %bitcast_add_fusion.3), channel_id=1, source_target_pairs={{0,4},{4,0},{8,12},{12,8},{1,5},{5,1},{9,13},{13,9},{2,6},{6,2},{1... | collective-permute-start | bytes 196616 | tf_op jit(solution)/shard_map/ppermute | solution.py:565
  73.3 5.2 %collective-permute-start.14 = (f32[1,2,64,128]{3,2,1,0:T(8,128)S(1)}, f32[1,2,64,128]{3,2,1,0:T(8,128)S(1)}, u32[]{:S(2)}, u32[]{:S(2)}) collective-permute-start(f32[1,2,64,128]{3,2,1,0:T(8,128)S(1)} %bitcast_add_fusion.2), channel_id=1, source_target_pairs={{0,4},{4,0},{8,12},{12,8},{1,5},{5,1},{9,13},{13,9},{2,6},{6,2},{1... | collective-permute-start | bytes 196616 | tf_op jit(solution)/shard_map/ppermute | solution.py:565
  73.4 9.0 %collective-permute-start.9 = (f32[1,2,64,128]{3,2,1,0:T(8,128)S(1)}, f32[1,2,64,128]{3,2,1,0:T(8,128)S(1)}, u32[]{:S(2)}, u32[]{:S(2)}) collective-permute-start(f32[1,2,64,128]{3,2,1,0:T(8,128)S(1)} %add.90), channel_id=1, source_target_pairs={{0,8},{4,12},{8,0},{12,4},{1,9},{5,13},{9,1},{13,5},{2,10},{6,14},... | collective-permute-start | bytes 196616 | tf_op jit(solution)/shard_map/ppermute | solution.py:565
  78.5 5.2 %collective-permute-start.15 = (f32[1,2,64,128]{3,2,1,0:T(8,128)S(1)}, f32[1,2,64,128]{3,2,1,0:T(8,128)S(1)}, u32[]{:S(2)}, u32[]{:S(2)}) collective-permute-start(f32[1,2,64,128]{3,2,1,0:T(8,128)S(1)} %add.95), channel_id=1, source_target_pairs={{0,8},{4,12},{8,0},{12,4},{1,9},{5,13},{9,1},{13,5},{2,10},{6,14},... | collective-permute-start | bytes 196616 | tf_op jit(solution)/shard_map/ppermute | solution.py:565
  82.4 4.3 %collective-permute-start.10 = (f32[1,2,64,128]{3,2,1,0:T(8,128)S(1)}, f32[1,2,64,128]{3,2,1,0:T(8,128)S(1)}, u32[]{:S(2)}, u32[]{:S(2)}) collective-permute-start(f32[1,2,64,128]{3,2,1,0:T(8,128)S(1)} %add.91), channel_id=1, source_target_pairs={{0,16},{16,0},{1,17},{17,1},{2,18},{18,2},{3,19},{19,3},{4,20},{20... | collective-permute-start | bytes 196616 | tf_op jit(solution)/shard_map/ppermute | solution.py:565
  83.7 4.3 %collective-permute-start.16 = (f32[1,2,64,128]{3,2,1,0:T(8,128)S(1)}, f32[1,2,64,128]{3,2,1,0:T(8,128)S(1)}, u32[]{:S(2)}, u32[]{:S(2)}) collective-permute-start(f32[1,2,64,128]{3,2,1,0:T(8,128)S(1)} %add.96), channel_id=1, source_target_pairs={{0,16},{16,0},{1,17},{17,1},{2,18},{18,2},{3,19},{19,3},{4,20},{20... | collective-permute-start | bytes 196616 | tf_op jit(solution)/shard_map/ppermute | solution.py:565
  (2 other events, 7.8 us)

commit v7 on v6

--- a/solution.py
+++ b/solution.py
@@ -11,6 +11,7 @@
 
 FREQS = 128
 BATCH = 4
+WIDE = 8
 CHUNKS = 2
 PARTS = 3
 NT = (((1,), (1,)), ((), ()))
@@ -409,8 +410,8 @@
 def spectra_kernel(live, dens, rec, cell, table, sp, dens3, onehot, src):
     slots, bp = cell.shape
     rows = dens.shape[0] // 2
-    total = (live[0] + BATCH - 1) // BATCH
-    span = BATCH * bp
+    total = (live[0] + WIDE - 1) // WIDE
+    span = WIDE * bp
 
     for h in range(2):
         d = dens[pl.ds(h, rows, stride=2), :]
@@ -424,8 +425,8 @@
 
     def group(g, _):
         lows = []
-        for j in range(BATCH):
-            cells = cell[pl.ds(g * BATCH + j, 1), :].astype(jnp.float32)
+        for j in range(WIDE):
+            cells = cell[pl.ds(g * WIDE + j, 1), :].astype(jnp.float32)
             col = jnp.transpose(jnp.broadcast_to(cells, (128, 128)))
             high = jnp.floor(col * (1.0 / 256.0))
             low = col - 256.0 * high
@@ -433,21 +434,22 @@
             for h in range(rows // 128):
                 hit = jnp.where(high == lane + float(128 * h), 1.0, 0.0).astype(jnp.bfloat16)
                 onehot[j * bp : (j + 1) * bp, h * 128 : (h + 1) * 128] = hit
-        hot = onehot[...]
-        picked = jnp.dot(hot, dens3[0], preferred_element_type=jnp.float32)
-        picked = picked + jnp.dot(hot, dens3[1], preferred_element_type=jnp.float32)
-        picked = picked + jnp.dot(hot, dens3[2], preferred_element_type=jnp.float32)
-        for j in range(BATCH):
-            own = picked[j * bp : (j + 1) * bp, :]
+        for j in range(WIDE):
+            if j % 2 == 0:
+                hot = onehot[j * bp : (j + 2) * bp, :]
+                picked = jnp.dot(hot, dens3[0], preferred_element_type=jnp.float32)
+                picked = picked + jnp.dot(hot, dens3[1], preferred_element_type=jnp.float32)
+                picked = picked + jnp.dot(hot, dens3[2], preferred_element_type=jnp.float32)
+            own = picked[j % 2 * bp : (j % 2 + 1) * bp, :]
             found = jnp.where(lows[j] == lane, own[:, 0:128], 0.0) + jnp.where(lows[j] == lane + 128.0, own[:, 128:256], 0.0)
             sampled = jnp.sum(found, axis=1, keepdims=True)
             record = rec[pl.ds(pl.multiple_of(g * span + j * bp, bp), bp), :].astype(jnp.float32)
             src[j * bp : (j + 1) * bp, :] = (record * sampled).astype(jnp.bfloat16)
-        for j in range(0, BATCH, 2):
+        for j in range(0, WIDE, 2):
             both = lax.dot_general(table[...], src[j * bp : (j + 2) * bp, :], NT, preferred_element_type=jnp.float32)
             both = both.astype(jnp.bfloat16)
-            sp[g * BATCH + j] = both[:, 0:bp]
-            sp[g * BATCH + j + 1] = both[:, bp : 2 * bp]
+            sp[g * WIDE + j] = both[:, 0:bp]
+            sp[g * WIDE + j + 1] = both[:, bp : 2 * bp]
         return 0
 
     lax.fori_loop(0, total, group, 0)
@@ -472,11 +474,11 @@
         out_specs=vm,
         scratch_shapes=[
             pltpu.VMEM((3, rows // 2, 256), jnp.bfloat16),
-            pltpu.VMEM((BATCH * bp, rows // 2), jnp.bfloat16),
-            pltpu.VMEM((BATCH * bp, samples), jnp.bfloat16),
+            pltpu.VMEM((WIDE * bp, rows // 2), jnp.bfloat16),
+            pltpu.VMEM((WIDE * bp, samples), jnp.bfloat16),
         ],
         name="spectra",
-        compiler_params=pltpu.CompilerParams(vmem_limit_bytes=3 * 1024 * 1024),
+        compiler_params=pltpu.CompilerParams(vmem_limit_bytes=7 * 1024 * 1024),
     )(live, dens, rec, cell, table)
 
 

time: 88.9 us -> 85.3 us (0.960)
  starting transfers between devices: 17.9 us -> 40.1 us
  Pallas kernels: 46.4 us -> 25.9 us
  waiting for transfers between devices: 20.2 us -> 15.3 us
    ppermute x13, starting transfers between devices: 12.3 us -> 34.5 us  [swap(): return lax.ppermute(value, axis, [(i, i ^ bit) for i in range(size)])]
    pallas_call x4, Pallas kernels: 11.9 us -> 2.18 us  [observe(): pl.pallas_call(functools.partial(observe_kernel, chunk=chunk, part=part,...]
    pallas_call x1, Pallas kernels: 6.91 us -> 1.12 us  [spectra(): pl.pallas_call(spectra_kernel, out_shape=jax.ShapeDtypeStruct((slots, k2,...]
    pallas_call x1, Pallas kernels: 7.1 us -> 2.02 us  [weights(): pl.pallas_call(functools.partial(weights_kernel, sizes=sizes, counts=coun...]
    ppermute x13, waiting for transfers between devices: 20.2 us -> 15.3 us  [swap(): return lax.ppermute(value, axis, [(i, i ^ bit) for i in range(size)])]
  transfers between devices with their start and end apart: 17 -> 17, of which waited for: 8 -> 8; matrix products, arithmetic and copies ran while one was open for 0% -> 0% of each run, Pallas kernels for 28% -> 19%
where the time goes in v7:
time: 85.3 us; the launch traced here: 85.4 us
  starting transfers between devices  40.1 us (47%)
  Pallas kernels  25.9 us (30%)
  waiting for transfers between devices  15.3 us (18%)
  between operations  1.68 us (2%)
  local copies, waits for them, and re-layouts  1.49 us (2%)
  other arithmetic  1 us (1%)
    ppermute x13, starting transfers between devices, swap(): return lax.ppermute(value, axis, [(i, i ^ bit) for i in range(size)])  34.5 us
    pallas_call x3, Pallas kernels, line_call(): pl.pallas_call(kernel, out_shape=[jax.ShapeDtypeStruct(shape, jnp.float32...  20 us
    ppermute x13, waiting for transfers between devices, swap(): return lax.ppermute(value, axis, [(i, i ^ bit) for i in range(size)])  15.3 us
    ppermute x4, starting transfers between devices, neighbours(): return (lax.ppermute(last, axis, up), lax.ppermute(first, axis, down))  5.57 us
    pallas_call x4, Pallas kernels, observe(): pl.pallas_call(functools.partial(observe_kernel, chunk=chunk, part=part,...  2.18 us
    pallas_call x1, Pallas kernels, weights(): pl.pallas_call(functools.partial(weights_kernel, sizes=sizes, counts=coun...  2.02 us
  transfers between devices with their start and end apart: 17, of which 8 were waited for; matrix products, arithmetic and copies ran while one was open for 0% of the time, Pallas kernels for 19%

profile of v7, /device:TPU:0, one launch (start us, length us, event | category | flops | bytes accessed | tf_op | source)
XLA Modules:
  0.0 85.4 jit_solution(6383806097370983408)
XLA Ops:
  0.6 1.3 %copy-done = f32[5,16,32,128]{3,2,1,0:T(8,128)S(1)} copy-done((f32[5,16,32,128]{3,2,1,0:T(8,128)S(1)}, f32[5,16,32,128]{3,2,1,0:T(8,128)}, u32[]{:S(2)}) %copy-start) | copy-done | bytes 1310744
  2.5 3.0 %collective-permute-start = (f32[960,128]{1,0:T(8,128)S(1)}, f32[960,128]{1,0:T(8,128)S(1)}, u32[]{:S(2)}, u32[]{:S(2)}) collective-permute-start(f32[960,128]{1,0:T(8,128)S(1)} %get-tuple-element.13), channel_id=1, source_target_pairs={{0,16},{16,0},{1,17},{17,1},{2,18},{18,2},{3,19},{19,3},{4,20},{20... | collective-permute-start | bytes 1474568 | tf_op jit(solution)/shard_map/ppermute | solution.py:567
  5.5 1.7 %collective-permute-start.4 = (f32[60,128]{1,0:T(8,128)S(1)}, f32[60,128]{1,0:T(8,128)S(1)}, u32[]{:S(2)}, u32[]{:S(2)}) collective-permute-start(f32[60,128]{1,0:T(8,128)S(1)} %get-tuple-element.18), channel_id=1, source_target_pairs={{1,0},{2,1},{3,2},{0,3},{5,4},{6,5},{7,6},{4,7},{9,8},{10,9},{11,1... | collective-permute-start | bytes 92168 | tf_op jit(solution)/shard_map/ppermute | solution.py:232
  7.3 1.6 %collective-permute-start.1 = (f32[240,128]{1,0:T(8,128)S(1)}, f32[240,128]{1,0:T(8,128)S(1)}, u32[]{:S(2)}, u32[]{:S(2)}) collective-permute-start(f32[240,128]{1,0:T(8,128)S(1)} %get-tuple-element.14), channel_id=1, source_target_pairs={{0,4},{4,8},{8,12},{12,0},{1,5},{5,9},{9,13},{13,1},{2,6},{6,10},{... | collective-permute-start | bytes 368648 | tf_op jit(solution)/shard_map/ppermute | solution.py:232
  8.8 2.2 %collective-permute-start.2 = (f32[240,128]{1,0:T(8,128)S(1)}, f32[240,128]{1,0:T(8,128)S(1)}, u32[]{:S(2)}, u32[]{:S(2)}) collective-permute-start(f32[240,128]{1,0:T(8,128)S(1)} %get-tuple-element.15), channel_id=1, source_target_pairs={{4,0},{8,4},{12,8},{0,12},{5,1},{9,5},{13,9},{1,13},{6,2},{10,6},{... | collective-permute-start | bytes 368648 | tf_op jit(solution)/shard_map/ppermute | solution.py:232
  12.0 2.0 %weights.1 = (bf16[32768,128]{1,0:T(8,128)(2,1)S(1)}, f32[3,32,128]{2,1,0:T(8,128)S(1)}, f32[3,8,128]{2,1,0:T(8,128)S(1)}) custom-call(s32[1]{0:T(128)S(6)} %copy.23.live, s32[3]{0:T(128)S(1)} %pad_add_fusion.corner, s32[32,128]{1,0:T(8,128)S(1)} %copy-done.5, f32[2,32,128]{2,1,0:T(8,128)S(1)} %bitcast.52, f32[3,8,128]{2,1,0:T(8,128)S(1)} %bitcast.53), custom_call_target="tpu_custom_call" | custom-call | tf_op jit(solution)/shard_map/weights/pallas_call | solution.py:387
  14.0 6.4 %along_z.1.start = f32[2560,128]{1,0:T(8,128)S(1)} custom-call(f32[2560,128]{1,0:T(8,128)S(1)} %get-tuple-element.16.turned, f32[60,128]{1,0:T(8,128)S(1)} %collective-permute-done.3.left, f32[60,128]{1,0:T(8,128)S(1)} %collective-permute-done.4.right), custom_call_target="tpu_custom_call" | custom-call | tf_op jit(solution)/shard_map/along_z/pallas_call | solution.py:211
  20.5 6.5 %along_y.1.start = f32[2560,128]{1,0:T(8,128)S(1)} custom-call(f32[2560,128]{1,0:T(8,128)S(1)} %bitcast.43, f32[240,128]{1,0:T(8,128)S(1)} %collective-permute-done.1.left, f32[240,128]{1,0:T(8,128)S(1)} %collective-permute-done.2.right, f32[2560,128]{1,0:T(8,128)S(1)} %along_z.1.start), custom_call_target="tpu_custom_call" | custom-call | tf_op jit(solution)/shard_map/along_y/pallas_call | solution.py:211
  27.1 7.1 %along_x.1 = (f32[2560,128]{1,0:T(8,128)}, f32[512,128]{1,0:T(8,128)S(1)}) custom-call(f32[2560,128]{1,0:T(8,128)S(1)} %bitcast.44, f32[960,128]{1,0:T(8,128)S(1)} %collective-permute-done.ends, f32[2560,128]{1,0:T(8,128)S(1)} %along_y.1.start, f32[2560,128]{1,0:T(8,128)S(1)} %bitcast.45), custom_call_target="tpu_custom_call" | custom-call | tf_op jit(solution)/shard_map/along_x/pallas_call | solution.py:211
  34.2 1.1 %spectra.1.sp = bf16[32,256,128]{2,1,0:T(8,128)(2,1)S(1)} custom-call(s32[1]{0:T(128)S(6)} %copy.23.live, f32[512,128]{1,0:T(8,128)S(1)} %get-tuple-element.21.dens, bf16[4096,512]{1,0:T(8,128)(2,1)S(1)} %copy-done.2, s32[32,128]{1,0:T(8,128)S(1)} %copy-done.5, bf16[256,512]{1,0:T(8,128)(2,1)S(1)} %copy-done.4), custom_call_target="tpu_custom_call" | custom-call | tf_op jit(solution)/shard_map/spectra/pallas_call | solution.py:464
  38.0 3.2 %collective-permute-start.6 = (f32[1,2,128,128]{3,2,1,0:T(8,128)S(1)}, f32[1,2,128,128]{3,2,1,0:T(8,128)S(1)}, u32[]{:S(2)}, u32[]{:S(2)}) collective-permute-start(f32[1,2,128,128]{3,2,1,0:T(8,128)S(1)} %constant_dynamic-slice_fusion.1), channel_id=1, source_target_pairs={{0,2},{1,3},{2,0},{3,1},{4,6},{5,7},{6,4},{7,5},{8,10},{9,11},{10,... | collective-permute-start | bytes 393224 | tf_op jit(solution)/shard_map/ppermute | solution.py:567
  41.3 3.8 %collective-permute-done.6 = f32[1,2,128,128]{3,2,1,0:T(8,128)S(1)} collective-permute-done((f32[1,2,128,128]{3,2,1,0:T(8,128)S(1)}, f32[1,2,128,128]{3,2,1,0:T(8,128)S(1)}, u32[]{:S(2)}, u32[]{:S(2)}) %collective-permute-start.6) | collective-permute-done | bytes 131104 | tf_op jit(solution)/shard_map/ppermute | solution.py:567
  45.4 1.5 %collective-permute-done.11 = f32[2,2,128,128]{3,2,1,0:T(8,128)S(1)} collective-permute-done((f32[2,2,128,128]{3,2,1,0:T(8,128)S(1)}, f32[2,2,128,128]{3,2,1,0:T(8,128)S(1)}, u32[]{:S(2)}, u32[]{:S(2)}) %collective-permute-start.11) | collective-permute-done | bytes 262176 | tf_op jit(solution)/shard_map/ppermute | solution.py:567
  47.0 1.8 %collective-permute-start.12 = (f32[1,2,128,128]{3,2,1,0:T(8,128)S(1)}, f32[1,2,128,128]{3,2,1,0:T(8,128)S(1)}, u32[]{:S(2)}, u32[]{:S(2)}) collective-permute-start(f32[1,2,128,128]{3,2,1,0:T(8,128)S(1)} %constant_dynamic-slice_fusion), channel_id=1, source_target_pairs={{0,2},{1,3},{2,0},{3,1},{4,6},{5,7},{6,4},{7,5},{8,10},{9,11},{10,... | collective-permute-start | bytes 393224 | tf_op jit(solution)/shard_map/ppermute | solution.py:567
  48.8 8.4 %collective-permute-start.7 = (f32[1,2,64,128]{3,2,1,0:T(8,128)S(1)}, f32[1,2,64,128]{3,2,1,0:T(8,128)S(1)}, u32[]{:S(2)}, u32[]{:S(2)}) collective-permute-start(f32[1,2,64,128]{3,2,1,0:T(8,128)S(1)} %dynamic-slice_bitcast_fusion.3), channel_id=1, source_target_pairs={{0,16},{16,0},{1,17},{17,1},{2,18},{18,2},{3,19},{19,3},{4,20},{20... | collective-permute-start | bytes 196616 | tf_op jit(solution)/shard_map/ppermute | solution.py:567
  57.2 3.9 %collective-permute-start.13 = (f32[1,2,64,128]{3,2,1,0:T(8,128)S(1)}, f32[1,2,64,128]{3,2,1,0:T(8,128)S(1)}, u32[]{:S(2)}, u32[]{:S(2)}) collective-permute-start(f32[1,2,64,128]{3,2,1,0:T(8,128)S(1)} %dynamic-slice_bitcast_fusion.2), channel_id=1, source_target_pairs={{0,16},{16,0},{1,17},{17,1},{2,18},{18,2},{3,19},{19,3},{4,20},{20... | collective-permute-start | bytes 196616 | tf_op jit(solution)/shard_map/ppermute | solution.py:567
  61.2 2.1 %collective-permute-done.13 = f32[1,2,64,128]{3,2,1,0:T(8,128)S(1)} collective-permute-done((f32[1,2,64,128]{3,2,1,0:T(8,128)S(1)}, f32[1,2,64,128]{3,2,1,0:T(8,128)S(1)}, u32[]{:S(2)}, u32[]{:S(2)}) %collective-permute-start.13) | collective-permute-done | bytes 65568 | tf_op jit(solution)/shard_map/ppermute | solution.py:567
  63.4 2.4 %collective-permute-done.8 = f32[1,2,64,128]{3,2,1,0:T(8,128)S(1)} collective-permute-done((f32[1,2,64,128]{3,2,1,0:T(8,128)S(1)}, f32[1,2,64,128]{3,2,1,0:T(8,128)S(1)}, u32[]{:S(2)}, u32[]{:S(2)}) %collective-permute-start.8) | collective-permute-done | bytes 65568 | tf_op jit(solution)/shard_map/ppermute | solution.py:567
  65.8 7.4 %collective-permute-start.9 = (f32[1,2,64,128]{3,2,1,0:T(8,128)S(1)}, f32[1,2,64,128]{3,2,1,0:T(8,128)S(1)}, u32[]{:S(2)}, u32[]{:S(2)}) collective-permute-start(f32[1,2,64,128]{3,2,1,0:T(8,128)S(1)} %add.90), channel_id=1, source_target_pairs={{0,8},{4,12},{8,0},{12,4},{1,9},{5,13},{9,1},{13,5},{2,10},{6,14},... | collective-permute-start | bytes 196616 | tf_op jit(solution)/shard_map/ppermute | solution.py:567
  73.3 4.6 %collective-permute-start.15 = (f32[1,2,64,128]{3,2,1,0:T(8,128)S(1)}, f32[1,2,64,128]{3,2,1,0:T(8,128)S(1)}, u32[]{:S(2)}, u32[]{:S(2)}) collective-permute-start(f32[1,2,64,128]{3,2,1,0:T(8,128)S(1)} %add.95), channel_id=1, source_target_pairs={{0,8},{4,12},{8,0},{12,4},{1,9},{5,13},{9,1},{13,5},{2,10},{6,14},... | collective-permute-start | bytes 196616 | tf_op jit(solution)/shard_map/ppermute | solution.py:567
  77.9 1.3 %collective-permute-start.10 = (f32[1,2,64,128]{3,2,1,0:T(8,128)S(1)}, f32[1,2,64,128]{3,2,1,0:T(8,128)S(1)}, u32[]{:S(2)}, u32[]{:S(2)}) collective-permute-start(f32[1,2,64,128]{3,2,1,0:T(8,128)S(1)} %add.91), channel_id=1, source_target_pairs={{0,16},{16,0},{1,17},{17,1},{2,18},{18,2},{3,19},{19,3},{4,20},{20... | collective-permute-start | bytes 196616 | tf_op jit(solution)/shard_map/ppermute | solution.py:567
  79.2 1.1 %collective-permute-done.15 = f32[1,2,64,128]{3,2,1,0:T(8,128)S(1)} collective-permute-done((f32[1,2,64,128]{3,2,1,0:T(8,128)S(1)}, f32[1,2,64,128]{3,2,1,0:T(8,128)S(1)}, u32[]{:S(2)}, u32[]{:S(2)}) %collective-permute-start.15) | collective-permute-done | bytes 65568 | tf_op jit(solution)/shard_map/ppermute | solution.py:567
  81.0 1.2 %collective-permute-done.10 = f32[1,2,64,128]{3,2,1,0:T(8,128)S(1)} collective-permute-done((f32[1,2,64,128]{3,2,1,0:T(8,128)S(1)}, f32[1,2,64,128]{3,2,1,0:T(8,128)S(1)}, u32[]{:S(2)}, u32[]{:S(2)}) %collective-permute-start.10) | collective-permute-done | bytes 65568 | tf_op jit(solution)/shard_map/ppermute | solution.py:567
  82.2 2.5 %collective-permute-done.16 = f32[1,2,64,128]{3,2,1,0:T(8,128)S(1)} collective-permute-done((f32[1,2,64,128]{3,2,1,0:T(8,128)S(1)}, f32[1,2,64,128]{3,2,1,0:T(8,128)S(1)}, u32[]{:S(2)}, u32[]{:S(2)}) %collective-permute-start.16) | collective-permute-done | bytes 65568 | tf_op jit(solution)/shard_map/ppermute | solution.py:567
  (64 shorter events, 5.4 us)
Async XLA Ops:
  2.0 9.1 %copy-start.7 = (f32[2,1024]{1,0:T(2,128)S(1)}, f32[2,1024]{1,0:T(2,128)}, u32[]{:S(2)}) copy-start(f32[2,1024]{1,0:T(2,128)} %param.15) | copy-start | bytes 24580
  2.0 9.2 %copy-start.8 = (f32[1024]{0:T(1024)S(1)}, f32[1024]{0:T(1024)}, u32[]{:S(2)}) copy-start(f32[1024]{0:T(1024)} %param.16) | copy-start | bytes 12292
  2.0 10.0 %copy-start.6 = (f32[2,4096]{1,0:T(2,128)S(1)}, f32[2,4096]{1,0:T(2,128)}, u32[]{:S(2)}) copy-start(f32[2,4096]{1,0:T(2,128)} %param.13) | copy-start | bytes 98308
  2.0 10.0 %copy-start.5 = (s32[32,128]{1,0:T(8,128)S(1)}, s32[32,128]{1,0:T(8,128)}, u32[]{:S(2)}) copy-start(s32[32,128]{1,0:T(8,128)} %cell.3) | copy-start | bytes 49156
  2.5 24.6 %collective-permute-start = (f32[960,128]{1,0:T(8,128)S(1)}, f32[960,128]{1,0:T(8,128)S(1)}, u32[]{:S(2)}, u32[]{:S(2)}) collective-permute-start(f32[960,128]{1,0:T(8,128)S(1)} %get-tuple-element.13), channel_id=1, source_target_pairs={{0,16},{16,0},{1,17},{17,1},{2,18},{18,2},{3,19},{19,3},{4,20},{20... | collective-permute-start | bytes 1474568 | tf_op jit(solution)/shard_map/ppermute | solution.py:567
  5.5 8.5 %collective-permute-start.3 = (f32[60,128]{1,0:T(8,128)S(1)}, f32[60,128]{1,0:T(8,128)S(1)}, u32[]{:S(2)}, u32[]{:S(2)}) collective-permute-start(f32[60,128]{1,0:T(8,128)S(1)} %get-tuple-element.17), channel_id=1, source_target_pairs={{0,1},{1,2},{2,3},{3,0},{4,5},{5,6},{6,7},{7,4},{8,9},{9,10},{10,1... | collective-permute-start | bytes 92168 | tf_op jit(solution)/shard_map/ppermute | solution.py:232
  5.5 8.5 %collective-permute-start.4 = (f32[60,128]{1,0:T(8,128)S(1)}, f32[60,128]{1,0:T(8,128)S(1)}, u32[]{:S(2)}, u32[]{:S(2)}) collective-permute-start(f32[60,128]{1,0:T(8,128)S(1)} %get-tuple-element.18), channel_id=1, source_target_pairs={{1,0},{2,1},{3,2},{0,3},{5,4},{6,5},{7,6},{4,7},{9,8},{10,9},{11,1... | collective-permute-start | bytes 92168 | tf_op jit(solution)/shard_map/ppermute | solution.py:232
  7.3 13.2 %collective-permute-start.1 = (f32[240,128]{1,0:T(8,128)S(1)}, f32[240,128]{1,0:T(8,128)S(1)}, u32[]{:S(2)}, u32[]{:S(2)}) collective-permute-start(f32[240,128]{1,0:T(8,128)S(1)} %get-tuple-element.14), channel_id=1, source_target_pairs={{0,4},{4,8},{8,12},{12,0},{1,5},{5,9},{9,13},{13,1},{2,6},{6,10},{... | collective-permute-start | bytes 368648 | tf_op jit(solution)/shard_map/ppermute | solution.py:232
  8.8 11.6 %collective-permute-start.2 = (f32[240,128]{1,0:T(8,128)S(1)}, f32[240,128]{1,0:T(8,128)S(1)}, u32[]{:S(2)}, u32[]{:S(2)}) collective-permute-start(f32[240,128]{1,0:T(8,128)S(1)} %get-tuple-element.15), channel_id=1, source_target_pairs={{4,0},{8,4},{12,8},{0,12},{5,1},{9,5},{13,9},{1,13},{6,2},{10,6},{... | collective-permute-start | bytes 368648 | tf_op jit(solution)/shard_map/ppermute | solution.py:232
  20.5 6.6 %copy-start.3 = (f32[5,16,32,128]{3,2,1,0:T(8,128)S(1)}, f32[5,16,32,128]{3,2,1,0:T(8,128)}, u32[]{:S(2)}) copy-start(f32[5,16,32,128]{3,2,1,0:T(8,128)} %param.9) | copy-start | bytes 3932164
  20.5 13.7 %copy-start.4 = (bf16[256,512]{1,0:T(8,128)(2,1)S(1)}, bf16[256,512]{1,0:T(8,128)(2,1)}, u32[]{:S(2)}) copy-start(bf16[256,512]{1,0:T(8,128)(2,1)} %constant.124.clone.table) | copy-start | bytes 786436
  27.1 7.1 %copy-start.2 = (bf16[4096,512]{1,0:T(8,128)(2,1)S(1)}, bf16[4096,512]{1,0:T(8,128)(2,1)}, u32[]{:S(2)}) copy-start(bf16[4096,512]{1,0:T(8,128)(2,1)} %rec.1) | copy-start | bytes 12582916
  36.3 1.6 %collective-permute-start.5 = (f32[2,2,128,128]{3,2,1,0:T(8,128)S(1)}, f32[2,2,128,128]{3,2,1,0:T(8,128)S(1)}, u32[]{:S(2)}, u32[]{:S(2)}) collective-permute-start(f32[2,2,128,128]{3,2,1,0:T(8,128)S(1)} %dynamic-slice_bitcast_fusion.1), channel_id=1, source_target_pairs={{0,1},{1,0},{2,3},{3,2},{4,5},{5,4},{6,7},{7,6},{8,9},{9,8},{10,11... | collective-permute-start | bytes 786440 | tf_op jit(solution)/shard_map/ppermute | solution.py:567
  38.0 7.0 %collective-permute-start.6 = (f32[1,2,128,128]{3,2,1,0:T(8,128)S(1)}, f32[1,2,128,128]{3,2,1,0:T(8,128)S(1)}, u32[]{:S(2)}, u32[]{:S(2)}) collective-permute-start(f32[1,2,128,128]{3,2,1,0:T(8,128)S(1)} %constant_dynamic-slice_fusion.1), channel_id=1, source_target_pairs={{0,2},{1,3},{2,0},{3,1},{4,6},{5,7},{6,4},{7,5},{8,10},{9,11},{10,... | collective-permute-start | bytes 393224 | tf_op jit(solution)/shard_map/ppermute | solution.py:567
  45.3 1.6 %collective-permute-start.11 = (f32[2,2,128,128]{3,2,1,0:T(8,128)S(1)}, f32[2,2,128,128]{3,2,1,0:T(8,128)S(1)}, u32[]{:S(2)}, u32[]{:S(2)}) collective-permute-start(f32[2,2,128,128]{3,2,1,0:T(8,128)S(1)} %dynamic-slice_bitcast_fusion), channel_id=1, source_target_pairs={{0,1},{1,0},{2,3},{3,2},{4,5},{5,4},{6,7},{7,6},{8,9},{9,8},{10,11... | collective-permute-start | bytes 786440 | tf_op jit(solution)/shard_map/ppermute | solution.py:567
  47.0 10.2 %collective-permute-start.12 = (f32[1,2,128,128]{3,2,1,0:T(8,128)S(1)}, f32[1,2,128,128]{3,2,1,0:T(8,128)S(1)}, u32[]{:S(2)}, u32[]{:S(2)}) collective-permute-start(f32[1,2,128,128]{3,2,1,0:T(8,128)S(1)} %constant_dynamic-slice_fusion), channel_id=1, source_target_pairs={{0,2},{1,3},{2,0},{3,1},{4,6},{5,7},{6,4},{7,5},{8,10},{9,11},{10,... | collective-permute-start | bytes 393224 | tf_op jit(solution)/shard_map/ppermute | solution.py:567
  48.8 12.3 %collective-permute-start.7 = (f32[1,2,64,128]{3,2,1,0:T(8,128)S(1)}, f32[1,2,64,128]{3,2,1,0:T(8,128)S(1)}, u32[]{:S(2)}, u32[]{:S(2)}) collective-permute-start(f32[1,2,64,128]{3,2,1,0:T(8,128)S(1)} %dynamic-slice_bitcast_fusion.3), channel_id=1, source_target_pairs={{0,16},{16,0},{1,17},{17,1},{2,18},{18,2},{3,19},{19,3},{4,20},{20... | collective-permute-start | bytes 196616 | tf_op jit(solution)/shard_map/ppermute | solution.py:567
  57.2 6.1 %collective-permute-start.13 = (f32[1,2,64,128]{3,2,1,0:T(8,128)S(1)}, f32[1,2,64,128]{3,2,1,0:T(8,128)S(1)}, u32[]{:S(2)}, u32[]{:S(2)}) collective-permute-start(f32[1,2,64,128]{3,2,1,0:T(8,128)S(1)} %dynamic-slice_bitcast_fusion.2), channel_id=1, source_target_pairs={{0,16},{16,0},{1,17},{17,1},{2,18},{18,2},{3,19},{19,3},{4,20},{20... | collective-permute-start | bytes 196616 | tf_op jit(solution)/shard_map/ppermute | solution.py:567
  61.1 4.7 %collective-permute-start.8 = (f32[1,2,64,128]{3,2,1,0:T(8,128)S(1)}, f32[1,2,64,128]{3,2,1,0:T(8,128)S(1)}, u32[]{:S(2)}, u32[]{:S(2)}) collective-permute-start(f32[1,2,64,128]{3,2,1,0:T(8,128)S(1)} %bitcast_add_fusion.3), channel_id=1, source_target_pairs={{0,4},{4,0},{8,12},{12,8},{1,5},{5,1},{9,13},{13,9},{2,6},{6,2},{1... | collective-permute-start | bytes 196616 | tf_op jit(solution)/shard_map/ppermute | solution.py:567
  63.4 9.9 %collective-permute-start.14 = (f32[1,2,64,128]{3,2,1,0:T(8,128)S(1)}, f32[1,2,64,128]{3,2,1,0:T(8,128)S(1)}, u32[]{:S(2)}, u32[]{:S(2)}) collective-permute-start(f32[1,2,64,128]{3,2,1,0:T(8,128)S(1)} %bitcast_add_fusion.2), channel_id=1, source_target_pairs={{0,4},{4,0},{8,12},{12,8},{1,5},{5,1},{9,13},{13,9},{2,6},{6,2},{1... | collective-permute-start | bytes 196616 | tf_op jit(solution)/shard_map/ppermute | solution.py:567
  65.8 12.0 %collective-permute-start.9 = (f32[1,2,64,128]{3,2,1,0:T(8,128)S(1)}, f32[1,2,64,128]{3,2,1,0:T(8,128)S(1)}, u32[]{:S(2)}, u32[]{:S(2)}) collective-permute-start(f32[1,2,64,128]{3,2,1,0:T(8,128)S(1)} %add.90), channel_id=1, source_target_pairs={{0,8},{4,12},{8,0},{12,4},{1,9},{5,13},{9,1},{13,5},{2,10},{6,14},... | collective-permute-start | bytes 196616 | tf_op jit(solution)/shard_map/ppermute | solution.py:567
  73.3 7.0 %collective-permute-start.15 = (f32[1,2,64,128]{3,2,1,0:T(8,128)S(1)}, f32[1,2,64,128]{3,2,1,0:T(8,128)S(1)}, u32[]{:S(2)}, u32[]{:S(2)}) collective-permute-start(f32[1,2,64,128]{3,2,1,0:T(8,128)S(1)} %add.95), channel_id=1, source_target_pairs={{0,8},{4,12},{8,0},{12,4},{1,9},{5,13},{9,1},{13,5},{2,10},{6,14},... | collective-permute-start | bytes 196616 | tf_op jit(solution)/shard_map/ppermute | solution.py:567
  77.9 4.3 %collective-permute-start.10 = (f32[1,2,64,128]{3,2,1,0:T(8,128)S(1)}, f32[1,2,64,128]{3,2,1,0:T(8,128)S(1)}, u32[]{:S(2)}, u32[]{:S(2)}) collective-permute-start(f32[1,2,64,128]{3,2,1,0:T(8,128)S(1)} %add.91), channel_id=1, source_target_pairs={{0,16},{16,0},{1,17},{17,1},{2,18},{18,2},{3,19},{19,3},{4,20},{20... | collective-permute-start | bytes 196616 | tf_op jit(solution)/shard_map/ppermute | solution.py:567
  80.3 4.3 %collective-permute-start.16 = (f32[1,2,64,128]{3,2,1,0:T(8,128)S(1)}, f32[1,2,64,128]{3,2,1,0:T(8,128)S(1)}, u32[]{:S(2)}, u32[]{:S(2)}) collective-permute-start(f32[1,2,64,128]{3,2,1,0:T(8,128)S(1)} %add.96), channel_id=1, source_target_pairs={{0,16},{16,0},{1,17},{17,1},{2,18},{18,2},{3,19},{19,3},{4,20},{20... | collective-permute-start | bytes 196616 | tf_op jit(solution)/shard_map/ppermute | solution.py:567
  (2 other events, 7.8 us)

commit v8 on v7

--- a/solution.py
+++ b/solution.py
@@ -13,7 +13,7 @@
 BATCH = 4
 WIDE = 8
 CHUNKS = 2
-PARTS = 3
+PARTS = 2
 NT = (((1,), (1,)), ((), ()))
 
 

time: 85.3 us -> 84.6 us (level)
  waiting for transfers between devices: 15.3 us -> 12.6 us
  starting transfers between devices: 40.1 us -> 42.1 us
    ppermute x13, waiting for transfers between devices: 15.3 us -> 12.6 us  [swap(): return lax.ppermute(value, axis, [(i, i ^ bit) for i in range(size)])]
    ppermute x13, starting transfers between devices: 34.5 us -> 36.5 us  [swap(): return lax.ppermute(value, axis, [(i, i ^ bit) for i in range(size)])]
    pallas_call x4 -> x3, Pallas kernels: 2.18 us -> 2.14 us  [observe(): pl.pallas_call(functools.partial(observe_kernel, chunk=chunk, part=part,...]
where the time goes in v8:
time: 84.6 us; the launch traced here: 84.7 us
  starting transfers between devices  42.1 us (50%)
  Pallas kernels  25.8 us (30%)
  waiting for transfers between devices  12.6 us (15%)
  between operations  1.64 us (2%)
  local copies, waits for them, and re-layouts  1.49 us (2%)
  other arithmetic  1 us (1%)
    ppermute x13, starting transfers between devices, swap(): return lax.ppermute(value, axis, [(i, i ^ bit) for i in range(size)])  36.5 us
    pallas_call x3, Pallas kernels, line_call(): pl.pallas_call(kernel, out_shape=[jax.ShapeDtypeStruct(shape, jnp.float32...  20 us
    ppermute x13, waiting for transfers between devices, swap(): return lax.ppermute(value, axis, [(i, i ^ bit) for i in range(size)])  12.6 us
    ppermute x4, starting transfers between devices, neighbours(): return (lax.ppermute(last, axis, up), lax.ppermute(first, axis, down))  5.57 us
    pallas_call x3, Pallas kernels, observe(): pl.pallas_call(functools.partial(observe_kernel, chunk=chunk, part=part,...  2.14 us
    pallas_call x1, Pallas kernels, weights(): pl.pallas_call(functools.partial(weights_kernel, sizes=sizes, counts=coun...  2 us
  transfers between devices with their start and end apart: 17, of which 8 were waited for; matrix products, arithmetic and copies ran while one was open for 0% of the time, Pallas kernels for 19%

profile of v8, /device:TPU:0, one launch (start us, length us, event | category | flops | bytes accessed | tf_op | source)
XLA Modules:
  0.0 84.7 jit_solution(9291876104514628454)
XLA Ops:
  0.6 1.3 %copy-done = f32[5,16,32,128]{3,2,1,0:T(8,128)S(1)} copy-done((f32[5,16,32,128]{3,2,1,0:T(8,128)S(1)}, f32[5,16,32,128]{3,2,1,0:T(8,128)}, u32[]{:S(2)}) %copy-start) | copy-done | bytes 1310744
  2.5 3.0 %collective-permute-start = (f32[960,128]{1,0:T(8,128)S(1)}, f32[960,128]{1,0:T(8,128)S(1)}, u32[]{:S(2)}, u32[]{:S(2)}) collective-permute-start(f32[960,128]{1,0:T(8,128)S(1)} %get-tuple-element.13), channel_id=1, source_target_pairs={{0,16},{16,0},{1,17},{17,1},{2,18},{18,2},{3,19},{19,3},{4,20},{20... | collective-permute-start | bytes 1474568 | tf_op jit(solution)/shard_map/ppermute | solution.py:567
  5.5 1.7 %collective-permute-start.4 = (f32[60,128]{1,0:T(8,128)S(1)}, f32[60,128]{1,0:T(8,128)S(1)}, u32[]{:S(2)}, u32[]{:S(2)}) collective-permute-start(f32[60,128]{1,0:T(8,128)S(1)} %get-tuple-element.18), channel_id=1, source_target_pairs={{1,0},{2,1},{3,2},{0,3},{5,4},{6,5},{7,6},{4,7},{9,8},{10,9},{11,1... | collective-permute-start | bytes 92168 | tf_op jit(solution)/shard_map/ppermute | solution.py:232
  7.3 1.6 %collective-permute-start.1 = (f32[240,128]{1,0:T(8,128)S(1)}, f32[240,128]{1,0:T(8,128)S(1)}, u32[]{:S(2)}, u32[]{:S(2)}) collective-permute-start(f32[240,128]{1,0:T(8,128)S(1)} %get-tuple-element.14), channel_id=1, source_target_pairs={{0,4},{4,8},{8,12},{12,0},{1,5},{5,9},{9,13},{13,1},{2,6},{6,10},{... | collective-permute-start | bytes 368648 | tf_op jit(solution)/shard_map/ppermute | solution.py:232
  8.8 2.2 %collective-permute-start.2 = (f32[240,128]{1,0:T(8,128)S(1)}, f32[240,128]{1,0:T(8,128)S(1)}, u32[]{:S(2)}, u32[]{:S(2)}) collective-permute-start(f32[240,128]{1,0:T(8,128)S(1)} %get-tuple-element.15), channel_id=1, source_target_pairs={{4,0},{8,4},{12,8},{0,12},{5,1},{9,5},{13,9},{1,13},{6,2},{10,6},{... | collective-permute-start | bytes 368648 | tf_op jit(solution)/shard_map/ppermute | solution.py:232
  11.9 2.0 %weights.1 = (bf16[32768,128]{1,0:T(8,128)(2,1)S(1)}, f32[3,32,128]{2,1,0:T(8,128)S(1)}, f32[3,8,128]{2,1,0:T(8,128)S(1)}) custom-call(s32[1]{0:T(128)S(6)} %copy.23.live, s32[3]{0:T(128)S(1)} %pad_add_fusion.corner, s32[32,128]{1,0:T(8,128)S(1)} %copy-done.5, f32[2,32,128]{2,1,0:T(8,128)S(1)} %bitcast.50, f32[3,8,128]{2,1,0:T(8,128)S(1)} %bitcast.51), custom_call_target="tpu_custom_call" | custom-call | tf_op jit(solution)/shard_map/weights/pallas_call | solution.py:387
  14.0 6.4 %along_z.1.start = f32[2560,128]{1,0:T(8,128)S(1)} custom-call(f32[2560,128]{1,0:T(8,128)S(1)} %get-tuple-element.16.turned, f32[60,128]{1,0:T(8,128)S(1)} %collective-permute-done.3.left, f32[60,128]{1,0:T(8,128)S(1)} %collective-permute-done.4.right), custom_call_target="tpu_custom_call" | custom-call | tf_op jit(solution)/shard_map/along_z/pallas_call | solution.py:211
  20.5 6.5 %along_y.1.start = f32[2560,128]{1,0:T(8,128)S(1)} custom-call(f32[2560,128]{1,0:T(8,128)S(1)} %bitcast.43, f32[240,128]{1,0:T(8,128)S(1)} %collective-permute-done.1.left, f32[240,128]{1,0:T(8,128)S(1)} %collective-permute-done.2.right, f32[2560,128]{1,0:T(8,128)S(1)} %along_z.1.start), custom_call_target="tpu_custom_call" | custom-call | tf_op jit(solution)/shard_map/along_y/pallas_call | solution.py:211
  27.1 7.1 %along_x.1 = (f32[2560,128]{1,0:T(8,128)}, f32[512,128]{1,0:T(8,128)S(1)}) custom-call(f32[2560,128]{1,0:T(8,128)S(1)} %bitcast.44, f32[960,128]{1,0:T(8,128)S(1)} %collective-permute-done.ends, f32[2560,128]{1,0:T(8,128)S(1)} %along_y.1.start, f32[2560,128]{1,0:T(8,128)S(1)} %bitcast.45), custom_call_target="tpu_custom_call" | custom-call | tf_op jit(solution)/shard_map/along_x/pallas_call | solution.py:211
  34.1 1.1 %spectra.1.sp = bf16[32,256,128]{2,1,0:T(8,128)(2,1)S(1)} custom-call(s32[1]{0:T(128)S(6)} %copy.23.live, f32[512,128]{1,0:T(8,128)S(1)} %get-tuple-element.21.dens, bf16[4096,512]{1,0:T(8,128)(2,1)S(1)} %copy-done.2, s32[32,128]{1,0:T(8,128)S(1)} %copy-done.5, bf16[256,512]{1,0:T(8,128)(2,1)S(1)} %copy-done.4), custom_call_target="tpu_custom_call" | custom-call | tf_op jit(solution)/shard_map/spectra/pallas_call | solution.py:464
  35.3 1.0 %observe.3 = f32[4,2,128,128]{3,2,1,0:T(8,128)S(1)} custom-call(s32[1]{0:T(128)S(6)} %copy.23.live, f32[3,32,128]{2,1,0:T(8,128)S(1)} %get-tuple-element.20.centre, bf16[32,256,128]{2,1,0:T(8,128)(2,1)S(1)} %spectra.1.sp, bf16[32768,128]{1,0:T(8,128)(2,1)S(1)} %get-tuple-element.22.wts, f32[3,8,128]{2,1,0:T(8,128)S(1)} %get-tuple-element.23.lis), custom_call_target="tpu_custom_call" | custom-call | flops 4000000000 | bytes 1000000 | tf_op jit(solution)/shard_map/observe/pallas_call | solution.py:553
  38.4 3.9 %collective-permute-start.6 = (f32[1,2,128,128]{3,2,1,0:T(8,128)S(1)}, f32[1,2,128,128]{3,2,1,0:T(8,128)S(1)}, u32[]{:S(2)}, u32[]{:S(2)}) collective-permute-start(f32[1,2,128,128]{3,2,1,0:T(8,128)S(1)} %constant_dynamic-slice_fusion.1), channel_id=1, source_target_pairs={{0,2},{1,3},{2,0},{3,1},{4,6},{5,7},{6,4},{7,5},{8,10},{9,11},{10,... | collective-permute-start | bytes 393224 | tf_op jit(solution)/shard_map/ppermute | solution.py:567
  42.4 1.4 %collective-permute-start.12 = (f32[1,2,128,128]{3,2,1,0:T(8,128)S(1)}, f32[1,2,128,128]{3,2,1,0:T(8,128)S(1)}, u32[]{:S(2)}, u32[]{:S(2)}) collective-permute-start(f32[1,2,128,128]{3,2,1,0:T(8,128)S(1)} %constant_dynamic-slice_fusion), channel_id=1, source_target_pairs={{0,2},{1,3},{2,0},{3,1},{4,6},{5,7},{6,4},{7,5},{8,10},{9,11},{10,... | collective-permute-start | bytes 393224 | tf_op jit(solution)/shard_map/ppermute | solution.py:567
  43.9 2.9 %collective-permute-done.6 = f32[1,2,128,128]{3,2,1,0:T(8,128)S(1)} collective-permute-done((f32[1,2,128,128]{3,2,1,0:T(8,128)S(1)}, f32[1,2,128,128]{3,2,1,0:T(8,128)S(1)}, u32[]{:S(2)}, u32[]{:S(2)}) %collective-permute-start.6) | collective-permute-done | bytes 131104 | tf_op jit(solution)/shard_map/ppermute | solution.py:567
  46.8 6.7 %collective-permute-start.7 = (f32[1,2,64,128]{3,2,1,0:T(8,128)S(1)}, f32[1,2,64,128]{3,2,1,0:T(8,128)S(1)}, u32[]{:S(2)}, u32[]{:S(2)}) collective-permute-start(f32[1,2,64,128]{3,2,1,0:T(8,128)S(1)} %dynamic-slice_bitcast_fusion.3), channel_id=1, source_target_pairs={{0,16},{16,0},{1,17},{17,1},{2,18},{18,2},{3,19},{19,3},{4,20},{20... | collective-permute-start | bytes 196616 | tf_op jit(solution)/shard_map/ppermute | solution.py:567
  53.5 1.9 %collective-permute-start.13 = (f32[1,2,64,128]{3,2,1,0:T(8,128)S(1)}, f32[1,2,64,128]{3,2,1,0:T(8,128)S(1)}, u32[]{:S(2)}, u32[]{:S(2)}) collective-permute-start(f32[1,2,64,128]{3,2,1,0:T(8,128)S(1)} %dynamic-slice_bitcast_fusion.2), channel_id=1, source_target_pairs={{0,16},{16,0},{1,17},{17,1},{2,18},{18,2},{3,19},{19,3},{4,20},{20... | collective-permute-start | bytes 196616 | tf_op jit(solution)/shard_map/ppermute | solution.py:567
  55.9 6.6 %collective-permute-start.8 = (f32[1,2,64,128]{3,2,1,0:T(8,128)S(1)}, f32[1,2,64,128]{3,2,1,0:T(8,128)S(1)}, u32[]{:S(2)}, u32[]{:S(2)}) collective-permute-start(f32[1,2,64,128]{3,2,1,0:T(8,128)S(1)} %bitcast_add_fusion.3), channel_id=1, source_target_pairs={{0,4},{4,0},{8,12},{12,8},{1,5},{5,1},{9,13},{13,9},{2,6},{6,2},{1... | collective-permute-start | bytes 196616 | tf_op jit(solution)/shard_map/ppermute | solution.py:567
  62.5 1.4 %collective-permute-start.14 = (f32[1,2,64,128]{3,2,1,0:T(8,128)S(1)}, f32[1,2,64,128]{3,2,1,0:T(8,128)S(1)}, u32[]{:S(2)}, u32[]{:S(2)}) collective-permute-start(f32[1,2,64,128]{3,2,1,0:T(8,128)S(1)} %bitcast_add_fusion.2), channel_id=1, source_target_pairs={{0,4},{4,0},{8,12},{12,8},{1,5},{5,1},{9,13},{13,9},{2,6},{6,2},{1... | collective-permute-start | bytes 196616 | tf_op jit(solution)/shard_map/ppermute | solution.py:567
  64.9 9.5 %collective-permute-start.9 = (f32[1,2,64,128]{3,2,1,0:T(8,128)S(1)}, f32[1,2,64,128]{3,2,1,0:T(8,128)S(1)}, u32[]{:S(2)}, u32[]{:S(2)}) collective-permute-start(f32[1,2,64,128]{3,2,1,0:T(8,128)S(1)} %add.90), channel_id=1, source_target_pairs={{0,8},{4,12},{8,0},{12,4},{1,9},{5,13},{9,1},{13,5},{2,10},{6,14},... | collective-permute-start | bytes 196616 | tf_op jit(solution)/shard_map/ppermute | solution.py:567
  74.4 1.3 %collective-permute-start.15 = (f32[1,2,64,128]{3,2,1,0:T(8,128)S(1)}, f32[1,2,64,128]{3,2,1,0:T(8,128)S(1)}, u32[]{:S(2)}, u32[]{:S(2)}) collective-permute-start(f32[1,2,64,128]{3,2,1,0:T(8,128)S(1)} %add.95), channel_id=1, source_target_pairs={{0,8},{4,12},{8,0},{12,4},{1,9},{5,13},{9,1},{13,5},{2,10},{6,14},... | collective-permute-start | bytes 196616 | tf_op jit(solution)/shard_map/ppermute | solution.py:567
  75.7 1.0 %collective-permute-done.9 = f32[1,2,64,128]{3,2,1,0:T(8,128)S(1)} collective-permute-done((f32[1,2,64,128]{3,2,1,0:T(8,128)S(1)}, f32[1,2,64,128]{3,2,1,0:T(8,128)S(1)}, u32[]{:S(2)}, u32[]{:S(2)}) %collective-permute-start.9) | collective-permute-done | bytes 65568 | tf_op jit(solution)/shard_map/ppermute | solution.py:567
  77.2 2.4 %collective-permute-done.15 = f32[1,2,64,128]{3,2,1,0:T(8,128)S(1)} collective-permute-done((f32[1,2,64,128]{3,2,1,0:T(8,128)S(1)}, f32[1,2,64,128]{3,2,1,0:T(8,128)S(1)}, u32[]{:S(2)}, u32[]{:S(2)}) %collective-permute-start.15) | collective-permute-done | bytes 65568 | tf_op jit(solution)/shard_map/ppermute | solution.py:567
  79.7 1.3 %collective-permute-done.10 = f32[1,2,64,128]{3,2,1,0:T(8,128)S(1)} collective-permute-done((f32[1,2,64,128]{3,2,1,0:T(8,128)S(1)}, f32[1,2,64,128]{3,2,1,0:T(8,128)S(1)}, u32[]{:S(2)}, u32[]{:S(2)}) %collective-permute-start.10) | collective-permute-done | bytes 65568 | tf_op jit(solution)/shard_map/ppermute | solution.py:567
  81.0 2.9 %collective-permute-done.16 = f32[1,2,64,128]{3,2,1,0:T(8,128)S(1)} collective-permute-done((f32[1,2,64,128]{3,2,1,0:T(8,128)S(1)}, f32[1,2,64,128]{3,2,1,0:T(8,128)S(1)}, u32[]{:S(2)}, u32[]{:S(2)}) %collective-permute-start.16) | collective-permute-done | bytes 65568 | tf_op jit(solution)/shard_map/ppermute | solution.py:567
  (63 shorter events, 5.8 us)
Async XLA Ops:
  2.0 9.1 %copy-start.7 = (f32[2,1024]{1,0:T(2,128)S(1)}, f32[2,1024]{1,0:T(2,128)}, u32[]{:S(2)}) copy-start(f32[2,1024]{1,0:T(2,128)} %param.15) | copy-start | bytes 24580
  2.0 9.2 %copy-start.8 = (f32[1024]{0:T(1024)S(1)}, f32[1024]{0:T(1024)}, u32[]{:S(2)}) copy-start(f32[1024]{0:T(1024)} %param.16) | copy-start | bytes 12292
  2.0 10.0 %copy-start.6 = (f32[2,4096]{1,0:T(2,128)S(1)}, f32[2,4096]{1,0:T(2,128)}, u32[]{:S(2)}) copy-start(f32[2,4096]{1,0:T(2,128)} %param.13) | copy-start | bytes 98308
  2.0 10.0 %copy-start.5 = (s32[32,128]{1,0:T(8,128)S(1)}, s32[32,128]{1,0:T(8,128)}, u32[]{:S(2)}) copy-start(s32[32,128]{1,0:T(8,128)} %cell.3) | copy-start | bytes 49156
  2.5 24.5 %collective-permute-start = (f32[960,128]{1,0:T(8,128)S(1)}, f32[960,128]{1,0:T(8,128)S(1)}, u32[]{:S(2)}, u32[]{:S(2)}) collective-permute-start(f32[960,128]{1,0:T(8,128)S(1)} %get-tuple-element.13), channel_id=1, source_target_pairs={{0,16},{16,0},{1,17},{17,1},{2,18},{18,2},{3,19},{19,3},{4,20},{20... | collective-permute-start | bytes 1474568 | tf_op jit(solution)/shard_map/ppermute | solution.py:567
  5.5 8.4 %collective-permute-start.3 = (f32[60,128]{1,0:T(8,128)S(1)}, f32[60,128]{1,0:T(8,128)S(1)}, u32[]{:S(2)}, u32[]{:S(2)}) collective-permute-start(f32[60,128]{1,0:T(8,128)S(1)} %get-tuple-element.17), channel_id=1, source_target_pairs={{0,1},{1,2},{2,3},{3,0},{4,5},{5,6},{6,7},{7,4},{8,9},{9,10},{10,1... | collective-permute-start | bytes 92168 | tf_op jit(solution)/shard_map/ppermute | solution.py:232
  5.5 8.4 %collective-permute-start.4 = (f32[60,128]{1,0:T(8,128)S(1)}, f32[60,128]{1,0:T(8,128)S(1)}, u32[]{:S(2)}, u32[]{:S(2)}) collective-permute-start(f32[60,128]{1,0:T(8,128)S(1)} %get-tuple-element.18), channel_id=1, source_target_pairs={{1,0},{2,1},{3,2},{0,3},{5,4},{6,5},{7,6},{4,7},{9,8},{10,9},{11,1... | collective-permute-start | bytes 92168 | tf_op jit(solution)/shard_map/ppermute | solution.py:232
  7.3 13.2 %collective-permute-start.1 = (f32[240,128]{1,0:T(8,128)S(1)}, f32[240,128]{1,0:T(8,128)S(1)}, u32[]{:S(2)}, u32[]{:S(2)}) collective-permute-start(f32[240,128]{1,0:T(8,128)S(1)} %get-tuple-element.14), channel_id=1, source_target_pairs={{0,4},{4,8},{8,12},{12,0},{1,5},{5,9},{9,13},{13,1},{2,6},{6,10},{... | collective-permute-start | bytes 368648 | tf_op jit(solution)/shard_map/ppermute | solution.py:232
  8.8 11.6 %collective-permute-start.2 = (f32[240,128]{1,0:T(8,128)S(1)}, f32[240,128]{1,0:T(8,128)S(1)}, u32[]{:S(2)}, u32[]{:S(2)}) collective-permute-start(f32[240,128]{1,0:T(8,128)S(1)} %get-tuple-element.15), channel_id=1, source_target_pairs={{4,0},{8,4},{12,8},{0,12},{5,1},{9,5},{13,9},{1,13},{6,2},{10,6},{... | collective-permute-start | bytes 368648 | tf_op jit(solution)/shard_map/ppermute | solution.py:232
  20.4 6.6 %copy-start.3 = (f32[5,16,32,128]{3,2,1,0:T(8,128)S(1)}, f32[5,16,32,128]{3,2,1,0:T(8,128)}, u32[]{:S(2)}) copy-start(f32[5,16,32,128]{3,2,1,0:T(8,128)} %param.9) | copy-start | bytes 3932164
  20.5 13.7 %copy-start.4 = (bf16[256,512]{1,0:T(8,128)(2,1)S(1)}, bf16[256,512]{1,0:T(8,128)(2,1)}, u32[]{:S(2)}) copy-start(bf16[256,512]{1,0:T(8,128)(2,1)} %constant.124.clone.table) | copy-start | bytes 786436
  27.0 7.1 %copy-start.2 = (bf16[4096,512]{1,0:T(8,128)(2,1)S(1)}, bf16[4096,512]{1,0:T(8,128)(2,1)}, u32[]{:S(2)}) copy-start(bf16[4096,512]{1,0:T(8,128)(2,1)} %rec.1) | copy-start | bytes 12582916
  36.3 1.6 %collective-permute-start.5 = (f32[2,2,128,128]{3,2,1,0:T(8,128)S(1)}, f32[2,2,128,128]{3,2,1,0:T(8,128)S(1)}, u32[]{:S(2)}, u32[]{:S(2)}) collective-permute-start(f32[2,2,128,128]{3,2,1,0:T(8,128)S(1)} %dynamic-slice_bitcast_fusion.1), channel_id=1, source_target_pairs={{0,1},{1,0},{2,3},{3,2},{4,5},{5,4},{6,7},{7,6},{8,9},{9,8},{10,11... | collective-permute-start | bytes 786440 | tf_op jit(solution)/shard_map/ppermute | solution.py:567
  38.2 4.1 %collective-permute-start.11 = (f32[2,2,128,128]{3,2,1,0:T(8,128)S(1)}, f32[2,2,128,128]{3,2,1,0:T(8,128)S(1)}, u32[]{:S(2)}, u32[]{:S(2)}) collective-permute-start(f32[2,2,128,128]{3,2,1,0:T(8,128)S(1)} %dynamic-slice_bitcast_fusion), channel_id=1, source_target_pairs={{0,1},{1,0},{2,3},{3,2},{4,5},{5,4},{6,7},{7,6},{8,9},{9,8},{10,11... | collective-permute-start | bytes 786440 | tf_op jit(solution)/shard_map/ppermute | solution.py:567
  38.4 8.3 %collective-permute-start.6 = (f32[1,2,128,128]{3,2,1,0:T(8,128)S(1)}, f32[1,2,128,128]{3,2,1,0:T(8,128)S(1)}, u32[]{:S(2)}, u32[]{:S(2)}) collective-permute-start(f32[1,2,128,128]{3,2,1,0:T(8,128)S(1)} %constant_dynamic-slice_fusion.1), channel_id=1, source_target_pairs={{0,2},{1,3},{2,0},{3,1},{4,6},{5,7},{6,4},{7,5},{8,10},{9,11},{10,... | collective-permute-start | bytes 393224 | tf_op jit(solution)/shard_map/ppermute | solution.py:567
  42.4 11.0 %collective-permute-start.12 = (f32[1,2,128,128]{3,2,1,0:T(8,128)S(1)}, f32[1,2,128,128]{3,2,1,0:T(8,128)S(1)}, u32[]{:S(2)}, u32[]{:S(2)}) collective-permute-start(f32[1,2,128,128]{3,2,1,0:T(8,128)S(1)} %constant_dynamic-slice_fusion), channel_id=1, source_target_pairs={{0,2},{1,3},{2,0},{3,1},{4,6},{5,7},{6,4},{7,5},{8,10},{9,11},{10,... | collective-permute-start | bytes 393224 | tf_op jit(solution)/shard_map/ppermute | solution.py:567
  46.8 9.1 %collective-permute-start.7 = (f32[1,2,64,128]{3,2,1,0:T(8,128)S(1)}, f32[1,2,64,128]{3,2,1,0:T(8,128)S(1)}, u32[]{:S(2)}, u32[]{:S(2)}) collective-permute-start(f32[1,2,64,128]{3,2,1,0:T(8,128)S(1)} %dynamic-slice_bitcast_fusion.3), channel_id=1, source_target_pairs={{0,16},{16,0},{1,17},{17,1},{2,18},{18,2},{3,19},{19,3},{4,20},{20... | collective-permute-start | bytes 196616 | tf_op jit(solution)/shard_map/ppermute | solution.py:567
  53.5 9.0 %collective-permute-start.13 = (f32[1,2,64,128]{3,2,1,0:T(8,128)S(1)}, f32[1,2,64,128]{3,2,1,0:T(8,128)S(1)}, u32[]{:S(2)}, u32[]{:S(2)}) collective-permute-start(f32[1,2,64,128]{3,2,1,0:T(8,128)S(1)} %dynamic-slice_bitcast_fusion.2), channel_id=1, source_target_pairs={{0,16},{16,0},{1,17},{17,1},{2,18},{18,2},{3,19},{19,3},{4,20},{20... | collective-permute-start | bytes 196616 | tf_op jit(solution)/shard_map/ppermute | solution.py:567
  55.9 8.9 %collective-permute-start.8 = (f32[1,2,64,128]{3,2,1,0:T(8,128)S(1)}, f32[1,2,64,128]{3,2,1,0:T(8,128)S(1)}, u32[]{:S(2)}, u32[]{:S(2)}) collective-permute-start(f32[1,2,64,128]{3,2,1,0:T(8,128)S(1)} %bitcast_add_fusion.3), channel_id=1, source_target_pairs={{0,4},{4,0},{8,12},{12,8},{1,5},{5,1},{9,13},{13,9},{2,6},{6,2},{1... | collective-permute-start | bytes 196616 | tf_op jit(solution)/shard_map/ppermute | solution.py:567
  62.5 11.8 %collective-permute-start.14 = (f32[1,2,64,128]{3,2,1,0:T(8,128)S(1)}, f32[1,2,64,128]{3,2,1,0:T(8,128)S(1)}, u32[]{:S(2)}, u32[]{:S(2)}) collective-permute-start(f32[1,2,64,128]{3,2,1,0:T(8,128)S(1)} %bitcast_add_fusion.2), channel_id=1, source_target_pairs={{0,4},{4,0},{8,12},{12,8},{1,5},{5,1},{9,13},{13,9},{2,6},{6,2},{1... | collective-permute-start | bytes 196616 | tf_op jit(solution)/shard_map/ppermute | solution.py:567
  64.9 11.8 %collective-permute-start.9 = (f32[1,2,64,128]{3,2,1,0:T(8,128)S(1)}, f32[1,2,64,128]{3,2,1,0:T(8,128)S(1)}, u32[]{:S(2)}, u32[]{:S(2)}) collective-permute-start(f32[1,2,64,128]{3,2,1,0:T(8,128)S(1)} %add.90), channel_id=1, source_target_pairs={{0,8},{4,12},{8,0},{12,4},{1,9},{5,13},{9,1},{13,5},{2,10},{6,14},... | collective-permute-start | bytes 196616 | tf_op jit(solution)/shard_map/ppermute | solution.py:567
  74.4 5.2 %collective-permute-start.15 = (f32[1,2,64,128]{3,2,1,0:T(8,128)S(1)}, f32[1,2,64,128]{3,2,1,0:T(8,128)S(1)}, u32[]{:S(2)}, u32[]{:S(2)}) collective-permute-start(f32[1,2,64,128]{3,2,1,0:T(8,128)S(1)} %add.95), channel_id=1, source_target_pairs={{0,8},{4,12},{8,0},{12,4},{1,9},{5,13},{9,1},{13,5},{2,10},{6,14},... | collective-permute-start | bytes 196616 | tf_op jit(solution)/shard_map/ppermute | solution.py:567
  76.7 4.3 %collective-permute-start.10 = (f32[1,2,64,128]{3,2,1,0:T(8,128)S(1)}, f32[1,2,64,128]{3,2,1,0:T(8,128)S(1)}, u32[]{:S(2)}, u32[]{:S(2)}) collective-permute-start(f32[1,2,64,128]{3,2,1,0:T(8,128)S(1)} %add.91), channel_id=1, source_target_pairs={{0,16},{16,0},{1,17},{17,1},{2,18},{18,2},{3,19},{19,3},{4,20},{20... | collective-permute-start | bytes 196616 | tf_op jit(solution)/shard_map/ppermute | solution.py:567
  79.6 4.3 %collective-permute-start.16 = (f32[1,2,64,128]{3,2,1,0:T(8,128)S(1)}, f32[1,2,64,128]{3,2,1,0:T(8,128)S(1)}, u32[]{:S(2)}, u32[]{:S(2)}) collective-permute-start(f32[1,2,64,128]{3,2,1,0:T(8,128)S(1)} %add.96), channel_id=1, source_target_pairs={{0,16},{16,0},{1,17},{17,1},{2,18},{18,2},{3,19},{19,3},{4,20},{20... | collective-permute-start | bytes 196616 | tf_op jit(solution)/shard_map/ppermute | solution.py:567
  (2 other events, 7.8 us)

commit v9 on v8

--- a/solution.py
+++ b/solution.py
@@ -13,7 +13,7 @@
 BATCH = 4
 WIDE = 8
 CHUNKS = 2
-PARTS = 2
+PARTS = 1
 NT = (((1,), (1,)), ((), ()))
 
 

time: 84.6 us -> 83.5 us (0.987)
  starting transfers between devices: 42.1 us -> 39.7 us
  waiting for transfers between devices: 12.6 us -> 14.7 us
    ppermute x13, starting transfers between devices: 36.5 us -> 34.1 us  [swap(): return lax.ppermute(value, axis, [(i, i ^ bit) for i in range(size)])]
    ppermute x13, waiting for transfers between devices: 12.6 us -> 14.7 us  [swap(): return lax.ppermute(value, axis, [(i, i ^ bit) for i in range(size)])]
    pallas_call x3 -> x2, Pallas kernels: 2.14 us -> 2.02 us  [observe(): pl.pallas_call(functools.partial(observe_kernel, chunk=chunk, part=part,...]
where the time goes in v9:
time: 83.5 us; the launch traced here: 84.2 us
  starting transfers between devices  39.7 us (48%)
  Pallas kernels  25.7 us (31%)
  waiting for transfers between devices  14.7 us (18%)
  between operations  1.66 us (2%)
  local copies, waits for them, and re-layouts  1.5 us (2%)
  other arithmetic  1 us (1%)
    ppermute x13, starting transfers between devices, swap(): return lax.ppermute(value, axis, [(i, i ^ bit) for i in range(size)])  34.1 us
    pallas_call x3, Pallas kernels, line_call(): pl.pallas_call(kernel, out_shape=[jax.ShapeDtypeStruct(shape, jnp.float32...  20 us
    ppermute x13, waiting for transfers between devices, swap(): return lax.ppermute(value, axis, [(i, i ^ bit) for i in range(size)])  14.7 us
    ppermute x4, starting transfers between devices, neighbours(): return (lax.ppermute(last, axis, up), lax.ppermute(first, axis, down))  5.57 us
    pallas_call x2, Pallas kernels, observe(): pl.pallas_call(functools.partial(observe_kernel, chunk=chunk, part=part,...  2.02 us
    pallas_call x1, Pallas kernels, weights(): pl.pallas_call(functools.partial(weights_kernel, sizes=sizes, counts=coun...  1.99 us
  transfers between devices with their start and end apart: 17, of which 8 were waited for; matrix products, arithmetic and copies ran while one was open for 0% of the time, Pallas kernels for 19%

profile of v9, /device:TPU:0, one launch (start us, length us, event | category | flops | bytes accessed | tf_op | source)
XLA Modules:
  0.0 84.2 jit_solution(8406404777701242405)
XLA Ops:
  0.6 1.3 %copy-done = f32[5,16,32,128]{3,2,1,0:T(8,128)S(1)} copy-done((f32[5,16,32,128]{3,2,1,0:T(8,128)S(1)}, f32[5,16,32,128]{3,2,1,0:T(8,128)}, u32[]{:S(2)}) %copy-start) | copy-done | bytes 1310744
  2.5 3.0 %collective-permute-start = (f32[960,128]{1,0:T(8,128)S(1)}, f32[960,128]{1,0:T(8,128)S(1)}, u32[]{:S(2)}, u32[]{:S(2)}) collective-permute-start(f32[960,128]{1,0:T(8,128)S(1)} %get-tuple-element.13), channel_id=1, source_target_pairs={{0,16},{16,0},{1,17},{17,1},{2,18},{18,2},{3,19},{19,3},{4,20},{20... | collective-permute-start | bytes 1474568 | tf_op jit(solution)/shard_map/ppermute | solution.py:567
  5.5 1.7 %collective-permute-start.4 = (f32[60,128]{1,0:T(8,128)S(1)}, f32[60,128]{1,0:T(8,128)S(1)}, u32[]{:S(2)}, u32[]{:S(2)}) collective-permute-start(f32[60,128]{1,0:T(8,128)S(1)} %get-tuple-element.18), channel_id=1, source_target_pairs={{1,0},{2,1},{3,2},{0,3},{5,4},{6,5},{7,6},{4,7},{9,8},{10,9},{11,1... | collective-permute-start | bytes 92168 | tf_op jit(solution)/shard_map/ppermute | solution.py:232
  7.3 1.6 %collective-permute-start.1 = (f32[240,128]{1,0:T(8,128)S(1)}, f32[240,128]{1,0:T(8,128)S(1)}, u32[]{:S(2)}, u32[]{:S(2)}) collective-permute-start(f32[240,128]{1,0:T(8,128)S(1)} %get-tuple-element.14), channel_id=1, source_target_pairs={{0,4},{4,8},{8,12},{12,0},{1,5},{5,9},{9,13},{13,1},{2,6},{6,10},{... | collective-permute-start | bytes 368648 | tf_op jit(solution)/shard_map/ppermute | solution.py:232
  8.8 2.2 %collective-permute-start.2 = (f32[240,128]{1,0:T(8,128)S(1)}, f32[240,128]{1,0:T(8,128)S(1)}, u32[]{:S(2)}, u32[]{:S(2)}) collective-permute-start(f32[240,128]{1,0:T(8,128)S(1)} %get-tuple-element.15), channel_id=1, source_target_pairs={{4,0},{8,4},{12,8},{0,12},{5,1},{9,5},{13,9},{1,13},{6,2},{10,6},{... | collective-permute-start | bytes 368648 | tf_op jit(solution)/shard_map/ppermute | solution.py:232
  12.0 2.0 %weights.1 = (bf16[32768,128]{1,0:T(8,128)(2,1)S(1)}, f32[3,32,128]{2,1,0:T(8,128)S(1)}, f32[3,8,128]{2,1,0:T(8,128)S(1)}) custom-call(s32[1]{0:T(128)S(6)} %copy.17.live, s32[3]{0:T(128)S(1)} %pad_add_fusion.corner, s32[32,128]{1,0:T(8,128)S(1)} %copy-done.5, f32[2,32,128]{2,1,0:T(8,128)S(1)} %bitcast.46, f32[3,8,128]{2,1,0:T(8,128)S(1)} %bitcast.47), custom_call_target="tpu_custom_call" | custom-call | tf_op jit(solution)/shard_map/weights/pallas_call | solution.py:387
  14.0 6.4 %along_z.1.start = f32[2560,128]{1,0:T(8,128)S(1)} custom-call(f32[2560,128]{1,0:T(8,128)S(1)} %get-tuple-element.16.turned, f32[60,128]{1,0:T(8,128)S(1)} %collective-permute-done.3.left, f32[60,128]{1,0:T(8,128)S(1)} %collective-permute-done.4.right), custom_call_target="tpu_custom_call" | custom-call | tf_op jit(solution)/shard_map/along_z/pallas_call | solution.py:211
  20.5 6.5 %along_y.1.start = f32[2560,128]{1,0:T(8,128)S(1)} custom-call(f32[2560,128]{1,0:T(8,128)S(1)} %bitcast.39, f32[240,128]{1,0:T(8,128)S(1)} %collective-permute-done.1.left, f32[240,128]{1,0:T(8,128)S(1)} %collective-permute-done.2.right, f32[2560,128]{1,0:T(8,128)S(1)} %along_z.1.start), custom_call_target="tpu_custom_call" | custom-call | tf_op jit(solution)/shard_map/along_y/pallas_call | solution.py:211
  27.1 7.1 %along_x.1 = (f32[2560,128]{1,0:T(8,128)}, f32[512,128]{1,0:T(8,128)S(1)}) custom-call(f32[2560,128]{1,0:T(8,128)S(1)} %bitcast.40, f32[960,128]{1,0:T(8,128)S(1)} %collective-permute-done.ends, f32[2560,128]{1,0:T(8,128)S(1)} %along_y.1.start, f32[2560,128]{1,0:T(8,128)S(1)} %bitcast.41), custom_call_target="tpu_custom_call" | custom-call | tf_op jit(solution)/shard_map/along_x/pallas_call | solution.py:211
  34.1 1.1 %spectra.1.sp = bf16[32,256,128]{2,1,0:T(8,128)(2,1)S(1)} custom-call(s32[1]{0:T(128)S(6)} %copy.17.live, f32[512,128]{1,0:T(8,128)S(1)} %get-tuple-element.21.dens, bf16[4096,512]{1,0:T(8,128)(2,1)S(1)} %copy-done.2, s32[32,128]{1,0:T(8,128)S(1)} %copy-done.5, bf16[256,512]{1,0:T(8,128)(2,1)S(1)} %copy-done.4), custom_call_target="tpu_custom_call" | custom-call | tf_op jit(solution)/shard_map/spectra/pallas_call | solution.py:464
  35.3 1.0 %observe.2 = f32[4,2,128,128]{3,2,1,0:T(8,128)S(1)} custom-call(s32[1]{0:T(128)S(6)} %copy.17.live, f32[3,32,128]{2,1,0:T(8,128)S(1)} %get-tuple-element.20.centre, bf16[32,256,128]{2,1,0:T(8,128)(2,1)S(1)} %spectra.1.sp, bf16[32768,128]{1,0:T(8,128)(2,1)S(1)} %get-tuple-element.22.wts, f32[3,8,128]{2,1,0:T(8,128)S(1)} %get-tuple-element.23.lis), custom_call_target="tpu_custom_call" | custom-call | flops 4000000000 | bytes 1000000 | tf_op jit(solution)/shard_map/observe/pallas_call | solution.py:553
  36.4 1.0 %observe.3 = f32[4,2,128,128]{3,2,1,0:T(8,128)S(1)} custom-call(s32[1]{0:T(128)S(6)} %copy.17.live, f32[3,32,128]{2,1,0:T(8,128)S(1)} %get-tuple-element.20.centre, bf16[32,256,128]{2,1,0:T(8,128)(2,1)S(1)} %spectra.1.sp, bf16[32768,128]{1,0:T(8,128)(2,1)S(1)} %get-tuple-element.22.wts, f32[3,8,128]{2,1,0:T(8,128)S(1)} %get-tuple-element.23.lis), custom_call_target="tpu_custom_call" | custom-call | flops 4000000000 | bytes 1000000 | tf_op jit(solution)/shard_map/observe/pallas_call | solution.py:553
  38.1 9.4 %collective-permute-start.6 = (f32[1,2,128,128]{3,2,1,0:T(8,128)S(1)}, f32[1,2,128,128]{3,2,1,0:T(8,128)S(1)}, u32[]{:S(2)}, u32[]{:S(2)}) collective-permute-start(f32[1,2,128,128]{3,2,1,0:T(8,128)S(1)} %constant_dynamic-slice_fusion.1), channel_id=1, source_target_pairs={{0,2},{1,3},{2,0},{3,1},{4,6},{5,7},{6,4},{7,5},{8,10},{9,11},{10,... | collective-permute-start | bytes 393224 | tf_op jit(solution)/shard_map/ppermute | solution.py:567
  47.6 1.4 %collective-permute-start.12 = (f32[1,2,128,128]{3,2,1,0:T(8,128)S(1)}, f32[1,2,128,128]{3,2,1,0:T(8,128)S(1)}, u32[]{:S(2)}, u32[]{:S(2)}) collective-permute-start(f32[1,2,128,128]{3,2,1,0:T(8,128)S(1)} %constant_dynamic-slice_fusion), channel_id=1, source_target_pairs={{0,2},{1,3},{2,0},{3,1},{4,6},{5,7},{6,4},{7,5},{8,10},{9,11},{10,... | collective-permute-start | bytes 393224 | tf_op jit(solution)/shard_map/ppermute | solution.py:567
  49.0 2.8 %collective-permute-done.6 = f32[1,2,128,128]{3,2,1,0:T(8,128)S(1)} collective-permute-done((f32[1,2,128,128]{3,2,1,0:T(8,128)S(1)}, f32[1,2,128,128]{3,2,1,0:T(8,128)S(1)}, u32[]{:S(2)}, u32[]{:S(2)}) %collective-permute-start.6) | collective-permute-done | bytes 131104 | tf_op jit(solution)/shard_map/ppermute | solution.py:567
  51.9 3.9 %collective-permute-start.7 = (f32[1,2,64,128]{3,2,1,0:T(8,128)S(1)}, f32[1,2,64,128]{3,2,1,0:T(8,128)S(1)}, u32[]{:S(2)}, u32[]{:S(2)}) collective-permute-start(f32[1,2,64,128]{3,2,1,0:T(8,128)S(1)} %dynamic-slice_bitcast_fusion.3), channel_id=1, source_target_pairs={{0,16},{16,0},{1,17},{17,1},{2,18},{18,2},{3,19},{19,3},{4,20},{20... | collective-permute-start | bytes 196616 | tf_op jit(solution)/shard_map/ppermute | solution.py:567
  55.8 1.8 %collective-permute-start.13 = (f32[1,2,64,128]{3,2,1,0:T(8,128)S(1)}, f32[1,2,64,128]{3,2,1,0:T(8,128)S(1)}, u32[]{:S(2)}, u32[]{:S(2)}) collective-permute-start(f32[1,2,64,128]{3,2,1,0:T(8,128)S(1)} %dynamic-slice_bitcast_fusion.2), channel_id=1, source_target_pairs={{0,16},{16,0},{1,17},{17,1},{2,18},{18,2},{3,19},{19,3},{4,20},{20... | collective-permute-start | bytes 196616 | tf_op jit(solution)/shard_map/ppermute | solution.py:567
  58.5 1.7 %collective-permute-done.13 = f32[1,2,64,128]{3,2,1,0:T(8,128)S(1)} collective-permute-done((f32[1,2,64,128]{3,2,1,0:T(8,128)S(1)}, f32[1,2,64,128]{3,2,1,0:T(8,128)S(1)}, u32[]{:S(2)}, u32[]{:S(2)}) %collective-permute-start.13) | collective-permute-done | bytes 65568 | tf_op jit(solution)/shard_map/ppermute | solution.py:567
  60.6 2.2 %collective-permute-done.8 = f32[1,2,64,128]{3,2,1,0:T(8,128)S(1)} collective-permute-done((f32[1,2,64,128]{3,2,1,0:T(8,128)S(1)}, f32[1,2,64,128]{3,2,1,0:T(8,128)S(1)}, u32[]{:S(2)}, u32[]{:S(2)}) %collective-permute-start.8) | collective-permute-done | bytes 65568 | tf_op jit(solution)/shard_map/ppermute | solution.py:567
  62.8 11.1 %collective-permute-start.9 = (f32[1,2,64,128]{3,2,1,0:T(8,128)S(1)}, f32[1,2,64,128]{3,2,1,0:T(8,128)S(1)}, u32[]{:S(2)}, u32[]{:S(2)}) collective-permute-start(f32[1,2,64,128]{3,2,1,0:T(8,128)S(1)} %add.90), channel_id=1, source_target_pairs={{0,8},{4,12},{8,0},{12,4},{1,9},{5,13},{9,1},{13,5},{2,10},{6,14},... | collective-permute-start | bytes 196616 | tf_op jit(solution)/shard_map/ppermute | solution.py:567
  73.9 1.6 %collective-permute-start.15 = (f32[1,2,64,128]{3,2,1,0:T(8,128)S(1)}, f32[1,2,64,128]{3,2,1,0:T(8,128)S(1)}, u32[]{:S(2)}, u32[]{:S(2)}) collective-permute-start(f32[1,2,64,128]{3,2,1,0:T(8,128)S(1)} %add.95), channel_id=1, source_target_pairs={{0,8},{4,12},{8,0},{12,4},{1,9},{5,13},{9,1},{13,5},{2,10},{6,14},... | collective-permute-start | bytes 196616 | tf_op jit(solution)/shard_map/ppermute | solution.py:567
  76.8 2.3 %collective-permute-done.15 = f32[1,2,64,128]{3,2,1,0:T(8,128)S(1)} collective-permute-done((f32[1,2,64,128]{3,2,1,0:T(8,128)S(1)}, f32[1,2,64,128]{3,2,1,0:T(8,128)S(1)}, u32[]{:S(2)}, u32[]{:S(2)}) %collective-permute-start.15) | collective-permute-done | bytes 65568 | tf_op jit(solution)/shard_map/ppermute | solution.py:567
  79.2 1.3 %collective-permute-done.10 = f32[1,2,64,128]{3,2,1,0:T(8,128)S(1)} collective-permute-done((f32[1,2,64,128]{3,2,1,0:T(8,128)S(1)}, f32[1,2,64,128]{3,2,1,0:T(8,128)S(1)}, u32[]{:S(2)}, u32[]{:S(2)}) %collective-permute-start.10) | collective-permute-done | bytes 65568 | tf_op jit(solution)/shard_map/ppermute | solution.py:567
  80.5 2.9 %collective-permute-done.16 = f32[1,2,64,128]{3,2,1,0:T(8,128)S(1)} collective-permute-done((f32[1,2,64,128]{3,2,1,0:T(8,128)S(1)}, f32[1,2,64,128]{3,2,1,0:T(8,128)S(1)}, u32[]{:S(2)}, u32[]{:S(2)}) %collective-permute-start.16) | collective-permute-done | bytes 65568 | tf_op jit(solution)/shard_map/ppermute | solution.py:567
  (62 shorter events, 5.0 us)
Async XLA Ops:
  2.0 9.1 %copy-start.8 = (f32[1024]{0:T(1024)S(1)}, f32[1024]{0:T(1024)}, u32[]{:S(2)}) copy-start(f32[1024]{0:T(1024)} %param.16) | copy-start | bytes 12292
  2.0 9.2 %copy-start.7 = (f32[2,1024]{1,0:T(2,128)S(1)}, f32[2,1024]{1,0:T(2,128)}, u32[]{:S(2)}) copy-start(f32[2,1024]{1,0:T(2,128)} %param.15) | copy-start | bytes 24580
  2.0 9.9 %copy-start.6 = (f32[2,4096]{1,0:T(2,128)S(1)}, f32[2,4096]{1,0:T(2,128)}, u32[]{:S(2)}) copy-start(f32[2,4096]{1,0:T(2,128)} %param.13) | copy-start | bytes 98308
  2.0 10.0 %copy-start.5 = (s32[32,128]{1,0:T(8,128)S(1)}, s32[32,128]{1,0:T(8,128)}, u32[]{:S(2)}) copy-start(s32[32,128]{1,0:T(8,128)} %cell.3) | copy-start | bytes 49156
  2.5 24.5 %collective-permute-start = (f32[960,128]{1,0:T(8,128)S(1)}, f32[960,128]{1,0:T(8,128)S(1)}, u32[]{:S(2)}, u32[]{:S(2)}) collective-permute-start(f32[960,128]{1,0:T(8,128)S(1)} %get-tuple-element.13), channel_id=1, source_target_pairs={{0,16},{16,0},{1,17},{17,1},{2,18},{18,2},{3,19},{19,3},{4,20},{20... | collective-permute-start | bytes 1474568 | tf_op jit(solution)/shard_map/ppermute | solution.py:567
  5.5 8.4 %collective-permute-start.3 = (f32[60,128]{1,0:T(8,128)S(1)}, f32[60,128]{1,0:T(8,128)S(1)}, u32[]{:S(2)}, u32[]{:S(2)}) collective-permute-start(f32[60,128]{1,0:T(8,128)S(1)} %get-tuple-element.17), channel_id=1, source_target_pairs={{0,1},{1,2},{2,3},{3,0},{4,5},{5,6},{6,7},{7,4},{8,9},{9,10},{10,1... | collective-permute-start | bytes 92168 | tf_op jit(solution)/shard_map/ppermute | solution.py:232
  5.5 8.4 %collective-permute-start.4 = (f32[60,128]{1,0:T(8,128)S(1)}, f32[60,128]{1,0:T(8,128)S(1)}, u32[]{:S(2)}, u32[]{:S(2)}) collective-permute-start(f32[60,128]{1,0:T(8,128)S(1)} %get-tuple-element.18), channel_id=1, source_target_pairs={{1,0},{2,1},{3,2},{0,3},{5,4},{6,5},{7,6},{4,7},{9,8},{10,9},{11,1... | collective-permute-start | bytes 92168 | tf_op jit(solution)/shard_map/ppermute | solution.py:232
  7.3 13.2 %collective-permute-start.1 = (f32[240,128]{1,0:T(8,128)S(1)}, f32[240,128]{1,0:T(8,128)S(1)}, u32[]{:S(2)}, u32[]{:S(2)}) collective-permute-start(f32[240,128]{1,0:T(8,128)S(1)} %get-tuple-element.14), channel_id=1, source_target_pairs={{0,4},{4,8},{8,12},{12,0},{1,5},{5,9},{9,13},{13,1},{2,6},{6,10},{... | collective-permute-start | bytes 368648 | tf_op jit(solution)/shard_map/ppermute | solution.py:232
  8.8 11.6 %collective-permute-start.2 = (f32[240,128]{1,0:T(8,128)S(1)}, f32[240,128]{1,0:T(8,128)S(1)}, u32[]{:S(2)}, u32[]{:S(2)}) collective-permute-start(f32[240,128]{1,0:T(8,128)S(1)} %get-tuple-element.15), channel_id=1, source_target_pairs={{4,0},{8,4},{12,8},{0,12},{5,1},{9,5},{13,9},{1,13},{6,2},{10,6},{... | collective-permute-start | bytes 368648 | tf_op jit(solution)/shard_map/ppermute | solution.py:232
  20.4 6.6 %copy-start.3 = (f32[5,16,32,128]{3,2,1,0:T(8,128)S(1)}, f32[5,16,32,128]{3,2,1,0:T(8,128)}, u32[]{:S(2)}) copy-start(f32[5,16,32,128]{3,2,1,0:T(8,128)} %param.9) | copy-start | bytes 3932164
  20.5 13.7 %copy-start.4 = (bf16[256,512]{1,0:T(8,128)(2,1)S(1)}, bf16[256,512]{1,0:T(8,128)(2,1)}, u32[]{:S(2)}) copy-start(bf16[256,512]{1,0:T(8,128)(2,1)} %constant.124.clone.table) | copy-start | bytes 786436
  27.1 7.1 %copy-start.2 = (bf16[4096,512]{1,0:T(8,128)(2,1)S(1)}, bf16[4096,512]{1,0:T(8,128)(2,1)}, u32[]{:S(2)}) copy-start(bf16[4096,512]{1,0:T(8,128)(2,1)} %rec.1) | copy-start | bytes 12582916
  36.3 1.7 %collective-permute-start.5 = (f32[2,2,128,128]{3,2,1,0:T(8,128)S(1)}, f32[2,2,128,128]{3,2,1,0:T(8,128)S(1)}, u32[]{:S(2)}, u32[]{:S(2)}) collective-permute-start(f32[2,2,128,128]{3,2,1,0:T(8,128)S(1)} %dynamic-slice_bitcast_fusion.1), channel_id=1, source_target_pairs={{0,1},{1,0},{2,3},{3,2},{4,5},{5,4},{6,7},{7,6},{8,9},{9,8},{10,11... | collective-permute-start | bytes 786440 | tf_op jit(solution)/shard_map/ppermute | solution.py:567
  37.5 10.0 %collective-permute-start.11 = (f32[2,2,128,128]{3,2,1,0:T(8,128)S(1)}, f32[2,2,128,128]{3,2,1,0:T(8,128)S(1)}, u32[]{:S(2)}, u32[]{:S(2)}) collective-permute-start(f32[2,2,128,128]{3,2,1,0:T(8,128)S(1)} %dynamic-slice_bitcast_fusion), channel_id=1, source_target_pairs={{0,1},{1,0},{2,3},{3,2},{4,5},{5,4},{6,7},{7,6},{8,9},{9,8},{10,11... | collective-permute-start | bytes 786440 | tf_op jit(solution)/shard_map/ppermute | solution.py:567
  38.1 13.8 %collective-permute-start.6 = (f32[1,2,128,128]{3,2,1,0:T(8,128)S(1)}, f32[1,2,128,128]{3,2,1,0:T(8,128)S(1)}, u32[]{:S(2)}, u32[]{:S(2)}) collective-permute-start(f32[1,2,128,128]{3,2,1,0:T(8,128)S(1)} %constant_dynamic-slice_fusion.1), channel_id=1, source_target_pairs={{0,2},{1,3},{2,0},{3,1},{4,6},{5,7},{6,4},{7,5},{8,10},{9,11},{10,... | collective-permute-start | bytes 393224 | tf_op jit(solution)/shard_map/ppermute | solution.py:567
  47.6 8.2 %collective-permute-start.12 = (f32[1,2,128,128]{3,2,1,0:T(8,128)S(1)}, f32[1,2,128,128]{3,2,1,0:T(8,128)S(1)}, u32[]{:S(2)}, u32[]{:S(2)}) collective-permute-start(f32[1,2,128,128]{3,2,1,0:T(8,128)S(1)} %constant_dynamic-slice_fusion), channel_id=1, source_target_pairs={{0,2},{1,3},{2,0},{3,1},{4,6},{5,7},{6,4},{7,5},{8,10},{9,11},{10,... | collective-permute-start | bytes 393224 | tf_op jit(solution)/shard_map/ppermute | solution.py:567
  51.9 6.5 %collective-permute-start.7 = (f32[1,2,64,128]{3,2,1,0:T(8,128)S(1)}, f32[1,2,64,128]{3,2,1,0:T(8,128)S(1)}, u32[]{:S(2)}, u32[]{:S(2)}) collective-permute-start(f32[1,2,64,128]{3,2,1,0:T(8,128)S(1)} %dynamic-slice_bitcast_fusion.3), channel_id=1, source_target_pairs={{0,16},{16,0},{1,17},{17,1},{2,18},{18,2},{3,19},{19,3},{4,20},{20... | collective-permute-start | bytes 196616 | tf_op jit(solution)/shard_map/ppermute | solution.py:567
  55.8 4.3 %collective-permute-start.13 = (f32[1,2,64,128]{3,2,1,0:T(8,128)S(1)}, f32[1,2,64,128]{3,2,1,0:T(8,128)S(1)}, u32[]{:S(2)}, u32[]{:S(2)}) collective-permute-start(f32[1,2,64,128]{3,2,1,0:T(8,128)S(1)} %dynamic-slice_bitcast_fusion.2), channel_id=1, source_target_pairs={{0,16},{16,0},{1,17},{17,1},{2,18},{18,2},{3,19},{19,3},{4,20},{20... | collective-permute-start | bytes 196616 | tf_op jit(solution)/shard_map/ppermute | solution.py:567
  58.4 4.3 %collective-permute-start.8 = (f32[1,2,64,128]{3,2,1,0:T(8,128)S(1)}, f32[1,2,64,128]{3,2,1,0:T(8,128)S(1)}, u32[]{:S(2)}, u32[]{:S(2)}) collective-permute-start(f32[1,2,64,128]{3,2,1,0:T(8,128)S(1)} %bitcast_add_fusion.3), channel_id=1, source_target_pairs={{0,4},{4,0},{8,12},{12,8},{1,5},{5,1},{9,13},{13,9},{2,6},{6,2},{1... | collective-permute-start | bytes 196616 | tf_op jit(solution)/shard_map/ppermute | solution.py:567
  60.2 13.7 %collective-permute-start.14 = (f32[1,2,64,128]{3,2,1,0:T(8,128)S(1)}, f32[1,2,64,128]{3,2,1,0:T(8,128)S(1)}, u32[]{:S(2)}, u32[]{:S(2)}) collective-permute-start(f32[1,2,64,128]{3,2,1,0:T(8,128)S(1)} %bitcast_add_fusion.2), channel_id=1, source_target_pairs={{0,4},{4,0},{8,12},{12,8},{1,5},{5,1},{9,13},{13,9},{2,6},{6,2},{1... | collective-permute-start | bytes 196616 | tf_op jit(solution)/shard_map/ppermute | solution.py:567
  62.8 13.4 %collective-permute-start.9 = (f32[1,2,64,128]{3,2,1,0:T(8,128)S(1)}, f32[1,2,64,128]{3,2,1,0:T(8,128)S(1)}, u32[]{:S(2)}, u32[]{:S(2)}) collective-permute-start(f32[1,2,64,128]{3,2,1,0:T(8,128)S(1)} %add.90), channel_id=1, source_target_pairs={{0,8},{4,12},{8,0},{12,4},{1,9},{5,13},{9,1},{13,5},{2,10},{6,14},... | collective-permute-start | bytes 196616 | tf_op jit(solution)/shard_map/ppermute | solution.py:567
  73.9 5.2 %collective-permute-start.15 = (f32[1,2,64,128]{3,2,1,0:T(8,128)S(1)}, f32[1,2,64,128]{3,2,1,0:T(8,128)S(1)}, u32[]{:S(2)}, u32[]{:S(2)}) collective-permute-start(f32[1,2,64,128]{3,2,1,0:T(8,128)S(1)} %add.95), channel_id=1, source_target_pairs={{0,8},{4,12},{8,0},{12,4},{1,9},{5,13},{9,1},{13,5},{2,10},{6,14},... | collective-permute-start | bytes 196616 | tf_op jit(solution)/shard_map/ppermute | solution.py:567
  76.2 4.3 %collective-permute-start.10 = (f32[1,2,64,128]{3,2,1,0:T(8,128)S(1)}, f32[1,2,64,128]{3,2,1,0:T(8,128)S(1)}, u32[]{:S(2)}, u32[]{:S(2)}) collective-permute-start(f32[1,2,64,128]{3,2,1,0:T(8,128)S(1)} %add.91), channel_id=1, source_target_pairs={{0,16},{16,0},{1,17},{17,1},{2,18},{18,2},{3,19},{19,3},{4,20},{20... | collective-permute-start | bytes 196616 | tf_op jit(solution)/shard_map/ppermute | solution.py:567
  79.1 4.3 %collective-permute-start.16 = (f32[1,2,64,128]{3,2,1,0:T(8,128)S(1)}, f32[1,2,64,128]{3,2,1,0:T(8,128)S(1)}, u32[]{:S(2)}, u32[]{:S(2)}) collective-permute-start(f32[1,2,64,128]{3,2,1,0:T(8,128)S(1)} %add.96), channel_id=1, source_target_pairs={{0,16},{16,0},{1,17},{17,1},{2,18},{18,2},{3,19},{19,3},{4,20},{20... | collective-permute-start | bytes 196616 | tf_op jit(solution)/shard_map/ppermute | solution.py:567
  (2 other events, 7.8 us)
